TPU v7x, 8 devices: a whole 2x2x1 slice. The times are simulated.
8 devices in a mesh: tp: 4 (over z, y, x), cp: 2 (over core).
Axes of the slice: x: 2, y: 2, z: 1, core: 2. Of those that a mesh axis runs over, the one named last changes fastest.
Arguments:
- hidden: bfloat16 [8, 1024, 6144], P(None, 'cp')
- grad_out: bfloat16 [8, 1024, 6144], P(None, 'cp')
- w_query: bfloat16 [6144, 48, 128], P(None, 'tp')
- w_key: bfloat16 [6144, 128], replicated
- w_value: bfloat16 [6144, 128], replicated
- w_out: bfloat16 [48, 128, 6144], P('tp')
Outputs:
- output 1: bfloat16 [8, 1024, 6144], P(None, 'cp')
- output 2: bfloat16 [8, 1024, 6144], P(None, 'cp')
- output 3: float32 [6144, 48, 128], P(None, 'tp')
- output 4: float32 [6144, 128], replicated
- output 5: float32 [6144, 128], replicated
- output 6: float32 [48, 128, 6144], P('tp')
All inputs are finite; a program needn't handle non-finite values.
Results may differ from a plain program's by a relative error of at most 0.0110935.
Values are sent between devices in bfloat16 or wider.
A program may use at most 1.25 GiB of HBM per device.

v0:
```python
import jax
import jax.numpy as jnp
from jax import lax
from jax.sharding import PartitionSpec as P

ROPE_BASE = 10000.0


def rope_tables(positions, head_dim):
    half_dim = head_dim // 2
    inv_freq = 1.0 / jnp.power(ROPE_BASE, jnp.arange(half_dim, dtype=jnp.float32) * (2.0 / head_dim))
    angles = positions.astype(jnp.float32)[:, None] * inv_freq[None, :]
    return jnp.cos(angles), jnp.sin(angles)


def rotate(rot_in, cos_tab, sin_tab):
    half_dim = rot_in.shape[-1] // 2
    low_half = rot_in[..., :half_dim]
    high_half = rot_in[..., half_dim:]
    return jnp.concatenate([low_half * cos_tab - high_half * sin_tab, high_half * cos_tab + low_half * sin_tab], axis=-1)


def unrotate(rot_in, cos_tab, sin_tab):
    half_dim = rot_in.shape[-1] // 2
    low_half = rot_in[..., :half_dim]
    high_half = rot_in[..., half_dim:]
    return jnp.concatenate([low_half * cos_tab + high_half * sin_tab, high_half * cos_tab - low_half * sin_tab], axis=-1)


def pair_scores(queries, key_blk, q_start, k_start):
    scores = jnp.einsum("bhqe,bke->bhqk", queries, key_blk, preferred_element_type=jnp.float32)
    q_pos = q_start + jnp.arange(queries.shape[2])
    k_pos = k_start + jnp.arange(key_blk.shape[1])
    allowed = k_pos[None, :] <= q_pos[:, None]
    return jnp.where(allowed, scores, -jnp.inf)


def forward_update(queries, kv_blk, q_start, k_start, soft_stats):
    run_max, run_sum, run_acc = soft_stats
    scores = pair_scores(queries, kv_blk[:, 0], q_start, k_start)
    new_max = jnp.maximum(run_max, jnp.max(scores, axis=-1))
    rescale = jnp.exp(run_max - new_max)
    weights = jnp.exp(scores - new_max[..., None])
    new_sum = run_sum * rescale + jnp.sum(weights, axis=-1)
    new_acc = run_acc * rescale[..., None] + jnp.einsum("bhqk,bke->bhqe", weights.astype(jnp.bfloat16), kv_blk[:, 1], preferred_element_type=jnp.float32)
    return new_max, new_sum, new_acc


def backward_update(queries, d_out, row_lse, row_delta, kv_blk, q_start, k_start):
    scores = pair_scores(queries, kv_blk[:, 0], q_start, k_start)
    prob_blk = jnp.exp(scores - row_lse[..., None])
    d_prob = jnp.einsum("bhqe,bke->bhqk", d_out, kv_blk[:, 1], preferred_element_type=jnp.float32)
    d_score = (prob_blk * (d_prob - row_delta[..., None])).astype(jnp.bfloat16)
    dq_part = jnp.einsum("bhqk,bke->bhqe", d_score, kv_blk[:, 0], preferred_element_type=jnp.float32)
    dk_part = jnp.einsum("bhqk,bhqe->bke", d_score, queries, preferred_element_type=jnp.float32)
    dv_part = jnp.einsum("bhqk,bhqe->bke", prob_blk.astype(jnp.bfloat16), d_out, preferred_element_type=jnp.float32)
    return dq_part, jnp.stack([dk_part, dv_part], axis=1)


def solution(mesh):
    cp_size = mesh.shape["cp"]
    shift_pairs = [(src_idx, (src_idx + 1) % cp_size) for src_idx in range(cp_size)]

    def local_program(hidden, grad_out, w_query, w_key, w_value, w_out):
        n_batch, block_len = hidden.shape[0], hidden.shape[1]
        n_local = w_query.shape[1]
        head_dim = w_key.shape[1]
        q_scale = head_dim ** -0.5
        cp_idx = lax.axis_index("cp")
        q_start = cp_idx * block_len
        cos_tab, sin_tab = rope_tables(q_start + jnp.arange(block_len), head_dim)
        q_pre = jnp.einsum("bsd,dhe->bhse", hidden, w_query, preferred_element_type=jnp.float32)
        queries = (rotate(q_pre, cos_tab, sin_tab) * q_scale).astype(jnp.bfloat16)
        key_pre = jnp.einsum("bsd,de->bse", hidden, w_key, preferred_element_type=jnp.float32)
        key_loc = rotate(key_pre, cos_tab, sin_tab).astype(jnp.bfloat16)
        val_loc = jnp.einsum("bsd,de->bse", hidden, w_value, preferred_element_type=jnp.float32).astype(jnp.bfloat16)
        kv_loc = jnp.stack([key_loc, val_loc], axis=1)

        def fwd_compute(step_idx, kv_blk, soft_stats):
            k_start = ((cp_idx - step_idx) % cp_size) * block_len
            return lax.cond(step_idx <= cp_idx, lambda stats_in: forward_update(queries, kv_blk, q_start, k_start, stats_in), lambda stats_in: stats_in, soft_stats)

        def fwd_body(step_idx, loop_state):
            kv_blk, soft_stats = loop_state
            soft_stats = fwd_compute(step_idx, kv_blk, soft_stats)
            return lax.ppermute(kv_blk, "cp", shift_pairs), soft_stats

        stats_init = (jnp.full((n_batch, n_local, block_len), -jnp.inf, jnp.float32), jnp.zeros((n_batch, n_local, block_len), jnp.float32), jnp.zeros((n_batch, n_local, block_len, head_dim), jnp.float32))
        kv_blk, soft_stats = lax.fori_loop(0, cp_size - 1, fwd_body, (kv_loc, stats_init))
        run_max, run_sum, run_acc = fwd_compute(cp_size - 1, kv_blk, soft_stats)
        attn_heads = (run_acc / run_sum[..., None]).astype(jnp.bfloat16)
        row_lse = run_max + jnp.log(run_sum)
        out_part = jnp.einsum("cirf,ife->cre", attn_heads, w_out, preferred_element_type=jnp.float32)
        attn_out = lax.psum(out_part, "tp").astype(jnp.bfloat16)
        d_out = jnp.einsum("cre,ife->cirf", grad_out, w_out, preferred_element_type=jnp.float32).astype(jnp.bfloat16)
        row_delta = jnp.einsum("bhqe,bhqe->bhq", d_out, attn_heads, preferred_element_type=jnp.float32)

        def bwd_compute(step_idx, kv_blk, dkv_blk, dq_acc):
            k_start = ((cp_idx - step_idx) % cp_size) * block_len

            def active(acc_pair):
                dq_in, dkv_in = acc_pair
                dq_part, dkv_part = backward_update(queries, d_out, row_lse, row_delta, kv_blk, q_start, k_start)
                return dq_in + dq_part, dkv_in + dkv_part

            return lax.cond(step_idx <= cp_idx, active, lambda acc_pair: acc_pair, (dq_acc, dkv_blk))

        def bwd_body(step_idx, loop_state):
            kv_blk, dkv_blk, dq_acc = loop_state
            dq_acc, dkv_blk = bwd_compute(step_idx, kv_blk, dkv_blk, dq_acc)
            kv_blk = lax.ppermute(kv_blk, "cp", shift_pairs)
            dkv_blk = lax.ppermute(dkv_blk, "cp", shift_pairs)
            return kv_blk, dkv_blk, dq_acc

        dkv_init = jnp.zeros((n_batch, 2, block_len, head_dim), jnp.float32)
        dq_init = jnp.zeros((n_batch, n_local, block_len, head_dim), jnp.float32)
        kv_blk, dkv_blk, dq_acc = lax.fori_loop(0, cp_size - 1, bwd_body, (kv_loc, dkv_init, dq_init))
        dq_acc, dkv_blk = bwd_compute(cp_size - 1, kv_blk, dkv_blk, dq_acc)
        dkv_blk = lax.ppermute(dkv_blk, "cp", shift_pairs)
        dkv_full = lax.psum(dkv_blk, "tp")
        dq_pre = (unrotate(dq_acc, cos_tab, sin_tab) * q_scale).astype(jnp.bfloat16)
        dk_pre = unrotate(dkv_full[:, 0], cos_tab, sin_tab).astype(jnp.bfloat16)
        dv_pre = dkv_full[:, 1].astype(jnp.bfloat16)
        d_w_query = lax.psum(jnp.einsum("cre,cirf->eif", hidden, dq_pre, preferred_element_type=jnp.float32), "cp")
        d_w_out = lax.psum(jnp.einsum("cirf,cre->ife", attn_heads, grad_out, preferred_element_type=jnp.float32), "cp")
        d_w_key = lax.psum(jnp.einsum("cre,crf->ef", hidden, dk_pre, preferred_element_type=jnp.float32), "cp")
        d_w_value = lax.psum(jnp.einsum("cre,crf->ef", hidden, dv_pre, preferred_element_type=jnp.float32), "cp")
        dh_heads = lax.psum(jnp.einsum("cirf,eif->cre", dq_pre, w_query, preferred_element_type=jnp.float32), "tp")
        dh_kv = jnp.einsum("crf,ef->cre", dk_pre, w_key, preferred_element_type=jnp.float32) + jnp.einsum("crf,ef->cre", dv_pre, w_value, preferred_element_type=jnp.float32)
        d_hidden = (dh_heads + dh_kv).astype(jnp.bfloat16)
        return attn_out, d_hidden, d_w_query, d_w_key, d_w_value, d_w_out

    row_spec = P(None, "cp", None)
    return jax.shard_map(local_program, mesh=mesh, in_specs=(row_spec, row_spec, P(None, "tp", None), P(), P(), P("tp", None, None)), out_specs=(row_spec, row_spec, P(None, "tp", None), P(), P(), P("tp", None, None)), check_vma=False)
```

profile of v0, /device:TPU:0, one launch (start us, length us, event | category | flops | bytes accessed | tf_op | source)
XLA Modules:
  0.0 6535.4 jit_solution(15389851609291978099)
XLA Ops:
  61.6 91.0 %fusion.82 = f32[8,12,512,128]{2,3,0,1:T(8,128)} fusion(bf16[8,512,6144]{2,1,0:T(8,128)(2,1)} %param.14, bf16[6144,12,128]{2,0,1:T(8,128)(2,1)} %param.16), kind=kOutput, calls=%fused_computation.108 | convolution fusion | flops 77309411328 | bytes 94371840 | tf_op jit(solution)/shard_map/bsd,dhe->bhse/dot_general | solution.py:72
  152.6 89.8 %convert_bitcast_fusion = bf16[8,12,512,128]{2,3,0,1:T(8,128)(2,1)} fusion(bf16[8,512,6144]{2,1,0:T(8,128)(2,1)} %param.15, bf16[12,128,6144]{2,1,0:T(8,128)(2,1)} %param.19), kind=kOutput, calls=%fused_computation.105 | convolution fusion | flops 77315702784 | bytes 81788928 | tf_op jit(solution)/shard_map/cre,ife->cirf/dot_general | solution.py:95
  301.7 125.1 %conditional.4 = (f32[8,12,512]{2,1,0:T(8,128)S(1)}, f32[8,12,512]{2,1,0:T(8,128)S(1)}, f32[8,12,512,128]{3,2,1,0:T(8,128)}) conditional(s32[]{:T(128)} %convert_element_type.75, (f32[8,12,512]{2,1,0:T(8,128)S(1)}, f32[8,12,512]{2,1,0:T(8,128)S(1)}, f32[8,12,512,128]{3,2,1,0:T(8,128)}) %tuple.58, (s32[]{:T(128)}, s32[]{:T(128)}, ...), branch_computations={%region_0.1_spmd, %region_1.4_spmd} | conditional | flops 13099172864 | bytes 375398432 | solution.py:81
  305.9 39.1 select_reduce_fusion
  345.1 31.3 fusion.1
  376.6 50.2 multiply_add_fusion
  451.4 211.2 %conditional.6 = ((f32[8,12,512,128]{3,2,1,0:T(8,128)}, f32[8,2,512,128]{3,2,0,1:T(8,128)})) conditional(s32[]{:T(128)} %convert_element_type.75, (f32[8,12,512,128]{3,2,1,0:T(8,128)}, f32[8,2,512,128]{3,2,0,1:T(8,128)}) %tuple.61, (s32[]{:T(128)}, s32[]{:T(128)}, bf16[8,2,512,128]{2,3,0,1:T(8,128)(2,1)}, bf16[8,12,512,128]{2,3,0,1:T(8,128)(2,1)}, ...), branch_computations={%region_9.10_spmd, %region_10.11_spmd} | conditional | flops 32422232064 | bytes 587669504 | solution.py:106
  455.4 39.0 fusion.20
  494.6 59.7 multiply_convert_fusion
  580.4 41.8 fusion.22
  626.9 35.7 convolution_add_fusion
  662.6 125.1 %collective-permute-start.1 = (f32[8,2,512,128]{3,2,0,1:T(8,128)}, f32[8,2,512,128]{3,2,0,1:T(8,128)}, u32[]{:S(2)}, u32[]{:S(2)}) collective-permute-start(f32[8,2,512,128]{3,2,0,1:T(8,128)} %get-tuple-element.235), channel_id=1, source_target_pairs={{0,1},{1,0},{2,3},{3,2},{4,5},{5,4},{6,7},{7,6}} | collective-permute-start | bytes 12582920 | tf_op jit(solution)/shard_map/while/body/eval_jaxpr/ppermute | solution.py:112
  794.5 79.7 %conditional.7 = (f32[8,2,512,128]{3,2,0,1:T(8,128)}, f32[8,12,512,64]{2,3,0,1:T(8,128)}, f32[8,12,512,64]{2,3,0,1:T(8,128)}) conditional(s32[]{:T(128)} %convert_element_type.74, (f32[8,2,512,128]{3,2,0,1:T(8,128)}, f32[8,12,512,128]{3,2,1,0:T(8,128)}) %tuple.63, (s32[]{:T(128)}, s32[]{:T(128)}, bf16[8,2,512,128]{2,3,0,1:T(8,128)(2,1)}, ...), branch_computations={%region_11.12_spmd.clone, %region_12.13_spmd.clone} | conditional | flops 32422232064 | bytes 738664448 | solution.py:106
  879.6 200.4 %collective-permute-start.2 = (f32[8,2,512,128]{2,3,0,1:T(8,128)}, f32[8,2,512,128]{2,3,0,1:T(8,128)}, u32[]{:S(2)}, u32[]{:S(2)}) collective-permute-start(f32[8,2,512,128]{2,3,0,1:T(8,128)} %copy.39), channel_id=1, source_target_pairs={{0,1},{1,0},{2,3},{3,2},{4,5},{5,4},{6,7},{7,6}} | collective-permute-start | bytes 12582920 | tf_op jit(solution)/shard_map/ppermute | solution.py:119
  1099.9 93.5 %convolution_bitcast_fusion = f32[8,512,6144]{2,1,0:T(8,128)} fusion(bf16[6144,12,128]{2,0,1:T(8,128)(2,1)} %param.16, f32[8,12,512,64]{2,3,0,1:T(8,128)} %get-tuple-element.355, f32[8,12,512,64]{2,3,0,1:T(8,128)} %get-tuple-element.354), kind=kOutput, calls=%fused_computation.81 | convolution fusion | flops 77328285696 | bytes 144703488 | tf_op jit(solution)/shard_map/cirf,eif->cre/dot_general | solution.py:128
  1193.7 89.4 %fusion.79 = f32[12,128,6144]{2,1,0:T(8,128)} fusion(bf16[8,12,512,128]{3,2,1,0:T(8,128)(2,1)} %get-tuple-element.337, bf16[8,512,6144]{2,1,0:T(8,128)(2,1)} %param.15), kind=kOutput, calls=%fused_computation.102 | convolution fusion | flops 77309411328 | bytes 100663296 | tf_op jit(solution)/shard_map/cirf,cre->ife/dot_general | solution.py:125
  1283.1 94.1 %fusion.76 = f32[6144,12,128]{0,2,1:T(8,128)} fusion(bf16[8,512,6144]{2,1,0:T(8,128)(2,1)} %param.14, f32[8,12,512,64]{2,3,0,1:T(8,128)} %get-tuple-element.355, f32[8,12,512,64]{2,3,0,1:T(8,128)} %get-tuple-element.354), kind=kOutput, calls=%fused_computation.101 | convolution fusion | flops 77328285696 | bytes 113246208 | tf_op jit(solution)/shard_map/cre,cirf->eif/dot_general | solution.py:124
  1377.2 1535.8 %all-reduce.6.cloned.1.call-done = (f32[8,512,6144]{2,1,0:T(8,128)}, f32[8,2,512,128]{2,3,0,1:T(8,128)}) async-done(((f32[8,512,6144]{2,1,0:T(8,128)}, f32[8,2,512,128]{2,3,0,1:T(8,128)}), (f32[8,512,6144]{2,1,0:T(8,128)}, f32[8,2,512,128]{2,3,0,1:T(8,128)})) %all-reduce.6.cloned.1.call-update) | async-done | bytes 104857616 | tf_op jit(solution)/shard_map/psum | solution.py:128
  2959.9 88.8 %convolution_bitcast_fusion.1 = f32[8,512,6144]{2,1,0:T(8,128)} fusion(bf16[8,12,512,128]{3,2,1,0:T(8,128)(2,1)} %get-tuple-element.337, bf16[12,128,6144]{2,1,0:T(8,128)(2,1)} %param.19), kind=kOutput, calls=%fused_computation.82 | convolution fusion | flops 77309411328 | bytes 132120576 | tf_op jit(solution)/shard_map/cirf,ife->cre/dot_general | solution.py:93
  3048.7 3293.1 %all-reduce.9 = bf16[8,512,6144]{2,1,0:T(8,128)(2,1)} all-reduce(f32[8,512,6144]{2,1,0:T(8,128)} %convolution_bitcast_fusion.1), channel_id=1, replica_groups=mesh['tp'=4,'cp'=2] {'tp'}, use_global_device_ids=true, to_apply=%region_8.9 | all-reduce | flops 25165824 | bytes 150994944 | tf_op jit(solution)/shard_map/psum | solution.py:94
  6341.8 35.8 fusion.94
  6377.6 79.5 %add_convert_fusion = bf16[8,512,6144]{2,1,0:T(8,128)(2,1)} fusion(f32[8,512,6144]{2,1,0:T(8,128)} %get-tuple-element.326, f32[8,512,6144]{2,1,0:T(8,128)} %fusion.94, bf16[6144,128]{1,0:T(8,128)(2,1)S(1)} %copy-done.4, f32[8,2,512,128]{2,3,0,1:T(8,128)} %get-tuple-element.327), kind=kOutput, calls=%fused_computation.80 | convolution fusion | flops 6517948416 | bytes 254279680 | tf_op jit(solution)/shard_map/crf,ef->cre/dot_general | solution.py:129
  6457.1 36.7 copy.43
  6500.8 27.5 copy.166
  (77 shorter events, 332.6 us)
Async XLA Ops:
  7.2 1.4 copy-start
  7.2 2905.8 %all-reduce.6.cloned.1.call-start = ((), (), s32[]{:S(2)}) async-start(), calls=%async_computation | async-start | bytes 209715200 | tf_op jit(solution)/shard_map/psum | solution.py:128
  8.6 23.3 copy-start.3
  55.5 0.6 copy-start.7
  55.5 2.5 copy-start.11
  60.7 366.1 %collective-permute-start = (bf16[8,2,512,128]{2,3,0,1:T(8,128)(2,1)}, bf16[8,2,512,128]{2,3,0,1:T(8,128)(2,1)}, u32[]{:S(2)}, u32[]{:S(2)}) collective-permute-start(bf16[8,2,512,128]{2,3,0,1:T(8,128)(2,1)} %pad_maximum_fusion), channel_id=1, source_target_pairs={{0,1},{1,0},{2,3},{3,2},{4,5},{5,4},{6,7},{7,6}} | collective-permute-start | bytes 6291464 | tf_op jit(solution)/shard_map/while/body/eval_jaxpr/ppermute | solution.py:86
  260.1 14.5 copy-start.8
  260.1 14.5 copy-start.12
  455.4 39.2 copy-start.1
  662.6 131.9 %collective-permute-start.1 = (f32[8,2,512,128]{3,2,0,1:T(8,128)}, f32[8,2,512,128]{3,2,0,1:T(8,128)}, u32[]{:S(2)}, u32[]{:S(2)}) collective-permute-start(f32[8,2,512,128]{3,2,0,1:T(8,128)} %get-tuple-element.235), channel_id=1, source_target_pairs={{0,1},{1,0},{2,3},{3,2},{4,5},{5,4},{6,7},{7,6}} | collective-permute-start | bytes 12582920 | tf_op jit(solution)/shard_map/while/body/eval_jaxpr/ppermute | solution.py:112
  794.5 285.4 %copy-start.9 = (f32[512,64]{0,1:T(8,128)S(1)}, f32[512,64]{0,1:T(8,128)}, u32[]{:S(2)}) copy-start(f32[512,64]{0,1:T(8,128)} %copy-done.7) | copy-start | bytes 393220
  794.5 285.4 %copy-start.13 = (f32[512,64]{0,1:T(8,128)S(1)}, f32[512,64]{0,1:T(8,128)}, u32[]{:S(2)}) copy-start(f32[512,64]{0,1:T(8,128)} %copy-done.11) | copy-start | bytes 393220
  879.6 313.8 %collective-permute-start.2 = (f32[8,2,512,128]{2,3,0,1:T(8,128)}, f32[8,2,512,128]{2,3,0,1:T(8,128)}, u32[]{:S(2)}, u32[]{:S(2)}) collective-permute-start(f32[8,2,512,128]{2,3,0,1:T(8,128)} %copy.39), channel_id=1, source_target_pairs={{0,1},{1,0},{2,3},{3,2},{4,5},{5,4},{6,7},{7,6}} | collective-permute-start | bytes 12582920 | tf_op jit(solution)/shard_map/ppermute | solution.py:119
  1193.4 5263.7 %all-reduce.8.cloned.1.call-start = ((), (), s32[]{:S(2)}) async-start(), calls=%async_computation.1 | async-start | bytes 163577856 | tf_op jit(solution)/shard_map/psum | solution.py:124
  2916.1 21.1 copy-start.10
  2916.1 21.1 copy-start.14
  2939.1 20.8 copy-start.5
  2939.1 20.8 copy-start.6
  6341.8 35.8 copy-start.4
Sparse Core Ops, SparseCore 0:
  1193.5 1719.4 all-reduce.5
  2960.1 194.7 all-reduce.7
where the time goes:
time: 6540 us
  blocking collectives  3290 us (50%)
  waiting for transfers between devices  1540 us (24%)
  matrix products  1040 us (16%)
  starting transfers between devices  327 us (5%)
  local copies, waits for them, and re-layouts  190 us (3%)
  other arithmetic  115 us (2%)
    psum x1, blocking collectives, local_program(): attn_out = lax.psum(out_part, 'tp').astype(jnp.bfloat16)  3290 us
    psum x1, waiting for transfers between devices, local_program(): lax.psum(jnp.einsum('cirf,eif->cre', dq_pre, w_query, preferred_element_t...  1540 us
    ppermute x1, starting transfers between devices, local_program(): dkv_blk = lax.ppermute(dkv_blk, 'cp', shift_pairs)  200 us
  transfers between devices with their start and end apart: 5, of which 2 were waited for; matrix products, arithmetic and copies ran while one was open for 13% of the time, Pallas kernels for 0%

commit v1 on v0

v1 whole, which is shorter than its diff:
```python
import functools

import jax
import jax.numpy as jnp
from jax import lax
from jax.experimental import pallas as pl
from jax.experimental.pallas import tpu as pltpu
from jax.sharding import PartitionSpec as P


F32 = jnp.float32
BF16 = jnp.bfloat16
ROPE_BASE = 10000.0
VMEM_LIMIT = 67043328
PIECE = 512
SUB = 256
E = 128
HALF = E // 2
ROWS = 2 * PIECE
N_SUB = ROWS // SUB
N_TILE = N_SUB * (N_SUB + 1) // 2
GROUP = 6
UNIT = 3
WIDE = GROUP * E
COLS = 512
DW_COLS = 1024
SCALE = E**-0.5


def rope_angles(n_pos):
    inv_freq = 1.0 / jnp.power(ROPE_BASE, jnp.arange(HALF, dtype=F32) * (2.0 / E))
    angles = jnp.arange(n_pos).astype(F32)[:, None] * inv_freq[None, :]
    return jnp.cos(angles), jnp.sin(angles)


def dot_nn(a, b):
    return jnp.dot(a, b, preferred_element_type=F32)


def dot_nt(a, b):
    return lax.dot_general(a, b, (((1,), (1,)), ((), ())), preferred_element_type=F32)


def lanes(parts):
    return jnp.concatenate(parts, axis=1)


def stack(parts):
    return jnp.concatenate(parts, axis=0)


def rows(p):
    return slice(PIECE * p, PIECE * (p + 1))


def heads(e):
    return slice(E * e, E * (e + 1))


def spec(block, index=None):
    rank = len(block)

    def full(*a):
        i = tuple(index(*a)) if index else ()
        return i + (0,) * (rank - len(i))

    mode = {} if index else {"pipeline_mode": pl.Buffered(1)}
    return pl.BlockSpec(block, full, **mode)


def struct(dtype, *shape):
    return jax.ShapeDtypeStruct(shape, dtype)


def call(body, grid, scal, ins, in_specs, outs, out_specs, flops, scratch=(), aliases=None):
    nbytes = sum(x.size * x.dtype.itemsize for x in jax.tree.leaves([ins, outs]))
    return pl.pallas_call(
        body,
        grid_spec=pltpu.PrefetchScalarGridSpec(
            num_scalar_prefetch=1, grid=grid, in_specs=in_specs, out_specs=out_specs, scratch_shapes=scratch
        ),
        out_shape=outs,
        input_output_aliases=aliases or {},
        cost_estimate=pl.CostEstimate(flops=int(flops), bytes_accessed=int(nbytes), transcendentals=0),
        compiler_params=pltpu.CompilerParams(vmem_limit_bytes=VMEM_LIMIT),
    )(scal, *ins)


def seq_of(l, s):
    return 2 * jnp.where(l == 0, s[0], 3 - s[0]) + s[1]


CHUNKS = 4


def proj_body(kind, n_w, n_kv, steps, nl, l0, s_ref, x_ref, r_ref, *refs):
    queries = kind == "q"
    if queries:
        cos_ref, sin_ref, *refs = refs
    w_refs, kv_refs, refs = refs[:n_w], refs[n_w : n_w + n_kv], refs[n_w + n_kv :]
    *outs, a_buf, w_buf, kv_buf, a_sem, w_sem, kv_sem = refs
    l, n = pl.program_id(0), pl.program_id(1)
    first = jnp.logical_and(l == 0, n == 0)
    d = x_ref.shape[-1]
    depth = d // CHUNKS
    c = s_ref[1]
    whole = slice(None)
    per = n_w // steps if n_w > 1 else 1

    def cut(k):
        return whole if k is None else pl.ds(k * depth, depth)

    def row_copies(i, k=None):
        return [
            pltpu.make_async_copy(src.at[at, :, cut(k)], a_buf.at[i, p, :, cut(k)], a_sem.at[i, p, k or 0])
            for p, (src, at) in enumerate(((x_ref, seq_of(i + l0, s_ref)), (r_ref, i + l0)))
        ]

    def weight_copies(j, k=None):
        copies = []
        for m in range(per):
            size = GROUP // per
            to = pl.ds(GROUP * j + size * m, size)
            src = w_refs[per * j + m] if n_w > 1 else w_refs[0]
            at = whole if n_w > 1 else pl.ds(GROUP * jnp.bitwise_xor(j, c), GROUP)
            at, to = ((at, cut(k)), (to, cut(k))) if queries else ((at, whole, cut(k)), (to, whole, cut(k)))
            copies.append(pltpu.make_async_copy(src.at[at], w_buf.at[to], w_sem.at[j, m, k or 0]))
        return copies

    def kv_copies():
        return [pltpu.make_async_copy(r, kv_buf.at[i], kv_sem.at[i]) for i, r in enumerate(kv_refs)]

    def wait(copies):
        for copy in copies:
            copy.wait()

    def product(i, h, k):
        a = stack([a_buf[i, p, :, cut(k)] for p in range(2)])
        if queries:
            return dot_nn(a, lanes([w_buf[h + e, cut(k), :] for e in range(GROUP)]))
        w = w_buf[pl.ds(h, GROUP), :, cut(k)]
        return dot_nt(a, w.reshape(WIDE, w.shape[2]))

    starts = [pl.multiple_of(PIECE * jnp.bitwise_xor(p, c), PIECE) for p in range(2)]

    def rotated(x, p):
        at = pl.ds(starts[p], PIECE)
        return x * cos_ref[at, :] + pltpu.roll(x, HALF, 1) * sin_ref[at, :]

    def store(x):
        for p in range(2):
            for e in range(GROUP):
                part = x[rows(p), heads(e)]
                outs[-1][p, e] = (rotated(part, p) * SCALE if queries else part).astype(BF16)

    @pl.when(first)
    def _():
        for k in range(CHUNKS):
            for copy in row_copies(0, k) + weight_copies(0, k):
                copy.start()
        later = [weight_copies(j) for j in range(1, steps)] + [kv_copies()] + [row_copies(i) for i in range(1, nl)]
        for copy in sum(later, []):
            copy.start()
        for k in range(CHUNKS):
            wait(row_copies(0, k) + weight_copies(0, k))
            part = product(0, 0, k)
            acc = part if k == 0 else acc + part
        store(acc)

    for i in range(1, nl):

        @pl.when(jnp.logical_and(l == i, n == 0))
        def _():
            wait(row_copies(i))

    for j in range(1, steps):

        @pl.when(jnp.logical_and(l == 0, n == j))
        def _():
            wait(weight_copies(j))

    @pl.when(jnp.logical_and(jnp.logical_not(first), n < steps))
    def _():
        store(product(l, GROUP * n, None))

    if n_kv:

        @pl.when(n == steps)
        def _():
            @pl.when(l == 0)
            def _():
                wait(kv_copies())

            x = dot_nn(stack([a_buf[l, p] for p in range(2)]), lanes([kv_buf[i] for i in range(n_kv)]))
            for p in range(2):
                outs[0][p] = rotated(x[rows(p), :E], p).astype(BF16)
                outs[1][p] = x[rows(p), E:].astype(BF16)


def proj(scal, kind, x, x_recv, weights, tables=(), kv=(), l0=0, nl=2):
    d = x.shape[-1]
    steps = 2 if len(weights) == 1 else len(weights) // 2
    hbm = pl.BlockSpec(memory_space=pl.ANY)
    kv_out = [struct(BF16, nl, 2, PIECE, E)] * len(kv)
    shape = (d, E) if kind == "q" else (E, d)
    dma = lambda *n: pltpu.SemaphoreType.DMA(n)
    return call(
        functools.partial(proj_body, kind, len(weights), len(kv), steps, nl, l0),
        (nl, steps + len(kv) // 2),
        scal,
        [x, x_recv, *tables, *weights, *kv],
        [hbm] * 2 + [spec((ROWS, E))] * len(tables) + [hbm] * (len(weights) + len(kv)),
        kv_out + [struct(BF16, nl, 2, steps * GROUP, PIECE, E)],
        [spec((None, 2, PIECE, E), lambda l, n, s: (l,))] * len(kv)
        + [spec((None, 2, GROUP, PIECE, E), lambda l, n, s: (l, 0, jnp.minimum(n, steps - 1)))],
        2 * nl * ROWS * d * steps * WIDE,
        scratch=[
            pltpu.VMEM((nl, 2, PIECE, d), BF16),
            pltpu.VMEM((steps * GROUP, *shape), BF16),
            pltpu.VMEM((len(kv) or 1, d if kv else GROUP, E), BF16),
            dma(nl, 2, CHUNKS),
            dma(steps, 2, CHUNKS),
            dma(2),
        ],
    )


def attn_body(mode, turned, s_ref, *refs):
    it = iter(refs)
    fwd, bwd = mode != "bwd", mode != "fwd"
    q_ref, k_ref, v_ref = next(it), next(it), next(it)
    if bwd:
        do_ref, cos_ref, sin_ref = next(it), next(it), next(it)
    if not fwd:
        ot_ref, lse_ref = next(it), next(it)
    if fwd:
        o_ref = next(it)
    if not bwd:
        ot_ref, lse_ref = next(it), next(it)
    if bwd:
        dq_ref, dk_ref, dv_ref = next(it), next(it), next(it)
    if turned:
        t_ref = next(it)
    keys, vals, keys_t, vals_t, s_buf, p_buf, ds_buf = it
    slot = [jnp.bitwise_xor(p, s_ref[1]) for p in range(2)]

    @pl.when(pl.program_id(1) == 0)
    def _():
        for p in range(2):
            kb, vb = k_ref[slot[p]], v_ref[slot[p]]
            keys[rows(p), :] = kb
            vals[rows(p), :] = vb
            keys_t[:, rows(p)] = kb.astype(F32).T.astype(BF16)
            vals_t[:, rows(p)] = vb.astype(F32).T.astype(BF16)
        if bwd:
            dk_ref[...] = jnp.zeros_like(dk_ref)
            dv_ref[...] = jnp.zeros_like(dv_ref)

    iota = functools.partial(lax.broadcasted_iota, jnp.int32, (SUB, SUB))
    causal = iota(0) <= iota(1)
    subs = range(N_SUB)
    tile = lambda j: slice(SUB * j, SUB * (j + 1))
    per = PIECE // SUB
    at = lambda i: (slot[i // per], tile(i % per))
    at_t = lambda i: (slot[i // per], slice(None), tile(i % per))
    base = lambda i, j: tile(i * (i + 1) // 2 + j)
    q = [q_ref[at(i)] for i in subs]
    d_o = [do_ref[at(i)] for i in subs] if bwd else None

    def score(i, j):
        s = dot_nt(keys[tile(j), :], q[i])
        return jnp.where(causal, s, -jnp.inf) if j == i else s

    top, inv, out_t = {}, {}, {}
    if fwd:
        for i in subs:
            for j in range(i + 1):
                s = score(i, j)
                s_buf[base(i, j), :] = s
                m = jnp.max(s, axis=0, keepdims=True)
                top[i] = m if j == 0 else jnp.maximum(top[i], m)
        for i in subs:
            for j in range(i + 1):
                p = jnp.exp(s_buf[base(i, j), :] - top[i])
                if bwd:
                    s_buf[base(i, j), :] = p
                part = jnp.sum(p, axis=0, keepdims=True)
                acc = dot_nn(vals_t[:, tile(j)], p.astype(BF16))
                total = part if j == 0 else total + part
                o_t = acc if j == 0 else o_t + acc
            inv[i] = 1.0 / total
            o_t = o_t * inv[i]
            out_t[i] = o_t.astype(BF16)
            o_ref[at(i)] = o_t.T.astype(BF16)
            if turned:
                t_ref[(slot[i // per], 0, slice(None), tile(i % per))] = out_t[i]
            if not bwd:
                ot_ref[at_t(i)] = out_t[i]
                lse_ref[:, tile(i)] = top[i] + jnp.log(total)
    if not bwd:
        return
    for i in subs:
        o_t = out_t[i] if fwd else ot_ref[at_t(i)]
        delta = jnp.sum(o_t.astype(F32) * d_o[i].astype(F32).T, axis=0, keepdims=True)
        for j in range(i + 1):
            p = s_buf[base(i, j), :] * inv[i] if fwd else jnp.exp(score(i, j) - lse_ref[:, tile(i)])
            dp = dot_nt(vals[tile(j), :], d_o[i])
            p_buf[tile(j), tile(i)] = p.astype(BF16)
            ds_buf[tile(j), tile(i)] = (p * (dp - delta)).astype(BF16)
    for i in subs:
        width = SUB * (i + 1)
        dq = dot_nn(keys_t[:, :width], ds_buf[:width, tile(i)]) * SCALE
        low, high, cos, sin = dq[:HALF], dq[HALF:], cos_ref[:, tile(i)], sin_ref[:, tile(i)]
        dq = stack([low * cos + high * sin, high * cos - low * sin])
        dq_ref[at(i)] = dq.T.astype(BF16)
        if turned:
            t_ref[(slot[i // per], 1, slice(None), tile(i % per))] = dq.astype(BF16)
    for j in subs:
        dv_ref[tile(j), :] += dot_nn(p_buf[tile(j), SUB * j :], stack(d_o[j:]))
        dk_ref[tile(j), :] += dot_nn(ds_buf[tile(j), SUB * j :], stack(q[j:]))


def attention(scal, mode, q, k, v, d_o=None, tables=(), saved=(), l0=0, turned=False):
    nl, _, n_heads = q.shape[:3]
    fwd, bwd = mode != "bwd", mode != "fwd"
    pick_head = lambda l, h, s: (l, 0, h)
    act = spec((None, 2, None, PIECE, E), pick_head)
    flat = spec((None, 2, None, E, PIECE), pick_head)
    kv_spec = spec((None, 2, PIECE, E), lambda l, h, s: (l + l0,))
    stat = spec((None, None, 1, ROWS), lambda l, h, s: (l, h))
    acc = spec((None, ROWS, E), lambda l, h, s: (l,))
    ins, specs, outs, out_specs = [q, k, v], [act, kv_spec, kv_spec], [], []
    act_shape = struct(BF16, nl, 2, n_heads, PIECE, E)
    if bwd:
        ins += [d_o, *tables]
        specs += [act] + [spec((HALF, ROWS))] * 2
    if not fwd:
        ins += saved
        specs += [flat, stat]
    if fwd:
        outs.append(act_shape)
        out_specs.append(act)
    if not bwd:
        outs += [struct(BF16, nl, 2, n_heads, E, PIECE), struct(F32, nl, n_heads, 1, ROWS)]
        out_specs += [flat, stat]
    if bwd:
        outs += [act_shape] + [struct(F32, nl, ROWS, E)] * 2
        out_specs += [act, acc, acc]
    if turned:
        outs.append(struct(BF16, nl, 2, n_heads, 2, E, PIECE))
        out_specs.append(spec((None, 2, None, 2, E, PIECE), pick_head))
    products = 2 * fwd + 4 * bwd + (not fwd)
    square = (ROWS, ROWS) if bwd else (SUB, SUB)
    return call(
        functools.partial(attn_body, mode, turned),
        (nl, n_heads),
        scal,
        ins,
        specs,
        outs,
        out_specs,
        nl * n_heads * products * 4 * E * SUB * SUB * N_TILE,
        scratch=[pltpu.VMEM((ROWS, E), BF16)] * 2
        + [pltpu.VMEM((E, ROWS), BF16)] * 2
        + [pltpu.VMEM((N_TILE * SUB if fwd else SUB, SUB), F32)]
        + [pltpu.VMEM(square, BF16)] * 2,
    )


def combine_body(kind, n_act, n_w, fresh, s_ref, *refs):
    acts, ws, refs = refs[:n_act], refs[n_act : n_act + n_w], refs[n_act + n_w :]
    c = s_ref[1]
    a = lanes([stack([r[0, h], r[1, h]]) for r in acts for h in range(r.shape[1])])
    pieces = [ws[0][pl.ds(GROUP * i, GROUP)] for i in (c, 1 - c)] + [w[...] for w in ws[1:]]
    if kind == "out":
        x = dot_nn(a, stack([w.reshape(w.shape[0] * E, w.shape[2]) for w in pieces]))
    else:
        x = dot_nt(a, lanes([w[h] for w in pieces for h in range(w.shape[0])] + [r[...] for r in refs[:2]]))
    x = x.astype(BF16)
    outs = refs[-3:] if fresh else refs[-2:]
    outs[0][...] = x[rows(0)]
    outs[1][...] = x[rows(1)]
    if fresh:
        outs[2][...] = x[rows(0)]


def combine(scal, kind, l, acts, ls, weights, kv=(), big=None):
    d = weights[0].shape[2 if kind == "out" else 1]
    in_specs = [
        spec((None, 2, a.shape[2], PIECE, E), lambda n, s, i=i: (i,)) for a, i in zip(acts, ls, strict=True)
    ]
    if kind == "out":
        in_specs += [spec((w.shape[0], E, COLS), lambda n, s: (0, 0, n)) for w in weights]
    else:
        in_specs += [spec((w.shape[0], COLS, E), lambda n, s: (0, n)) for w in weights]
        in_specs += [spec((COLS, E), lambda n, s: (n,))] * 2
    ins, aliases = [*acts, *weights, *kv], {}
    piece = spec((PIECE, COLS), lambda n, s: (0, n))
    fresh = big is None
    if not fresh:
        aliases = {1 + len(ins): 0}
        ins.append(big)
        in_specs.append(pl.BlockSpec(memory_space=pl.ANY))
    return call(
        functools.partial(combine_body, kind, len(acts), len(weights), fresh),
        (d // COLS,),
        scal,
        ins,
        in_specs,
        [struct(BF16, 8, PIECE, d)] + [struct(BF16, PIECE, d)] * (1 + fresh),
        [spec((None, PIECE, COLS), lambda n, s: (seq_of(l, s), 0, n))] + [piece] * (1 + fresh),
        2 * ROWS * sum(a.shape[2] for a in acts) * E * d,
        aliases=aliases,
    )


def dw_local_body(s_ref, t_ref, *refs):
    xs, o_ref = refs[:4], refs[4]
    a = lanes([stack([t_ref[l, p, h] for h in range(t_ref.shape[2])]) for l in range(2) for p in range(2)])
    o_ref[...] = dot_nn(a, stack([x[...] for x in xs])).reshape(o_ref.shape)


def dw_local(scal, which, turned, x, x_recv):
    d = x.shape[-1]
    block = (None, PIECE, DW_COLS)
    mine = [spec(block, lambda n, s, l=l: (seq_of(l, s), 0, n)) for l in range(2)]
    recv = [spec(block, lambda n, s, l=l: (l, 0, n)) for l in range(2)]
    n_heads = turned.shape[2]
    return call(
        dw_local_body,
        (d // DW_COLS,),
        scal,
        [turned, x, x_recv, x, x_recv],
        [spec((2, 2, n_heads, None, E, PIECE), lambda n, s: (0, 0, 0, which)), mine[0], recv[0], mine[1], recv[1]],
        struct(F32, n_heads, E, d),
        spec((n_heads, E, DW_COLS), lambda n, s: (0, 0, n)),
        4 * n_heads * E * ROWS * d,
    )


def dw_rest_body(n_t, last, flip, s_ref, *refs):
    ts, xs, refs = refs[:n_t], refs[n_t : n_t + 4], refs[n_t + 4 :]
    half = n_t // 4
    a = lanes([stack([t[h] for t in ts[half * g : half * (g + 1)] for h in range(UNIT)]) for g in range(4)])
    acc = dot_nn(a, stack([x[...] for x in xs])).reshape(GROUP, E, DW_COLS) + refs[0][...]
    if last:
        acc = acc + refs[1][...]
    outs = refs[-2:] if last else refs[-1:]
    for h in range(GROUP):
        x = acc[h].T if flip else acc[h]
        for o in outs:
            o[h] = x


def dw_rest(scal, which, half, turned, x, local, recv=None):
    d = x.shape[-1]
    last = recv is not None
    flip = last and which == 1
    specs = []
    for g, group in enumerate(turned):
        i = half ^ (g % 2)
        specs += [spec((UNIT, None, E, PIECE), lambda n, s, i=i: (i, which)) for _ in group]
    for g in range(4):
        seq = lambda s, g=g: 2 * jnp.bitwise_xor(s[0], 1 + g // 2) + jnp.bitwise_xor(s[1], g % 2)
        specs.append(spec((None, PIECE, DW_COLS), lambda n, s, seq=seq: (seq(s), 0, n)))
    block, at_n = (GROUP, E, DW_COLS), lambda n, s: (0, 0, n)
    specs += [spec(block, lambda n, s: (half, 0, n))]
    flat = [t for group in turned for t in group]
    ins = [*flat, x, x, x, x, local]
    outs, out_specs = [struct(F32, GROUP, E, d)], [spec(block, at_n)]
    if last:
        ins.append(recv)
        specs.append(spec(block, at_n))
        if flip:
            block = (GROUP, DW_COLS, E)
            outs = [struct(F32, n * GROUP, d, E) for n in (2, 1)]
            out_specs = [spec(block, lambda n, s: (s[1], n)), spec(block, lambda n, s: (0, n))]
        else:
            outs = [struct(F32, n * GROUP, E, d) for n in (2, 1)]
            out_specs = [spec(block, lambda n, s: (s[1], 0, n)), spec(block, at_n)]
    return call(
        functools.partial(dw_rest_body, len(flat), last, flip),
        (d // DW_COLS,),
        scal,
        ins,
        specs,
        outs,
        out_specs,
        4 * GROUP * E * ROWS * d,
    )


def copy_body(s_ref, x_ref, o_ref):
    o_ref[...] = x_ref[...]


def pick(indices, x, block):
    count, rest = indices.shape[0], x.shape[1:]
    return call(
        copy_body,
        (count,),
        indices,
        [x],
        [spec((block, *rest), lambda i, s: (s[i],))],
        struct(x.dtype, count * block, *rest),
        spec((block, *rest), lambda i, s: (i,)),
        x.size,
    )


def place_body(n, s_ref, *refs):
    for j in range(n):

        @pl.when(pl.program_id(0) == j)
        def _():
            refs[-1][...] = refs[j][...]


def place(seqs, big, pieces):
    n, d = len(pieces), big.shape[-1]
    return call(
        functools.partial(place_body, n),
        (n,),
        seqs,
        [*pieces, big],
        [spec((PIECE, d))] * n + [pl.BlockSpec(memory_space=pl.ANY)],
        struct(big.dtype, *big.shape),
        spec((None, PIECE, d), lambda i, s: (s[i],)),
        n * PIECE * d,
        aliases={1 + n: 0},
    )


def dkv_body(n, s_ref, *refs):
    acc = dot_nn(lanes([r[...].reshape(2 * E, PIECE) for r in refs[:n]]), stack([x[...] for x in refs[n:-2]]))
    for i, o in enumerate(refs[-2:]):
        o[...] = acc[E * i : E * (i + 1)].T


def d_w_kv(seqs, pieces, x):
    n, d = len(pieces), x.shape[-1]
    return call(
        functools.partial(dkv_body, n),
        (d // DW_COLS,),
        seqs,
        [*pieces] + [x] * n,
        [spec((2, E, PIECE))] * n
        + [spec((None, PIECE, DW_COLS), lambda i, s, j=j: (s[j], 0, i)) for j in range(n)],
        [struct(F32, d, E)] * 2,
        [spec((DW_COLS, E), lambda i, s: (i,))] * 2,
        4 * n * PIECE * E * d,
    )


def after(x, *deps):
    return lax.optimization_barrier((x, *deps))[0]


def solution(mesh):
    n_tp, n_cp = mesh.shape["tp"], mesh.shape["cp"]
    chips = range(n_tp)

    def on_chip(x):
        return lax.ppermute(x, "cp", [(c, n_cp - 1 - c) for c in range(n_cp)])

    def to_chip(x, flip):
        return lax.ppermute(x, "tp", [(i, i ^ flip) for i in chips])

    def to_chip_other(x, flip):
        pairs = [(i * n_cp + c, (i ^ flip) * n_cp + (1 - c)) for i in chips for c in range(n_cp)]
        return lax.ppermute(x, ("tp", "cp"), pairs)

    def spread(m, r):
        return [f(x, flip) for flip in (1, 2) for f, x in ((to_chip, m), (to_chip_other, r))] + [on_chip(r)]

    def swap_heads(x):
        return [
            f(x[0, p, GROUP * i : GROUP * (i + 1)], 1 + i)
            for i in range(2)
            for p, f in enumerate((to_chip, to_chip_other))
        ]

    def with_partner(ws):
        return [x for w in ws for x in (w, on_chip(w))]

    def relay(w_in, u, dep):
        ws = [after(w_in[a, u], dep) for a in (1, 2)]
        return with_partner(ws), to_chip(ws[u], 2 - u)

    def local_program(hidden, grad, w_query, w_key, w_value, w_out):
        t, c = lax.axis_index("tp"), lax.axis_index("cp")
        chain = [jnp.stack([t, c]).astype(jnp.int32)]

        def step(f, *args, **kw):
            out = f(chain[0], *args, **kw)
            chain[0] = after(chain[0], jax.tree.leaves(out)[0])
            return out

        cos, sin = rope_angles(ROWS)
        tables = lanes([cos, cos]), lanes([-sin, sin])
        tables_t = cos.T, sin.T
        wq, wo = w_query.transpose(1, 0, 2), w_out
        kv_w = (w_key, w_value)
        own, ext, nx, ny = 2 * t, 2 * (3 - t), 2 * (t ^ 1), 2 * (t ^ 2)
        theirs = jnp.stack([own + 1 - c, ext + 1 - c]).astype(jnp.int32)
        unit = lambda u: (2 * c + u).astype(jnp.int32)[None]

        wq_in, wo_in = {}, {}
        sent = pick(unit(0), wq, UNIT)
        for a in (1, 2):
            wq_in[a, 0] = to_chip(sent, a)
        sent = pick(after(theirs, sent), hidden, 1)
        h_recv = on_chip(sent)
        sent = pick(after(unit(0), sent), wo, UNIT)
        for a in (1, 2):
            wo_in[a, 0] = to_chip(sent, a)
        sent = pick(after(theirs, sent), grad, 1)
        g_recv = on_chip(sent)

        k, v, q_0 = step(proj, "q", hidden, h_recv, [wq], tables, kv=kv_w)
        sent_q = pick(after(unit(1), q_0), wq, UNIT)
        sent_o = pick(after(unit(1), sent_q), wo, UNIT)
        for w_in, sent in ((wq_in, sent_q), (wo_in, sent_o)):
            for a in (1, 2):
                w_in[a, 1] = to_chip(sent, a)
        chain[0] = after(chain[0], sent_o)
        (do_0,) = step(proj, "do", grad, g_recv, [wo])
        wq_n0, wq_d0 = relay(wq_in, 0, do_0)
        o_0, dq_0, dk_0, dv_0, t_0 = step(attention, "fused", q_0, k, v, do_0, tables_t, turned=True)
        dwo = step(dw_local, 0, t_0, grad, g_recv)

        wo_n0, wo_d0 = relay(wo_in, 0, dwo)
        (q_n0,) = step(proj, "q", hidden, h_recv, wq_n0, tables)
        (do_n0,) = step(proj, "do", grad, g_recv, wo_n0)
        wq_n1, wq_d1 = relay(wq_in, 1, do_n0)
        o_n0, dq_n0, dk_n0, dv_n0, t_n0 = step(attention, "fused", q_n0, k, v, do_n0, tables_t, turned=True)
        dwq = step(dw_local, 1, t_0, hidden, h_recv)
        wo_n1, wo_d1 = relay(wo_in, 1, dwq)
        (q_n1,) = step(proj, "q", hidden, h_recv, wq_n1, tables)
        (do_n1,) = step(proj, "do", grad, g_recv, wo_n1)
        t_nb0 = swap_heads(after(t_n0, do_n1))
        wq_d = with_partner([after(w, do_n1) for w in (wq_d0, wq_d1)])
        o_n1, dq_n1, dk_n1, dv_n1, t_n1 = step(attention, "fused", q_n1, k, v, do_n1, tables_t, turned=True)
        t_nb1 = swap_heads(t_n1)
        t_nb = list(zip(t_nb0, t_nb1, strict=True))

        wo_d = with_partner([after(w, o_n1) for w in (wo_d0, wo_d1)])
        wo_all = [wo, *wo_n0, *wo_n1, *wo_d]
        wq_all = [wq, *wq_n0, *wq_n1, *wq_d]
        (q_d,) = step(proj, "q", hidden, h_recv, wq_d, tables, nl=1)
        o_d, ot_d, lse_d = step(attention, "fwd", q_d, k, v)
        out_big, out_r, out_m = step(combine, "out", 0, [o_0, o_n0, o_n1, o_d], [0] * 4, wo_all)
        out_in = spread(out_m, out_r)
        (do_d,) = step(proj, "do", grad, g_recv, wo_d, nl=1)
        dq_d, dk_d, dv_d = step(attention, "bwd", q_d, k, v, do_d, tables_t, saved=[ot_d, lse_d])

        def finish_kv(l, *last):
            dk, dv = [
                x[l] + y[l] + z[l] + w[0]
                for x, y, z, w in zip((dk_0, dv_0), (dk_n0, dv_n0), (dk_n1, dv_n1), last, strict=True)
            ]
            dk = dk * tables[0] - jnp.roll(dk, HALF, axis=1) * tables[1]
            x = jnp.stack([dk, dv]).astype(BF16).reshape(2, 2, PIECE, E).transpose(1, 0, 2, 3)
            x = jnp.where(c == 0, x, x[::-1])
            return x[None], x.transpose(0, 1, 3, 2)

        dkv_0, dkv_t = finish_kv(0, dk_d, dv_d)
        dkv_in = spread(dkv_t[0], dkv_t[1])
        dh_big, dh_r, dh_m = step(combine, "dh", 0, [dq_0, dq_n0, dq_n1, dq_d, dkv_0], [0] * 5, wq_all, kv=kv_w)
        dh_in = spread(dh_m, dh_r)

        (q_e,) = step(proj, "q", hidden, h_recv, wq_d, tables, l0=1, nl=1)
        (do_e,) = step(proj, "do", grad, g_recv, wo_d, l0=1, nl=1)
        o_e, dq_e, dk_e, dv_e = step(attention, "fused", q_e, k, v, do_e, tables_t, l0=1)
        dkv_1, dkv_u = finish_kv(1, dk_e, dv_e)
        dkv_in.append(on_chip(dkv_u[1]))

        (wo_part,) = step(dw_rest, 0, 1, t_nb, grad, dwo)
        wo_part = on_chip(wo_part)
        (wq_part,) = step(dw_rest, 1, 1, t_nb, hidden, dwq)
        wq_part = on_chip(wq_part)
        out_big, out_er = step(combine, "out", 1, [o_0, o_n0, o_n1, o_e], [1, 1, 1, 0], wo_all, big=out_big)
        out_in.append(on_chip(out_er))
        dwo_big, dwo_mine = step(dw_rest, 0, 0, t_nb, grad, dwo, wo_part)
        dwo_theirs = on_chip(dwo_mine)
        dwq_big, dwq_mine = step(dw_rest, 1, 0, t_nb, hidden, dwq, wq_part)
        dwq_theirs = on_chip(dwq_mine)
        dh_big, dh_er = step(
            combine, "dh", 1, [dq_0, dq_n0, dq_n1, dq_e, dkv_1], [1, 1, 1, 0, 0], wq_all, kv=kv_w, big=dh_big
        )
        dh_in.append(on_chip(dh_er))

        seqs = [nx + c, nx + 1 - c, ny + c, ny + 1 - c, own + 1 - c, ext + 1 - c]
        put = lambda big, x: lax.dynamic_update_slice_in_dim(big, x, GROUP * (1 - c), 0)
        places = jnp.stack([*seqs, own + c, ext + c]).astype(jnp.int32)
        attn_out = place(after(places, dh_er), out_big, out_in)
        d_kv = d_w_kv(after(places, attn_out), [*dkv_in, dkv_t[0], dkv_u[0]], hidden)
        d_w_key, d_w_value = [x + on_chip(x) for x in d_kv]
        d_w_out = put(dwo_big, dwo_theirs)
        d_w_query = put(dwq_big, dwq_theirs).transpose(1, 0, 2)
        d_hidden = place(after(places, d_kv[0]), dh_big, dh_in)
        return attn_out, d_hidden, d_w_query, d_w_key, d_w_value, d_w_out

    row = P(None, "cp", None)
    wq_spec, wo_spec = P(None, "tp", None), P("tp", None, None)
    return jax.shard_map(
        local_program,
        mesh=mesh,
        in_specs=(row, row, wq_spec, P(), P(), wo_spec),
        out_specs=(row, row, wq_spec, P(), P(), wo_spec),
        check_vma=False,
    )
```

time: 6540 us -> 2020 us (0.31)
  blocking collectives: 3290 us -> 0 us
  Pallas kernels: 0 us -> 1430 us
  waiting for transfers between devices: 1540 us -> 468 us
  matrix products: 1040 us -> 0 us
  starting transfers between devices: 327 us -> 35.4 us
  local copies, waits for them, and re-layouts: 190 us -> 45.1 us
  other arithmetic: 115 us -> 28.9 us
    psum x1 -> x0, blocking collectives: 3290 us -> none  [local_program(): attn_out = lax.psum(out_part, 'tp').astype(jnp.bfloat16)]
    psum x2 -> x0, waiting for transfers between devices: 1540 us -> none  [the longest x1 1540 us: local_program(): lax.psum(jnp.einsum('cirf,eif->cre', dq_pre, w_query, preferred_element_t...]
    pallas_call x0 -> x35, Pallas kernels: none -> 1430 us  [call(): pl.pallas_call(body, grid_spec=pltpu.PrefetchScalarGridSpec(num_scalar_pr...]
    dot_general x19 -> x0, matrix products: 1040 us -> none  [the longest x1 94.1 us: local_program(): jnp.einsum('cre,cirf->eif', hidden, dq_pre, preferred_element_type=jnp.fl...]
    ppermute x3 -> x58, waiting for transfers between devices: 6.79 us -> 468 us  [the longest x10 373 us: to_chip_other(): return lax.ppermute(x, ('tp', 'cp'), pairs)]
    ppermute x3 -> x58, starting transfers between devices: 326 us -> 35.4 us  [the longest x22 21.1 us: to_chip(): return lax.ppermute(x, 'tp', [(i, i ^ flip) for i in chips])]
    unnamed x31 -> x30, local copies, waits for them, and re-layouts: 90.9 us -> 2.18 us
  transfers between devices with their start and end apart: 5 -> 58, of which waited for: 2 -> 16; matrix products, arithmetic and copies ran while one was open for 13% -> 3% of each run, Pallas kernels for 0% -> 69%
where the time goes in v1:
time: 2020 us; the launch traced here: 2010 us
  Pallas kernels  1430 us (71%)
  waiting for transfers between devices  468 us (23%)
  local copies, waits for them, and re-layouts  45.1 us (2%)
  starting transfers between devices  35.4 us (2%)
  other arithmetic  28.9 us (1%)
    pallas_call x35, Pallas kernels, call(): pl.pallas_call(body, grid_spec=pltpu.PrefetchScalarGridSpec(num_scalar_pr...  1430 us
    ppermute x10, waiting for transfers between devices, to_chip_other(): return lax.ppermute(x, ('tp', 'cp'), pairs)  373 us
    ppermute x22, waiting for transfers between devices, to_chip(): return lax.ppermute(x, 'tp', [(i, i ^ flip) for i in chips])  80.4 us
  transfers between devices with their start and end apart: 58, of which 16 were waited for; matrix products, arithmetic and copies ran while one was open for 3% of the time, Pallas kernels for 69%

profile of v1, /device:TPU:0, one launch (start us, length us, event | category | flops | bytes accessed | tf_op | source)
XLA Modules:
  0.0 2010.9 jit_solution(14971067373546721342)
XLA Ops:
  42.3 73.2 %shard_map.111 = (bf16[2,2,512,128]{3,2,1,0:T(8,128)(2,1)}, bf16[2,2,512,128]{3,2,1,0:T(8,128)(2,1)}, bf16[2,2,12,512,128]{4,3,2,1,0:T(8,128)(2,1)}) custom-call(s32[2]{0:T(128)} %pad_add_fusion.s_ref, bf16[8,512,6144]{2,1,0:T(8,128)(2,1)} %refs_15_.1, bf16[2,512,6144]{2,1,0:T(8,128)(2,1)} %collective-permute-done.r_ref.refs_1_.refs_3_, ...), custom_call_target="tpu_custom_call" | custom-call | flops 38654705664 | bytes 93323264 | tf_op jit(solution)/shard_map/pallas_call | solution.py:77
  125.1 50.7 %shard_map.116.refs_3_ = bf16[2,2,12,512,128]{4,3,2,1,0:T(8,128)(2,1)} custom-call(s32[2]{0:T(128)} %pad_add_fusion.s_ref, bf16[8,512,6144]{2,1,0:T(8,128)(2,1)} %refs_11_.7, bf16[2,512,6144]{2,1,0:T(8,128)(2,1)} %collective-permute-done.1.r_ref.refs_1_.refs_3_, bf16[12,128,6144]{2,1,0:T(8,128)(2,1)} %refs_4_.5), custom_call_target="tpu_custom_call" | custom-call | flops 38654705664 | bytes 88080384 | tf_op jit(solution)/shard_map/pallas_call | solution.py:77
  175.8 63.6 %shard_map.117 = (bf16[2,2,12,512,128]{4,3,2,1,0:T(8,128)(2,1)}, bf16[2,2,12,512,128]{4,3,2,1,0:T(8,128)(2,1)}, f32[2,1024,128]{2,1,0:T(8,128)}, f32[2,1024,128]...) custom-call(s32[2]{0:T(128)} %pad_add_fusion.s_ref, bf16[2,2,12,512,128]{4,3,2,1,0:T(8,128)(2,1)} %get-tuple-element.100.refs_0_, ...), custom_call_target="tpu_custom_call" | custom-call | flops 48318382080 | bytes 41418752 | tf_op jit(solution)/shard_map/pallas_call | solution.py:77
  240.0 48.1 %shard_map.118.refs_12_ = f32[12,128,6144]{2,1,0:T(8,128)} custom-call(s32[2]{0:T(128)} %pad_add_fusion.s_ref, bf16[2,2,12,2,128,512]{5,4,3,2,1,0:T(8,128)(2,1)} %get-tuple-element.110.t_ref, bf16[8,512,6144]{2,1,0:T(8,128)(2,1)} %refs_11_.7, bf16[2,512,6144]{2,1,0:T(8,128)(2,1)} %collective-permute-done.1.r_ref.refs_1_.refs_3_, ...), custom_call_target="tpu_custom_call" | custom-call | flops 38654705664 | bytes 176160768 | tf_op jit(solution)/shard_map/pallas_call | solution.py:77
  292.7 52.3 %shard_map.119.refs_0_ = bf16[2,2,12,512,128]{4,3,2,1,0:T(8,128)(2,1)} custom-call(s32[2]{0:T(128)} %pad_add_fusion.s_ref, bf16[8,512,6144]{2,1,0:T(8,128)(2,1)} %refs_15_.1, bf16[2,512,6144]{2,1,0:T(8,128)(2,1)} %collective-permute-done.r_ref.refs_1_.refs_3_, f32[1024,128]{1,0:T(8,128)} %get-tuple-element.215.refs_0_, ...), custom_call_target="tpu_custom_call" | custom-call | flops 38654705664 | bytes 89128960 | tf_op jit(solution)/shard_map/pallas_call | solution.py:77
  345.0 50.2 %shard_map.120.refs_3_ = bf16[2,2,12,512,128]{4,3,2,1,0:T(8,128)(2,1)} custom-call(s32[2]{0:T(128)} %pad_add_fusion.s_ref, bf16[8,512,6144]{2,1,0:T(8,128)(2,1)} %refs_11_.7, bf16[2,512,6144]{2,1,0:T(8,128)(2,1)} %collective-permute-done.1.r_ref.refs_1_.refs_3_, bf16[3,128,6144]{2,1,0:T(8,128)(2,1)} %collective-permute-done.6.refs_0_.refs_5_, ...), custom_call_target="tpu_custom_call" | custom-call | flops 38654705664 | bytes 88080384 | tf_op jit(solution)/shard_map/pallas_call | solution.py:77
  395.2 63.7 %shard_map.121 = (bf16[2,2,12,512,128]{4,3,2,1,0:T(8,128)(2,1)}, bf16[2,2,12,512,128]{4,3,2,1,0:T(8,128)(2,1)}, f32[2,1024,128]{2,1,0:T(8,128)}, f32[2,1024,128]...) custom-call(s32[2]{0:T(128)} %pad_add_fusion.s_ref, bf16[2,2,12,512,128]{4,3,2,1,0:T(8,128)(2,1)} %shard_map.119.refs_0_, ...), custom_call_target="tpu_custom_call" | custom-call | flops 48318382080 | bytes 41418752 | tf_op jit(solution)/shard_map/pallas_call | solution.py:77
  459.4 48.1 %shard_map.122.refs_12_ = f32[12,128,6144]{2,1,0:T(8,128)} custom-call(s32[2]{0:T(128)} %pad_add_fusion.s_ref, bf16[2,2,12,2,128,512]{5,4,3,2,1,0:T(8,128)(2,1)} %get-tuple-element.110.t_ref, bf16[8,512,6144]{2,1,0:T(8,128)(2,1)} %refs_15_.1, bf16[2,512,6144]{2,1,0:T(8,128)(2,1)} %collective-permute-done.r_ref.refs_1_.refs_3_, ...), custom_call_target="tpu_custom_call" | custom-call | flops 38654705664 | bytes 176160768 | tf_op jit(solution)/shard_map/pallas_call | solution.py:77
  512.1 52.0 %shard_map.123.refs_0_ = bf16[2,2,12,512,128]{4,3,2,1,0:T(8,128)(2,1)} custom-call(s32[2]{0:T(128)} %pad_add_fusion.s_ref, bf16[8,512,6144]{2,1,0:T(8,128)(2,1)} %refs_15_.1, bf16[2,512,6144]{2,1,0:T(8,128)(2,1)} %collective-permute-done.r_ref.refs_1_.refs_3_, f32[1024,128]{1,0:T(8,128)} %get-tuple-element.215.refs_0_, ...), custom_call_target="tpu_custom_call" | custom-call | flops 38654705664 | bytes 89128960 | tf_op jit(solution)/shard_map/pallas_call | solution.py:77
  564.2 50.1 %shard_map.124.refs_3_ = bf16[2,2,12,512,128]{4,3,2,1,0:T(8,128)(2,1)} custom-call(s32[2]{0:T(128)} %pad_add_fusion.s_ref, bf16[8,512,6144]{2,1,0:T(8,128)(2,1)} %refs_11_.7, bf16[2,512,6144]{2,1,0:T(8,128)(2,1)} %collective-permute-done.1.r_ref.refs_1_.refs_3_, bf16[3,128,6144]{2,1,0:T(8,128)(2,1)} %collective-permute-done.14.refs_0_.refs_9_, ...), custom_call_target="tpu_custom_call" | custom-call | flops 38654705664 | bytes 88080384 | tf_op jit(solution)/shard_map/pallas_call | solution.py:77
  615.1 63.6 %shard_map.125 = (bf16[2,2,12,512,128]{4,3,2,1,0:T(8,128)(2,1)}, bf16[2,2,12,512,128]{4,3,2,1,0:T(8,128)(2,1)}, f32[2,1024,128]{2,1,0:T(8,128)}, f32[2,1024,128]...) custom-call(s32[2]{0:T(128)} %pad_add_fusion.s_ref, bf16[2,2,12,512,128]{4,3,2,1,0:T(8,128)(2,1)} %shard_map.123.refs_0_, ...), custom_call_target="tpu_custom_call" | custom-call | flops 48318382080 | bytes 41418752 | tf_op jit(solution)/shard_map/pallas_call | solution.py:77
  678.7 34.8 %collective-permute-done.22.refs_13_.refs_0_ = bf16[3,128,6144]{2,1,0:T(8,128)(2,1)} collective-permute-done((bf16[3,128,6144]{2,1,0:T(8,128)(2,1)}, bf16[3,128,6144]{2,1,0:T(8,128)(2,1)}, u32[]{:S(2)}, u32[]{:S(2)}) %collective-permute-start.22) | collective-permute-done | bytes 4718624 | tf_op jit(solution)/shard_map/ppermute | solution.py:567
  784.0 88.8 %shard_map.128 = (bf16[8,512,6144]{2,1,0:T(8,128)(2,1)}, bf16[512,6144]{1,0:T(8,128)(2,1)}, bf16[512,6144]{1,0:T(8,128)(2,1)}) custom-call(s32[2]{0:T(128)} %pad_add_fusion.s_ref, bf16[2,2,12,512,128]{4,3,2,1,0:T(8,128)(2,1)} %get-tuple-element.108.refs_0_, bf16[2,2,12,512,128]{4,3,2,1,0:T(8,128)(2,1)} %get-tuple-element.118.refs_1_, ...), custom_call_target="tpu_custom_call" | custom-call | flops 77309411328 | bytes 160432128 | tf_op jit(solution)/shard_map/pallas_call | solution.py:77
  935.2 93.3 %shard_map.131 = (bf16[8,512,6144]{2,1,0:T(8,128)(2,1)}, bf16[512,6144]{1,0:T(8,128)(2,1)}, bf16[512,6144]{1,0:T(8,128)(2,1)}) custom-call(s32[2]{0:T(128)} %pad_add_fusion.s_ref, bf16[2,2,12,512,128]{4,3,2,1,0:T(8,128)(2,1)} %get-tuple-element.143.refs_0_, bf16[2,2,12,512,128]{4,3,2,1,0:T(8,128)(2,1)} %get-tuple-element.144.refs_1_, ...), custom_call_target="tpu_custom_call" | custom-call | flops 80530636800 | bytes 164102144 | tf_op jit(solution)/shard_map/pallas_call | solution.py:77
  1093.1 32.9 %shard_map.134 = (bf16[1,2,12,512,128]{4,3,2,1,0:T(8,128)(2,1)}, bf16[1,2,12,512,128]{4,3,2,1,0:T(8,128)(2,1)}, f32[1,1024,128]{2,1,0:T(8,128)}, f32[1,1024,128]{2,1,0:T(8,128)}) custom-call(s32[2]{0:T(128)} %pad_add_fusion.s_ref, bf16[1,2,12,512,128]{4,3,2,1,0:T(8,128)(2,1)} %shard_map.132.refs_0_, bf16[2,2,512,128]{3,2,1,0:T(8,128)(2,1)} %get-tuple-element.98.refs_1_, ...), custom_call_target="tpu_custom_call" | custom-call | flops 24159191040 | bytes 15204352 | tf_op jit(solution)/shard_map/pallas_call | solution.py:77
  1160.1 33.5 %collective-permute-done.33.refs_7_ = bf16[6,2,128,512]{3,2,1,0:T(8,128)(2,1)} collective-permute-done((bf16[6,2,128,512]{3,2,1,0:T(8,128)(2,1)}, bf16[6,2,128,512]{3,2,1,0:T(8,128)(2,1)}, u32[]{:S(2)}, u32[]{:S(2)}) %collective-permute-start.33) | collective-permute-done | bytes 1572896 | tf_op jit(solution)/shard_map/ppermute | solution.py:571
  1282.1 88.6 %shard_map.137 = (bf16[8,512,6144]{2,1,0:T(8,128)(2,1)}, bf16[512,6144]{1,0:T(8,128)(2,1)}) custom-call(s32[2]{0:T(128)} %pad_add_fusion.s_ref, bf16[2,2,12,512,128]{4,3,2,1,0:T(8,128)(2,1)} %get-tuple-element.108.refs_0_, bf16[2,2,12,512,128]{4,3,2,1,0:T(8,128)(2,1)} %get-tuple-element.118.refs_1_, ...), custom_call_target="tpu_custom_call", output_to_operand_aliasing={{0}: (18, {})} | custom-call | flops 77309411328 | bytes 204472320 | tf_op jit(solution)/shard_map/pallas_call | solution.py:77
  1370.8 40.1 %collective-permute-done.36.refs_0_ = bf16[512,6144]{1,0:T(8,128)(2,1)} collective-permute-done((bf16[512,6144]{1,0:T(8,128)(2,1)}, bf16[512,6144]{1,0:T(8,128)(2,1)}, u32[]{:S(2)}, u32[]{:S(2)}) %collective-permute-start.36) | collective-permute-done | bytes 6291488 | tf_op jit(solution)/shard_map/ppermute | solution.py:567
  1411.4 39.7 %shard_map.138 = (f32[12,128,6144]{2,1,0:T(8,128)}, f32[6,128,6144]{2,1,0:T(8,128)}) custom-call(s32[2]{0:T(128)} %pad_add_fusion.s_ref, bf16[6,2,128,512]{3,2,1,0:T(8,128)(2,1)} %collective-permute-done.26.refs_0_, bf16[6,2,128,512]{3,2,1,0:T(8,128)(2,1)} %collective-permute-done.27.refs_1_, bf16[6,2,128,512]{3,2,1,0:T(8,128)(2,1)} %collective-permute-done.28.refs_2_, ...), custom_call_target="tpu_custom_call" | custom-call | flops 19327352832 | bytes 327155712 | tf_op jit(solution)/shard_map/pallas_call | solution.py:77
  1451.1 40.6 %shard_map.139 = (f32[12,6144,128]{2,1,0:T(8,128)}, f32[6,6144,128]{2,1,0:T(8,128)}) custom-call(s32[2]{0:T(128)} %pad_add_fusion.s_ref, bf16[6,2,128,512]{3,2,1,0:T(8,128)(2,1)} %collective-permute-done.26.refs_0_, bf16[6,2,128,512]{3,2,1,0:T(8,128)(2,1)} %collective-permute-done.27.refs_1_, bf16[6,2,128,512]{3,2,1,0:T(8,128)(2,1)} %collective-permute-done.28.refs_2_, ...), custom_call_target="tpu_custom_call" | custom-call | flops 19327352832 | bytes 327155712 | tf_op jit(solution)/shard_map/pallas_call | solution.py:77
  1491.7 52.1 %collective-permute-done.37.refs_1_ = bf16[512,6144]{1,0:T(8,128)(2,1)} collective-permute-done((bf16[512,6144]{1,0:T(8,128)(2,1)}, bf16[512,6144]{1,0:T(8,128)(2,1)}, u32[]{:S(2)}, u32[]{:S(2)}) %collective-permute-start.37) | collective-permute-done | bytes 6291488 | tf_op jit(solution)/shard_map/ppermute | solution.py:571
  1554.7 93.2 %shard_map.140 = (bf16[8,512,6144]{2,1,0:T(8,128)(2,1)}, bf16[512,6144]{1,0:T(8,128)(2,1)}) custom-call(s32[2]{0:T(128)} %pad_add_fusion.s_ref, bf16[2,2,12,512,128]{4,3,2,1,0:T(8,128)(2,1)} %get-tuple-element.143.refs_0_, bf16[2,2,12,512,128]{4,3,2,1,0:T(8,128)(2,1)} %get-tuple-element.144.refs_1_, ...), custom_call_target="tpu_custom_call", output_to_operand_aliasing={{0}: (21, {})} | custom-call | flops 80530636800 | bytes 208142336 | tf_op jit(solution)/shard_map/pallas_call | solution.py:77
  1698.6 120.5 %collective-permute-done.49.refs_1_ = bf16[512,6144]{1,0:T(8,128)(2,1)} collective-permute-done((bf16[512,6144]{1,0:T(8,128)(2,1)}, bf16[512,6144]{1,0:T(8,128)(2,1)}, u32[]{:S(2)}, u32[]{:S(2)}) %collective-permute-start.49) | collective-permute-done | bytes 6291488 | tf_op jit(solution)/shard_map/ppermute | solution.py:571
  1834.6 123.2 %collective-permute-done.51.refs_3_ = bf16[512,6144]{1,0:T(8,128)(2,1)} collective-permute-done((bf16[512,6144]{1,0:T(8,128)(2,1)}, bf16[512,6144]{1,0:T(8,128)(2,1)}, u32[]{:S(2)}, u32[]{:S(2)}) %collective-permute-start.51) | collective-permute-done | bytes 6291488 | tf_op jit(solution)/shard_map/ppermute | solution.py:571
  (192 shorter events, 512.3 us)
Async XLA Ops:
  30.4 209.0 %collective-permute-start.2 = (bf16[3,6144,128]{2,1,0:T(8,128)(2,1)}, bf16[3,6144,128]{2,1,0:T(8,128)(2,1)}, u32[]{:S(2)}, u32[]{:S(2)}) collective-permute-start(bf16[3,6144,128]{2,1,0:T(8,128)(2,1)} %shard_map.109), channel_id=1, source_target_pairs={{0,2},{2,0},{4,6},{6,4},{1,3},{3,1},{5,7},{7,5}} | collective-permute-start | bytes 14155784 | tf_op jit(solution)/shard_map/ppermute | solution.py:567
  33.4 206.1 %collective-permute-start.4 = (bf16[3,6144,128]{2,1,0:T(8,128)(2,1)}, bf16[3,6144,128]{2,1,0:T(8,128)(2,1)}, u32[]{:S(2)}, u32[]{:S(2)}) collective-permute-start(bf16[3,6144,128]{2,1,0:T(8,128)(2,1)} %shard_map.109), channel_id=1, source_target_pairs={{0,4},{2,6},{4,0},{6,2},{1,5},{3,7},{5,1},{7,3}} | collective-permute-start | bytes 14155784 | tf_op jit(solution)/shard_map/ppermute | solution.py:567
  34.9 253.2 %collective-permute-start.6 = (bf16[3,128,6144]{2,1,0:T(8,128)(2,1)}, bf16[3,128,6144]{2,1,0:T(8,128)(2,1)}, u32[]{:S(2)}, u32[]{:S(2)}) collective-permute-start(bf16[3,128,6144]{2,1,0:T(8,128)(2,1)} %shard_map.114), channel_id=1, source_target_pairs={{0,2},{2,0},{4,6},{6,4},{1,3},{3,1},{5,7},{7,5}} | collective-permute-start | bytes 14155784 | tf_op jit(solution)/shard_map/ppermute | solution.py:567
  42.3 245.8 %collective-permute-start.8 = (bf16[3,128,6144]{2,1,0:T(8,128)(2,1)}, bf16[3,128,6144]{2,1,0:T(8,128)(2,1)}, u32[]{:S(2)}, u32[]{:S(2)}) collective-permute-start(bf16[3,128,6144]{2,1,0:T(8,128)(2,1)} %shard_map.114), channel_id=1, source_target_pairs={{0,4},{2,6},{4,0},{6,2},{1,5},{3,7},{5,1},{7,3}} | collective-permute-start | bytes 14155784 | tf_op jit(solution)/shard_map/ppermute | solution.py:567
  288.6 170.3 %collective-permute-start.10 = (bf16[3,6144,128]{2,1,0:T(8,128)(2,1)}, bf16[3,6144,128]{2,1,0:T(8,128)(2,1)}, u32[]{:S(2)}, u32[]{:S(2)}) collective-permute-start(bf16[3,6144,128]{2,1,0:T(8,128)(2,1)} %shard_map.112), channel_id=1, source_target_pairs={{0,2},{2,0},{4,6},{6,4},{1,3},{3,1},{5,7},{7,5}} | collective-permute-start | bytes 14155784 | tf_op jit(solution)/shard_map/ppermute | solution.py:567
  290.6 168.3 %collective-permute-start.12 = (bf16[3,6144,128]{2,1,0:T(8,128)(2,1)}, bf16[3,6144,128]{2,1,0:T(8,128)(2,1)}, u32[]{:S(2)}, u32[]{:S(2)}) collective-permute-start(bf16[3,6144,128]{2,1,0:T(8,128)(2,1)} %shard_map.112), channel_id=1, source_target_pairs={{0,4},{2,6},{4,0},{6,2},{1,5},{3,7},{5,1},{7,3}} | collective-permute-start | bytes 14155784 | tf_op jit(solution)/shard_map/ppermute | solution.py:567
  292.1 215.4 %collective-permute-start.14 = (bf16[3,128,6144]{2,1,0:T(8,128)(2,1)}, bf16[3,128,6144]{2,1,0:T(8,128)(2,1)}, u32[]{:S(2)}, u32[]{:S(2)}) collective-permute-start(bf16[3,128,6144]{2,1,0:T(8,128)(2,1)} %shard_map.113), channel_id=1, source_target_pairs={{0,2},{2,0},{4,6},{6,4},{1,3},{3,1},{5,7},{7,5}} | collective-permute-start | bytes 14155784 | tf_op jit(solution)/shard_map/ppermute | solution.py:567
  345.0 162.6 %collective-permute-start.16 = (bf16[3,128,6144]{2,1,0:T(8,128)(2,1)}, bf16[3,128,6144]{2,1,0:T(8,128)(2,1)}, u32[]{:S(2)}, u32[]{:S(2)}) collective-permute-start(bf16[3,128,6144]{2,1,0:T(8,128)(2,1)} %shard_map.113), channel_id=1, source_target_pairs={{0,4},{2,6},{4,0},{6,2},{1,5},{3,7},{5,1},{7,3}} | collective-permute-start | bytes 14155784 | tf_op jit(solution)/shard_map/ppermute | solution.py:567
  510.1 203.4 %collective-permute-start.22 = (bf16[3,128,6144]{2,1,0:T(8,128)(2,1)}, bf16[3,128,6144]{2,1,0:T(8,128)(2,1)}, u32[]{:S(2)}, u32[]{:S(2)}) collective-permute-start(bf16[3,128,6144]{2,1,0:T(8,128)(2,1)} %collective-permute-done.6.refs_0_.refs_5_), channel_id=1, source_target_pairs={{0,4},{2,6},{4,0},{6,2},{1,5},{3,7},{5,1},{7,3}} | collective-permute-start | bytes 14155784 | tf_op jit(solution)/shard_map/ppermute | solution.py:567
  564.2 150.8 %collective-permute-start.24 = (bf16[3,128,6144]{2,1,0:T(8,128)(2,1)}, bf16[3,128,6144]{2,1,0:T(8,128)(2,1)}, u32[]{:S(2)}, u32[]{:S(2)}) collective-permute-start(bf16[3,128,6144]{2,1,0:T(8,128)(2,1)} %collective-permute-done.16.refs_2_.refs_11_), channel_id=1, source_target_pairs={{0,2},{2,0},{4,6},{6,4},{1,3},{3,1},{5,7},{7,5}} | collective-permute-start | bytes 14155784 | tf_op jit(solution)/shard_map/ppermute | solution.py:567
  724.5 366.3 %collective-permute-start.26 = (bf16[6,2,128,512]{3,2,1,0:T(8,128)(2,1)}, bf16[6,2,128,512]{3,2,1,0:T(8,128)(2,1)}, u32[]{:S(2)}, u32[]{:S(2)}) collective-permute-start(bf16[6,2,128,512]{3,2,1,0:T(8,128)(2,1)} %get-tuple-element.195), channel_id=1, source_target_pairs={{0,2},{2,0},{4,6},{6,4},{1,3},{3,1},{5,7},{7,5}} | collective-permute-start | bytes 4718600 | tf_op jit(solution)/shard_map/ppermute | solution.py:567
  729.7 361.6 %collective-permute-start.27 = (bf16[6,2,128,512]{3,2,1,0:T(8,128)(2,1)}, bf16[6,2,128,512]{3,2,1,0:T(8,128)(2,1)}, u32[]{:S(2)}, u32[]{:S(2)}) collective-permute-start(bf16[6,2,128,512]{3,2,1,0:T(8,128)(2,1)} %get-tuple-element.191), channel_id=1, source_target_pairs={{0,2},{2,0},{4,6},{6,4},{1,3},{3,1},{5,7},{7,5}} | collective-permute-start | bytes 4718600 | tf_op jit(solution)/shard_map/ppermute | solution.py:567
  731.4 360.6 %collective-permute-start.28 = (bf16[6,2,128,512]{3,2,1,0:T(8,128)(2,1)}, bf16[6,2,128,512]{3,2,1,0:T(8,128)(2,1)}, u32[]{:S(2)}, u32[]{:S(2)}) collective-permute-start(bf16[6,2,128,512]{3,2,1,0:T(8,128)(2,1)} %get-tuple-element.194), channel_id=1, source_target_pairs={{0,3},{1,2},{2,1},{3,0},{4,7},{5,6},{6,5},{7,4}} | collective-permute-start | bytes 4718600 | tf_op jit(solution)/shard_map/ppermute | solution.py:571
  780.8 345.1 %collective-permute-start.29 = (bf16[6,2,128,512]{3,2,1,0:T(8,128)(2,1)}, bf16[6,2,128,512]{3,2,1,0:T(8,128)(2,1)}, u32[]{:S(2)}, u32[]{:S(2)}) collective-permute-start(bf16[6,2,128,512]{3,2,1,0:T(8,128)(2,1)} %get-tuple-element.190), channel_id=1, source_target_pairs={{0,3},{1,2},{2,1},{3,0},{4,7},{5,6},{6,5},{7,4}} | collective-permute-start | bytes 4718600 | tf_op jit(solution)/shard_map/ppermute | solution.py:571
  782.5 343.5 %collective-permute-start.30 = (bf16[6,2,128,512]{3,2,1,0:T(8,128)(2,1)}, bf16[6,2,128,512]{3,2,1,0:T(8,128)(2,1)}, u32[]{:S(2)}, u32[]{:S(2)}) collective-permute-start(bf16[6,2,128,512]{3,2,1,0:T(8,128)(2,1)} %get-tuple-element.193), channel_id=1, source_target_pairs={{0,4},{2,6},{4,0},{6,2},{1,5},{3,7},{5,1},{7,3}} | collective-permute-start | bytes 4718600 | tf_op jit(solution)/shard_map/ppermute | solution.py:567
  1222.6 188.2 %collective-permute-start.34 = (f32[6,128,6144]{2,1,0:T(8,128)}, f32[6,128,6144]{2,1,0:T(8,128)}, u32[]{:S(2)}, u32[]{:S(2)}) collective-permute-start(f32[6,128,6144]{2,1,0:T(8,128)} %shard_map.135), channel_id=1, source_target_pairs={{0,1},{1,0},{2,3},{3,2},{4,5},{5,4},{6,7},{7,6}} | collective-permute-start | bytes 56623112 | tf_op jit(solution)/shard_map/ppermute | solution.py:564
  1252.6 158.3 %collective-permute-start.35 = (f32[6,128,6144]{2,1,0:T(8,128)}, f32[6,128,6144]{2,1,0:T(8,128)}, u32[]{:S(2)}, u32[]{:S(2)}) collective-permute-start(f32[6,128,6144]{2,1,0:T(8,128)} %shard_map.136), channel_id=1, source_target_pairs={{0,1},{1,0},{2,3},{3,2},{4,5},{5,4},{6,7},{7,6}} | collective-permute-start | bytes 56623112 | tf_op jit(solution)/shard_map/ppermute | solution.py:564
  1281.5 266.0 %collective-permute-start.38 = (bf16[512,6144]{1,0:T(8,128)(2,1)}, bf16[512,6144]{1,0:T(8,128)(2,1)}, u32[]{:S(2)}, u32[]{:S(2)}) collective-permute-start(bf16[512,6144]{1,0:T(8,128)(2,1)} %get-tuple-element.176), channel_id=1, source_target_pairs={{0,4},{2,6},{4,0},{6,2},{1,5},{3,7},{5,1},{7,3}} | collective-permute-start | bytes 18874376 | tf_op jit(solution)/shard_map/ppermute | solution.py:567
  1282.1 261.7 %collective-permute-start.37 = (bf16[512,6144]{1,0:T(8,128)(2,1)}, bf16[512,6144]{1,0:T(8,128)(2,1)}, u32[]{:S(2)}, u32[]{:S(2)}) collective-permute-start(bf16[512,6144]{1,0:T(8,128)(2,1)} %get-tuple-element.177), channel_id=1, source_target_pairs={{0,3},{1,2},{2,1},{3,0},{4,7},{5,6},{6,5},{7,4}} | collective-permute-start | bytes 18874376 | tf_op jit(solution)/shard_map/ppermute | solution.py:571
  1543.8 439.4 %collective-permute-start.54 = (f32[6,6144,128]{2,1,0:T(8,128)}, f32[6,6144,128]{2,1,0:T(8,128)}, u32[]{:S(2)}, u32[]{:S(2)}) collective-permute-start(f32[6,6144,128]{2,1,0:T(8,128)} %get-tuple-element.185), channel_id=1, source_target_pairs={{0,1},{1,0},{2,3},{3,2},{4,5},{5,4},{6,7},{7,6}} | collective-permute-start | bytes 56623112 | tf_op jit(solution)/shard_map/ppermute | solution.py:564
  1547.5 150.8 %collective-permute-start.48 = (bf16[512,6144]{1,0:T(8,128)(2,1)}, bf16[512,6144]{1,0:T(8,128)(2,1)}, u32[]{:S(2)}, u32[]{:S(2)}) collective-permute-start(bf16[512,6144]{1,0:T(8,128)(2,1)} %get-tuple-element.182), channel_id=1, source_target_pairs={{0,2},{2,0},{4,6},{6,4},{1,3},{3,1},{5,7},{7,5}} | collective-permute-start | bytes 18874376 | tf_op jit(solution)/shard_map/ppermute | solution.py:567
  1553.3 266.6 %collective-permute-start.50 = (bf16[512,6144]{1,0:T(8,128)(2,1)}, bf16[512,6144]{1,0:T(8,128)(2,1)}, u32[]{:S(2)}, u32[]{:S(2)}) collective-permute-start(bf16[512,6144]{1,0:T(8,128)(2,1)} %get-tuple-element.182), channel_id=1, source_target_pairs={{0,4},{2,6},{4,0},{6,2},{1,5},{3,7},{5,1},{7,3}} | collective-permute-start | bytes 18874376 | tf_op jit(solution)/shard_map/ppermute | solution.py:567
  1554.0 265.1 %collective-permute-start.49 = (bf16[512,6144]{1,0:T(8,128)(2,1)}, bf16[512,6144]{1,0:T(8,128)(2,1)}, u32[]{:S(2)}, u32[]{:S(2)}) collective-permute-start(bf16[512,6144]{1,0:T(8,128)(2,1)} %get-tuple-element.183), channel_id=1, source_target_pairs={{0,3},{1,2},{2,1},{3,0},{4,7},{5,6},{6,5},{7,4}} | collective-permute-start | bytes 18874376 | tf_op jit(solution)/shard_map/ppermute | solution.py:571
  1554.4 443.4 %collective-permute-start.57 = (f32[6,128,6144]{2,1,0:T(8,128)}, f32[6,128,6144]{2,1,0:T(8,128)}, u32[]{:S(2)}, u32[]{:S(2)}) collective-permute-start(f32[6,128,6144]{2,1,0:T(8,128)} %get-tuple-element.187), channel_id=1, source_target_pairs={{0,1},{1,0},{2,3},{3,2},{4,5},{5,4},{6,7},{7,6}} | collective-permute-start | bytes 56623112 | tf_op jit(solution)/shard_map/ppermute | solution.py:564
  (49 other events, 2706.8 us)

commit v2 on v1

v2 whole, which is shorter than its diff:
```python
import functools

import jax
import jax.numpy as jnp
from jax import lax
from jax.experimental import pallas as pl
from jax.experimental.pallas import tpu as pltpu
from jax.sharding import PartitionSpec as P


F32 = jnp.float32
BF16 = jnp.bfloat16
ROPE_BASE = 10000.0
VMEM_LIMIT = 67043328
PIECE = 512
SUB = 256
E = 128
HALF = E // 2
ROWS = 2 * PIECE
N_SUB = ROWS // SUB
N_TILE = N_SUB * (N_SUB + 1) // 2
GROUP = 6
UNIT = 3
WIDE = GROUP * E
COLS = 512
DW_COLS = 1024
SCALE = E**-0.5
OWN = "own"
ALL = slice(None)
HBM = pl.BlockSpec(memory_space=pl.ANY)


def rope_angles(n_pos):
    inv_freq = 1.0 / jnp.power(ROPE_BASE, jnp.arange(HALF, dtype=F32) * (2.0 / E))
    angles = jnp.arange(n_pos).astype(F32)[:, None] * inv_freq[None, :]
    return jnp.cos(angles), jnp.sin(angles)


def dot_nn(a, b):
    return jnp.dot(a, b, preferred_element_type=F32)


def dot_nt(a, b):
    return lax.dot_general(a, b, (((1,), (1,)), ((), ())), preferred_element_type=F32)


def lanes(parts):
    return jnp.concatenate(parts, axis=1)


def stack(parts):
    return jnp.concatenate(parts, axis=0)


def rows(p):
    return slice(PIECE * p, PIECE * (p + 1))


def heads(e):
    return slice(E * e, E * (e + 1))


def spec(block, index=None, once=False):
    rank = len(block)

    def full(*a):
        i = tuple(index(*a)) if index else ()
        return i + (0,) * (rank - len(i))

    mode = {"pipeline_mode": pl.Buffered(1)} if once or not index else {}
    return pl.BlockSpec(block, full, **mode)


def struct(dtype, *shape):
    return jax.ShapeDtypeStruct(shape, dtype)


def call(body, grid, scal, ins, in_specs, outs, out_specs, flops, scratch=(), aliases=None):
    nbytes = sum(x.size * x.dtype.itemsize for x in jax.tree.leaves([ins, outs]))
    return pl.pallas_call(
        body,
        grid_spec=pltpu.PrefetchScalarGridSpec(
            num_scalar_prefetch=1, grid=grid, in_specs=in_specs, out_specs=out_specs, scratch_shapes=scratch
        ),
        out_shape=outs,
        input_output_aliases=aliases or {},
        cost_estimate=pl.CostEstimate(flops=int(flops), bytes_accessed=int(nbytes), transcendentals=0),
        compiler_params=pltpu.CompilerParams(vmem_limit_bytes=VMEM_LIMIT),
    )(scal, *ins)


def seq_of(l, s):
    return 2 * jnp.where(l == 0, s[0], 3 - s[0]) + s[1]


def proj_body(kind, n_w, n_kv, steps, nl, s_ref, x_ref, r_ref, *refs):
    queries = kind == "q"
    if queries:
        cos_ref, sin_ref, *refs = refs
    w_refs, kv_refs, refs = refs[:n_w], refs[n_w : n_w + n_kv], refs[n_w + n_kv :]
    *outs, a_buf, w_buf, kv_buf, a_sem, w_sem, kv_sem = refs
    l, n = pl.program_id(0), pl.program_id(1)
    c = s_ref[1]
    per = n_w // steps if n_w > 1 else 1
    size = GROUP // per

    def row_copies(i):
        parts = (x_ref, seq_of(i, s_ref)), (r_ref, i)
        return [pltpu.make_async_copy(x.at[at], a_buf.at[i, p], a_sem.at[i, p]) for p, (x, at) in enumerate(parts)]

    def weight_copies(j):
        copies = []
        for m in range(per):
            src = w_refs[per * j + m] if n_w > 1 else w_refs[0].at[pl.ds(GROUP * jnp.bitwise_xor(j, c), GROUP)]
            copies.append(pltpu.make_async_copy(src, w_buf.at[pl.ds(GROUP * j + size * m, size)], w_sem.at[j, m]))
        return copies

    def kv_copies():
        return [pltpu.make_async_copy(r, kv_buf.at[i], kv_sem.at[i]) for i, r in enumerate(kv_refs)]

    def at_step(i, j, f, copies):
        @pl.when(jnp.logical_and(l == i, n == j))
        def _():
            for copy in copies():
                getattr(copy, f)()

    def product(ws):
        return dot_nn(stack([a_buf[l, p] for p in range(2)]), lanes(ws))

    def rotated(x, p):
        at = pl.ds(pl.multiple_of(PIECE * jnp.bitwise_xor(p, c), PIECE), PIECE)
        return x * cos_ref[at, :] + pltpu.roll(x, HALF, 1) * sin_ref[at, :]

    everything = lambda: sum(
        [row_copies(0), *map(weight_copies, range(steps)), kv_copies(), *map(row_copies, range(1, nl))], []
    )
    at_step(0, 0, "start", everything)
    for i in range(nl):
        at_step(i, 0, "wait", functools.partial(row_copies, i))
    for j in range(steps):
        at_step(0, j, "wait", functools.partial(weight_copies, j))

    @pl.when(n < steps)
    def _():
        if queries:
            x = product([w_buf[GROUP * n + e] for e in range(GROUP)])
        else:
            w = w_buf[pl.ds(GROUP * n, GROUP)]
            x = dot_nt(stack([a_buf[l, p] for p in range(2)]), w.reshape(WIDE, w.shape[2]))
        for p in range(2):
            for e in range(GROUP):
                part = x[rows(p), heads(e)]
                outs[-1][p, e] = (rotated(part, p) * SCALE if queries else part).astype(BF16)

    if n_kv:
        at_step(0, steps, "wait", kv_copies)

        @pl.when(n == steps)
        def _():
            x = product([kv_buf[i] for i in range(n_kv)])
            for p in range(2):
                outs[0][p] = rotated(x[rows(p), :E], p).astype(BF16)
                outs[1][p] = x[rows(p), E:].astype(BF16)


def proj(scal, kind, x, x_recv, weights, tables=(), kv=(), nl=2):
    d = x.shape[-1]
    steps = 2 if len(weights) == 1 else len(weights) // 2
    shape = (d, E) if kind == "q" else (E, d)
    dma = pltpu.SemaphoreType.DMA
    last = steps - 1
    return call(
        functools.partial(proj_body, kind, len(weights), len(kv), steps, nl),
        (nl, steps + len(kv) // 2),
        scal,
        [x, x_recv, *tables, *weights, *kv],
        [HBM] * 2 + [spec((ROWS, E))] * len(tables) + [HBM] * (len(weights) + len(kv)),
        [struct(BF16, nl, 2, PIECE, E)] * len(kv) + [struct(BF16, nl, 2, steps * GROUP, PIECE, E)],
        [spec((None, 2, PIECE, E), lambda l, n, s: (l,))] * len(kv)
        + [spec((None, 2, GROUP, PIECE, E), lambda l, n, s: (l, 0, jnp.minimum(n, last)))],
        2 * nl * ROWS * d * steps * WIDE,
        scratch=[
            pltpu.VMEM((nl, 2, PIECE, d), BF16),
            pltpu.VMEM((steps * GROUP, *shape), BF16),
            pltpu.VMEM((len(kv) or 1, d if kv else GROUP, E), BF16),
            dma((nl, 2)),
            dma((steps, 2)),
            dma((2,)),
        ],
    )


TRIO = 3


def over_keys(f, x):
    return f(x, axis=0, keepdims=True)


PART = 32


def weave(*lists):
    order = sorted((i / len(fs), j, f) for j, fs in enumerate(lists) for i, f in enumerate(fs))
    for _, _, f in order:
        f()


def attn_body(mode, turned, joined, s_ref, *refs):
    it = iter(refs)
    fwd, bwd = mode != "bwd", mode != "fwd"
    q_ref, k_ref, v_ref = next(it), next(it), next(it)
    if bwd:
        do_ref, cos_ref, sin_ref = next(it), next(it), next(it)
    if not fwd:
        ot_ref, lse_ref = next(it), next(it)
    if joined:
        next(it)
    if fwd:
        o_ref = next(it)
    if not bwd:
        ot_ref, lse_ref = next(it), next(it)
    if bwd:
        dq_ref, dk_ref, dv_ref = next(it), next(it), next(it)
    if turned:
        t_ref = next(it)
    keys, vals, keys_t, vals_t, s_bufs, p_buf, ds_buf = it
    slot = [jnp.bitwise_xor(p, s_ref[1]) for p in range(2)]

    @pl.when(pl.program_id(1) == 0)
    def _():
        for p in range(2):
            kb, vb = k_ref[slot[p]], v_ref[slot[p]]
            keys[rows(p), :] = kb
            vals[rows(p), :] = vb
            keys_t[:, rows(p)] = kb.astype(F32).T.astype(BF16)
            vals_t[:, rows(p)] = vb.astype(F32).T.astype(BF16)
        if bwd:
            dk_ref[...] = jnp.zeros_like(dk_ref)
            dv_ref[...] = jnp.zeros_like(dv_ref)

    iota = functools.partial(lax.broadcasted_iota, jnp.int32, (SUB, SUB))
    causal = iota(0) <= iota(1)
    subs = range(N_SUB)
    tiles = [(i, j) for i in subs for j in range(i + 1)]
    tile = lambda j: slice(SUB * j, SUB * (j + 1))
    per = PIECE // SUB
    base = lambda i, j: tile(i * (i + 1) // 2 + j)
    here = lambda i, h: (slot[i // per], h)
    q = [[q_ref[(*here(i, h), tile(i % per))] for i in subs] for h in range(TRIO)]
    d_o = [[do_ref[(*here(i, h), tile(i % per))] for i in subs] for h in range(TRIO)] if bwd else None

    def phases(h):
        top, inv, total, out_t, delta = {}, {}, {}, {}, {}
        s_buf = s_bufs.at[h]

        def score(i, j):
            s = dot_nt(keys[tile(j), :], q[h][i])
            return jnp.where(causal, s, -jnp.inf) if j == i else s

        def add(sums, i, first, x, f):
            sums[i] = x if first else f(sums[i], x)

        def fold(x, f):
            return f(x.reshape(PART // 8, 8, SUB), axis=0)

        def parts(i, j):
            start = base(i, j).start
            return [(slice(PART * r, PART * (r + 1)), slice(start + PART * r, start + PART * (r + 1))) for r in range(SUB // PART)]

        def scores(i, j):
            s = score(i, j)
            for r, at in parts(i, j):
                s_buf[at, :] = s[r]
                add(top, i, j == 0 and r.start == 0, fold(s[r], jnp.max), jnp.maximum)
            if j == i:
                top[i] = over_keys(jnp.max, top[i])

        def weights(i, j):
            for r, at in parts(i, j):
                p = jnp.exp(s_buf[at, :] - top[i])
                if bwd:
                    s_buf[at, :] = p
                add(total, i, j == 0 and r.start == 0, fold(p, jnp.sum), jnp.add)
                p_buf[h, SUB * j + r.start : SUB * j + r.stop, tile(i)] = p.astype(BF16)
            if j == i:
                width = SUB * (i + 1)
                total[i] = over_keys(jnp.sum, total[i])
                inv[i] = 1.0 / total[i]
                o_t = dot_nn(vals_t[:, :width], p_buf[h, :width, tile(i)]) * inv[i]
                out_t[i] = o_t.astype(BF16)
                o_ref[(*here(i, h), tile(i % per))] = o_t.T.astype(BF16)
                if turned:
                    t_ref[(*here(i, h), 0, ALL, tile(i % per))] = out_t[i]
                if not bwd:
                    ot_ref[(*here(i, h), ALL, tile(i % per))] = out_t[i]
                    lse_ref[h, :, tile(i)] = top[i] + jnp.log(total[i])

        def score_grads(i, j):
            if j == 0:
                o_t = out_t[i] if fwd else ot_ref[(*here(i, h), ALL, tile(i % per))]
                delta[i] = over_keys(jnp.sum, o_t.astype(F32) * d_o[h][i].astype(F32).T)
            s = None if fwd else score(i, j)
            dp = dot_nt(vals[tile(j), :], d_o[h][i])
            for r, at in parts(i, j):
                p = s_buf[at, :] * inv[i] if fwd else jnp.exp(s[r] - lse_ref[h, :, tile(i)])
                to = slice(SUB * j + r.start, SUB * j + r.stop)
                p_buf[h, to, tile(i)] = p.astype(BF16)
                ds_buf[h, to, tile(i)] = (p * (dp[r] - delta[i])).astype(BF16)

        def query_grads(i):
            width = SUB * (i + 1)
            dq = dot_nn(keys_t[:, :width], ds_buf[h, :width, tile(i)]) * SCALE
            low, high, cos, sin = dq[:HALF], dq[HALF:], cos_ref[:, tile(i)], sin_ref[:, tile(i)]
            dq = stack([low * cos + high * sin, high * cos - low * sin])
            dq_ref[(*here(i, h), tile(i % per))] = dq.T.astype(BF16)
            if turned:
                t_ref[(*here(i, h), 1, ALL, tile(i % per))] = dq.astype(BF16)

        def key_grads(j):
            dv_ref[tile(j), :] += dot_nn(p_buf[h, tile(j), SUB * j :], stack(d_o[h][j:]))
            dk_ref[tile(j), :] += dot_nn(ds_buf[h, tile(j), SUB * j :], stack(q[h][j:]))

        each = lambda f, some: [functools.partial(f, *x) for x in some]
        lists = [each(scores, tiles), each(weights, tiles)] if fwd else []
        if bwd:
            alone = [(i,) for i in subs]
            lists += [each(score_grads, tiles), each(query_grads, alone) + each(key_grads, alone)]
        return lists

    work = [phases(h) for h in range(TRIO)]
    n_phases = len(work[0])
    for stage in range(TRIO + n_phases - 1):
        weave(*(work[h][stage - h] for h in range(TRIO) if 0 <= stage - h < n_phases))


def attention(scal, mode, q, k, v, d_o=None, tables=(), saved=(), l0=0, nl=2, turned=None, prior=()):
    n_heads = q.shape[2]
    fwd, bwd = mode != "bwd", mode != "fwd"
    at_in, at_out = lambda l, h, s: (l + l0, 0, h), lambda l, h, s: (l, 0, h)
    block = (None, 2, TRIO, PIECE, E)
    act_in, act = spec(block, at_in), spec(block, at_out)
    flat = spec((None, 2, TRIO, E, PIECE), at_out)
    kv_spec = spec((None, 2, PIECE, E), lambda l, h, s: (l + l0,))
    stat = spec((None, TRIO, 1, ROWS), lambda l, h, s: (l, h))
    acc = spec((None, ROWS, E), lambda l, h, s: (l,))
    ins, specs, outs, out_specs = [q, k, v], [act_in, kv_spec, kv_spec], [], []
    act_shape = struct(BF16, nl, 2, n_heads, PIECE, E)
    if bwd:
        ins += [d_o, *tables]
        specs += [act_in] + [spec((HALF, ROWS))] * 2
    if not fwd:
        ins += saved
        specs += [flat, stat]
    if fwd:
        outs.append(act_shape)
        out_specs.append(act)
    if not bwd:
        outs += [struct(BF16, nl, 2, n_heads, E, PIECE), struct(F32, nl, n_heads, 1, ROWS)]
        out_specs += [flat, stat]
    if bwd:
        outs += [act_shape] + [struct(F32, nl, ROWS, E)] * 2
        out_specs += [act, acc, acc]
    if turned is not None:
        per = GROUP // TRIO
        shift = 0 if turned == OWN else per
        outs.append(struct(BF16, nl, 2, n_heads * (2 if shift else 1), 2, E, PIECE))
        place_head = lambda l, h, s: (l, 0, h + (per * (h // per + turned) if shift else 0))
        out_specs.append(spec((None, 2, TRIO, 2, E, PIECE), place_head))
    aliases = {1 + len(ins): len(outs) - 1} if prior else {}
    ins += prior
    specs += [HBM] * len(prior)
    products = 2 * fwd + 4 * bwd + (not fwd)
    square = TRIO, ROWS, ROWS
    return call(
        functools.partial(attn_body, mode, turned is not None, len(prior)),
        (nl, n_heads // TRIO),
        scal,
        ins,
        specs,
        outs,
        out_specs,
        nl * n_heads * products * 4 * E * SUB * SUB * N_TILE,
        scratch=[pltpu.VMEM((ROWS, E), BF16)] * 2
        + [pltpu.VMEM((E, ROWS), BF16)] * 2
        + [pltpu.VMEM((TRIO, N_TILE * SUB if fwd else SUB, SUB), F32)]
        + [pltpu.VMEM(square, BF16)] * 2,
        aliases=aliases,
    )


def in_flight(n, steps, chunks, buf, sem):
    slots = buf.shape[0]
    per = slots // 2

    def load(i):
        return pltpu.make_async_copy(chunks[i][0], buf.at[i % slots], sem.at[0, i % slots])

    def save(i):
        return pltpu.make_async_copy(buf.at[i % slots], chunks[i][1], sem.at[1, i % slots])

    for m in range(steps):

        @pl.when(n == m)
        def _():
            for i in range(max(per * (m - 1), 0), min(per * m, len(chunks))):
                load(i).wait()
                save(i).start()
            for i in range(per * m, min(per * (m + 1), len(chunks))):
                if i >= slots:
                    save(i - slots).wait()
                load(i).start()

    def finish():
        @pl.when(n == steps - 1)
        def _():
            for i in range(max(len(chunks) - slots, 0), len(chunks)):
                save(i).wait()

    return finish


def seq_near(s, flip, other):
    return 2 * jnp.bitwise_xor(s[0], flip) + jnp.bitwise_xor(s[1], other)


def combine_body(kind, n_act, n_w, near, fresh, steps, s_ref, *refs):
    acts, ws, refs = refs[:n_act], refs[n_act : n_act + n_w], refs[n_act + n_w :]
    c, n = s_ref[1], pl.program_id(0)
    if kind == "dh":
        kv_refs, refs = refs[:2], refs[2:]
    if not fresh:
        refs = refs[1:]
    finish = []
    if near:
        pieces, theirs, refs = refs[2 : 2 + len(near)], refs[2 + len(near)], refs[len(near) + 3 :]
        *refs, rows_out, grad_out, row_buf, grad_buf, row_sem, grad_sem = refs
        row_chunks = [
            (r.at[cut], rows_out.at[seq_near(s_ref, *at), cut])
            for r, at in zip(pieces, near, strict=True)
            for cut in (pl.ds(SUB * i, SUB) for i in range(PIECE // SUB))
        ]
        grad_chunks = [(theirs.at[i], grad_out.at[GROUP * (1 - c) + i]) for i in range(GROUP)]
        finish.append(in_flight(n, steps, row_chunks, row_buf, row_sem))
        finish.append(in_flight(n, steps, grad_chunks, grad_buf, grad_sem))
    a = lanes([stack([r[0, h], r[1, h]]) for r in acts for h in range(r.shape[1])])
    held = [ws[0][pl.ds(GROUP * i, GROUP)] for i in (c, 1 - c)] + [w[...] for w in ws[1:]]
    if kind == "out":
        x = dot_nn(a, stack([w.reshape(w.shape[0] * E, w.shape[2]) for w in held]))
    else:
        x = dot_nt(a, lanes([w[h] for w in held for h in range(w.shape[0])] + [r[...] for r in kv_refs]))
    x = x.astype(BF16)
    refs[0][...] = x[rows(0)]
    refs[1][...] = x[rows(1)]
    if fresh:
        refs[2][...] = x[rows(0)]
    for f in finish:
        f()


def combine(scal, kind, l, acts, ls, weights, kv=(), big=None, side=None):
    d = weights[0].shape[2 if kind == "out" else 1]
    steps = d // COLS
    in_specs = [
        spec((None, 2, a.shape[2], PIECE, E), lambda n, s, i=i: (i,), once=True) for a, i in zip(acts, ls, strict=True)
    ]
    if kind == "out":
        in_specs += [spec((w.shape[0], E, COLS), lambda n, s: (0, 0, n)) for w in weights]
    else:
        in_specs += [spec((w.shape[0], COLS, E), lambda n, s: (0, n)) for w in weights]
        in_specs += [spec((COLS, E), lambda n, s: (n,))] * 2
    piece = spec((PIECE, COLS), lambda n, s: (0, n))
    fresh = big is None
    ins, aliases, scratch, near = [*acts, *weights, *kv], {}, [], ()
    outs = [struct(BF16, 8, PIECE, d)] + [struct(BF16, PIECE, d)] * (1 + fresh)
    out_specs = [spec((None, PIECE, COLS), lambda n, s: (seq_of(l, s), 0, n))] + [piece] * (1 + fresh)
    moved = [] if fresh else [big]
    if side:
        whole, pieces, near, grad, theirs = side
        moved += [whole, grad, *pieces, theirs]
        outs += [struct(x.dtype, *x.shape) for x in (whole, grad)]
        out_specs += [HBM] * 2
        dma = pltpu.SemaphoreType.DMA
        scratch = [
            pltpu.VMEM((4, SUB, d), BF16),
            pltpu.VMEM((2, *theirs.shape[1:]), F32),
            dma((2, 4)),
            dma((2, 2)),
        ]
    for i, o in zip(range(3 if side else len(moved)), (0, 2, 3), strict=False):
        aliases[1 + len(ins) + i] = o
    return call(
        functools.partial(combine_body, kind, len(acts), len(weights), near, fresh, steps),
        (steps,),
        scal,
        ins + moved,
        in_specs + [HBM] * len(moved),
        outs,
        out_specs,
        2 * ROWS * sum(a.shape[2] for a in acts) * E * d,
        scratch=scratch,
        aliases=aliases,
    )


def dw_local_body(s_ref, t_ref, *refs):
    xs, o_ref = refs[:4], refs[4]
    a = lanes([stack([t_ref[l, p, h] for h in range(t_ref.shape[2])]) for l in range(2) for p in range(2)])
    o_ref[...] = dot_nn(a, stack([x[...] for x in xs])).reshape(o_ref.shape)


def dw_local(scal, which, turned, x, x_recv):
    d = x.shape[-1]
    block = (None, PIECE, DW_COLS)
    mine = [spec(block, lambda n, s, l=l: (seq_of(l, s), 0, n)) for l in range(2)]
    recv = [spec(block, lambda n, s, l=l: (l, 0, n)) for l in range(2)]
    n_heads = turned.shape[2]
    return call(
        dw_local_body,
        (d // DW_COLS,),
        scal,
        [turned, x, x_recv, x, x_recv],
        [spec((2, 2, n_heads, None, E, PIECE), lambda n, s: (0, 0, 0, which)), mine[0], recv[0], mine[1], recv[1]],
        struct(F32, n_heads, E, d),
        spec((n_heads, E, DW_COLS), lambda n, s: (0, 0, n)),
        4 * n_heads * E * ROWS * d,
    )


def dw_rest_body(last, s_ref, *refs):
    ts, xs, refs = refs[:8], refs[8:12], refs[12:]
    a = lanes([stack([t[h] for t in ts[2 * g : 2 * g + 2] for h in range(UNIT)]) for g in range(4)])
    acc = dot_nn(a, stack([x[...] for x in xs])).reshape(GROUP, E, DW_COLS) + refs[0][...]
    if last:
        acc = acc + refs[1][...]
    for o in refs[-2:] if last else refs[-1:]:
        o[...] = acc


NEAR = ((1, 0), (2, 0), (1, 1), (2, 1))


def near_specs(half, which):
    specs = []
    for _, other in NEAR:
        i = half ^ other
        specs += [spec((UNIT, None, E, PIECE), lambda n, s, j=j: (j, which)) for j in (i, 2 + i)]
    rows_at = [spec((None, PIECE, DW_COLS), lambda n, s, at=at: (seq_near(s, *at), 0, n)) for at in NEAR]
    return specs, rows_at


def dw_rest(scal, half, turned, x, local, recv=None):
    d = x.shape[-1]
    block, at_n = (GROUP, E, DW_COLS), lambda n, s: (0, 0, n)
    specs, rows_at = near_specs(half, 0)
    specs += rows_at + [spec(block, lambda n, s: (half, 0, n))]
    ins = [*(t for t in turned for _ in range(2)), x, x, x, x, local]
    outs, out_specs = [struct(F32, GROUP, E, d)], [spec(block, at_n)]
    last = recv is not None
    if last:
        ins.append(recv)
        specs.append(spec(block, at_n))
        outs.insert(0, struct(F32, 2 * GROUP, E, d))
        out_specs.insert(0, spec(block, lambda n, s: (s[1], 0, n)))
    return call(
        functools.partial(dw_rest_body, last),
        (d // DW_COLS,),
        scal,
        ins,
        specs,
        outs,
        out_specs,
        4 * GROUP * E * ROWS * d,
    )


def dw_in_body(last, s_ref, t_ref, u0_ref, u1_ref, *refs):
    ts, kvs, xs, refs = refs[:8], refs[8:12], refs[12:20], refs[20:]
    groups = [
        stack([t_ref[l, p, h] for h in range(GROUP)] + [u[p]]) for l, u in enumerate((u0_ref, u1_ref)) for p in range(2)
    ]
    groups += [
        stack([t[h] for t in ts[2 * g : 2 * g + 2] for h in range(UNIT)] + [kvs[g][...]]) for g in range(len(kvs))
    ]
    acc = dot_nn(lanes(groups), stack([x[...] for x in xs])).reshape(GROUP + 1, E, DW_COLS)
    if not last:
        refs[0][...] = acc
        return
    acc = acc + refs[0][...]
    for h in range(GROUP):
        refs[1][h] = refs[2][h] = acc[h].T
    refs[3][...] = acc[GROUP].T


def dw_in(scal, half, turned_0, kv_0, kv_1, turned, kv, x, x_recv, recv=None):
    d = x.shape[-1]
    kv_half = lambda s: jnp.bitwise_xor(half, s[1])
    near, rows_at = near_specs(half, 1)
    local = [spec((2, 2, GROUP, None, E, PIECE), lambda n, s: (0, 0, half, 1))]
    local += [spec((2, None, E, PIECE), lambda n, s: (0, kv_half(s)))] * 2
    block = (None, PIECE, DW_COLS)
    for l in range(2):
        rows_at.insert(2 * l, spec(block, lambda n, s, l=l: (seq_of(l, s), 0, n)))
        rows_at.insert(2 * l + 1, spec(block, lambda n, s, l=l: (l, 0, n)))
    near += [spec((None, E, PIECE), lambda n, s: (kv_half(s),))] * len(kv)
    ins = [turned_0, kv_0, kv_1, *(t for t in turned for _ in range(2)), *kv, x, x_recv, x, x_recv, x, x, x, x]
    specs = local + near + rows_at
    part = spec((GROUP + 1, E, DW_COLS), lambda n, s: (0, 0, n))
    outs, out_specs = [struct(F32, GROUP + 1, E, d)], [part]
    last = recv is not None
    if last:
        ins.append(recv)
        specs.append(part)
        block = (GROUP, DW_COLS, E)
        outs = [struct(F32, 2 * GROUP, d, E), struct(F32, GROUP, d, E), struct(F32, d, E)]
        out_specs = [spec(block, lambda n, s: (s[1], n)), spec(block, lambda n, s: (0, n))]
        out_specs.append(spec((DW_COLS, E), lambda n, s: (n,)))
    return call(
        functools.partial(dw_in_body, last),
        (d // DW_COLS,),
        scal,
        ins,
        specs,
        outs,
        out_specs,
        8 * (GROUP + 1) * E * ROWS * d,
    )


def copy_body(s_ref, x_ref, o_ref):
    o_ref[...] = x_ref[...]


def pick(indices, x, block):
    count, rest = indices.shape[0], x.shape[1:]
    return call(
        copy_body,
        (count,),
        indices,
        [x],
        [spec((block, *rest), lambda i, s: (s[i],))],
        struct(x.dtype, count * block, *rest),
        spec((block, *rest), lambda i, s: (i,)),
        x.size,
    )


def place_body(n, s_ref, *refs):
    for j in range(n):

        @pl.when(pl.program_id(0) == j)
        def _():
            refs[-1][...] = refs[j][...]


def place(seqs, big, pieces):
    n, d = len(pieces), big.shape[-1]
    return call(
        functools.partial(place_body, n),
        (n,),
        seqs,
        [*pieces, big],
        [spec((PIECE, d))] * n + [HBM],
        struct(big.dtype, *big.shape),
        spec((None, PIECE, d), lambda i, s: (s[i],)),
        n * PIECE * d,
        aliases={1 + n: 0},
    )


def after(x, *deps):
    return lax.optimization_barrier((x, *deps))[0]


def solution(mesh):
    n_tp, n_cp = mesh.shape["tp"], mesh.shape["cp"]
    chips = range(n_tp)

    def on_chip(x):
        return lax.ppermute(x, "cp", [(c, n_cp - 1 - c) for c in range(n_cp)])

    def to_chip(x, flip):
        return lax.ppermute(x, "tp", [(i, i ^ flip) for i in chips])

    def to_chip_other(x, flip):
        pairs = [(i * n_cp + c, (i ^ flip) * n_cp + (1 - c)) for i in chips for c in range(n_cp)]
        return lax.ppermute(x, ("tp", "cp"), pairs)

    def to_both(f, x):
        return [f(x, 1), f(x, 2)]

    def spread(m, r):
        return to_both(to_chip, m) + to_both(to_chip_other, r)

    def swap_heads(x):
        return [
            f(x[0, p, 2 * GROUP * i : 2 * GROUP * (i + 1)], 1 + i)
            for p, f in enumerate((to_chip, to_chip_other))
            for i in range(2)
        ]

    def with_partner(ws):
        return [x for w in ws for x in (w, on_chip(w))]

    def relay(w_in, u, dep):
        ws = [after(w_in[a, u], dep) for a in (1, 2)]
        return with_partner(ws), to_chip(ws[u], 2 - u)

    def local_program(hidden, grad, w_query, w_key, w_value, w_out):
        t, c = lax.axis_index("tp"), lax.axis_index("cp")
        chain = [jnp.stack([t, c]).astype(jnp.int32)]

        def step(f, *args, **kw):
            out = f(chain[0], *args, **kw)
            chain[0] = after(chain[0], jax.tree.leaves(out)[0])
            return out

        cos, sin = rope_angles(ROWS)
        tables = lanes([cos, cos]), lanes([-sin, sin])
        tables_t = cos.T, sin.T
        wq, wo = w_query.transpose(1, 0, 2), w_out
        kv_w = (w_key, w_value)
        own, ext, nx, ny = 2 * t, 2 * (3 - t), 2 * (t ^ 1), 2 * (t ^ 2)
        theirs = jnp.stack([own + 1 - c, ext + 1 - c]).astype(jnp.int32)
        unit = lambda u: (2 * c + u).astype(jnp.int32)[None]

        wq_in, wo_in = {}, {}
        sent = pick(unit(0), wq, UNIT)
        for a in (1, 2):
            wq_in[a, 0] = to_chip(sent, a)
        sent = pick(after(theirs, sent), hidden, 1)
        h_recv = on_chip(sent)
        sent = pick(after(unit(0), sent), wo, UNIT)
        for a in (1, 2):
            wo_in[a, 0] = to_chip(sent, a)
        sent = pick(after(theirs, sent), grad, 1)
        g_recv = on_chip(sent)

        k, v, q_0 = step(proj, "q", hidden, h_recv, [wq], tables, kv=kv_w)
        sent_q = pick(after(unit(1), q_0), wq, UNIT)
        sent_o = pick(after(unit(1), sent_q), wo, UNIT)
        for w_in, sent in ((wq_in, sent_q), (wo_in, sent_o)):
            for a in (1, 2):
                w_in[a, 1] = to_chip(sent, a)
        chain[0] = after(chain[0], sent_o)
        (do_0,) = step(proj, "do", grad, g_recv, [wo])
        wq_n0, wq_d0 = relay(wq_in, 0, do_0)
        o_0, dq_0, dk_0, dv_0, t_0 = step(attention, "fused", q_0, k, v, do_0, tables_t, turned=OWN)
        dwo = step(dw_local, 0, t_0, grad, g_recv)

        wo_n0, wo_d0 = relay(wo_in, 0, dwo)
        (q_n0,) = step(proj, "q", hidden, h_recv, wq_n0, tables)
        wq_n1, wq_d1 = relay(wq_in, 1, q_n0)
        (do_n0,) = step(proj, "do", grad, g_recv, wo_n0)
        (q_n1,) = step(proj, "q", hidden, h_recv, wq_n1, tables)
        wo_n1, wo_d1 = relay(wo_in, 1, q_n1)
        o_n0, dq_n0, dk_n0, dv_n0, t_n0 = step(attention, "fused", q_n0, k, v, do_n0, tables_t, turned=0)
        (do_n1,) = step(proj, "do", grad, g_recv, wo_n1)
        wq_d = with_partner([after(w, do_n1) for w in (wq_d0, wq_d1)])
        o_n1, dq_n1, dk_n1, dv_n1, t_n1 = step(attention, "fused", q_n1, k, v, do_n1, tables_t, turned=1, prior=[t_n0])
        t_nb = swap_heads(t_n1)

        (q_d,) = step(proj, "q", hidden, h_recv, wq_d, tables)
        wo_d = with_partner([after(w, q_d) for w in (wo_d0, wo_d1)])
        wo_all = [wo, *wo_n0, *wo_n1, *wo_d]
        wq_all = [wq, *wq_n0, *wq_n1, *wq_d]
        o_d, ot_d, lse_d = step(attention, "fwd", q_d, k, v, nl=1)
        out_big, out_r, out_m = step(combine, "out", 0, [o_0, o_n0, o_n1, o_d], [0] * 4, wo_all)
        out_m = to_both(to_chip, out_m)
        (do_d,) = step(proj, "do", grad, g_recv, wo_d)
        dq_d, dk_d, dv_d = step(attention, "bwd", q_d, k, v, do_d, tables_t, saved=[ot_d, lse_d], nl=1)

        def finish_kv(l, *last):
            dk, dv = [
                x[l] + y[l] + z[l] + w[0]
                for x, y, z, w in zip((dk_0, dv_0), (dk_n0, dv_n0), (dk_n1, dv_n1), last, strict=True)
            ]
            dk = dk * tables[0] - jnp.roll(dk, HALF, axis=1) * tables[1]
            x = jnp.stack([dk, dv]).astype(BF16).reshape(2, 2, PIECE, E).transpose(1, 0, 2, 3)
            x = jnp.where(c == 0, x, x[::-1])
            return x[None], x.transpose(0, 1, 3, 2)

        dkv_0, dkv_t = finish_kv(0, dk_d, dv_d)
        kv_nb = spread(dkv_t[0], dkv_t[1])
        out_r = after(out_r, dkv_t)
        out_r = to_both(to_chip_other, out_r) + [on_chip(out_r)]
        dh_big, dh_r, dh_m = step(combine, "dh", 0, [dq_0, dq_n0, dq_n1, dq_d, dkv_0], [0] * 5, wq_all, kv=kv_w)
        dh_in = spread(dh_m, dh_r) + [on_chip(dh_r)]

        o_e, dq_e, dk_e, dv_e = step(attention, "fused", q_d, k, v, do_d, tables_t, l0=1, nl=1)
        dkv_1, dkv_u = finish_kv(1, dk_e, dv_e)

        (wo_part,) = step(dw_rest, 1, t_nb, grad, dwo)
        wo_part = on_chip(wo_part)
        dw_args = t_0, dkv_t, dkv_u, t_nb, kv_nb, hidden, h_recv
        (wq_part,) = step(dw_in, 1, *dw_args)
        wq_part = on_chip(wq_part)
        dwo_big, dwo_mine = step(dw_rest, 0, t_nb, grad, dwo, wo_part)
        dwo_theirs = on_chip(dwo_mine)
        dwq_big, dwq_mine, dkv_mine = step(dw_in, 0, *dw_args, wq_part)
        dwq_theirs = on_chip(dwq_mine)
        dkv_theirs = on_chip(dkv_mine)

        acts = [dq_0, dq_n0, dq_n1, dq_e, dkv_1]
        side = out_big, out_m + out_r, [*NEAR, (0, 1)], dwo_big, dwo_theirs
        dh_big, dh_er, out_big, d_w_out = step(
            combine, "dh", 1, acts, [1, 1, 1, 0, 0], wq_all, kv=kv_w, big=dh_big, side=side
        )
        dh_er = on_chip(dh_er)
        early = dh_in[:2] + dh_in[4:]
        side = dh_big, early, [*NEAR[:2], (0, 1)], dwq_big, dwq_theirs
        out_big, out_er, dh_big, dwq = step(
            combine, "out", 1, [o_0, o_n0, o_n1, o_e], [1, 1, 1, 0], wo_all, big=out_big, side=side
        )
        out_er = on_chip(out_er)
        late = jnp.stack([nx + 1 - c, ny + 1 - c, ext + 1 - c]).astype(jnp.int32)
        d_hidden = place(after(late, out_er), dh_big, [*dh_in[2:4], dh_er])
        attn_out = place(late[2:], out_big, [out_er])
        d_w_key = jnp.where(c == 0, dkv_mine, dkv_theirs)
        d_w_value = jnp.where(c == 0, dkv_theirs, dkv_mine)
        return attn_out, d_hidden, dwq.transpose(1, 0, 2), d_w_key, d_w_value, d_w_out

    row = P(None, "cp", None)
    wq_spec, wo_spec = P(None, "tp", None), P("tp", None, None)
    return jax.shard_map(
        local_program,
        mesh=mesh,
        in_specs=(row, row, wq_spec, P(), P(), wo_spec),
        out_specs=(row, row, wq_spec, P(), P(), wo_spec),
        check_vma=False,
    )
```

time: 2020 us -> 1820 us (0.901)
  Pallas kernels: 1430 us -> 1340 us
  waiting for transfers between devices: 468 us -> 385 us
  local copies, waits for them, and re-layouts: 45.1 us -> 23.6 us
    ppermute x10 -> x8, waiting for transfers between devices: 373 us -> 240 us  [to_chip_other(): return lax.ppermute(x, ('tp', 'cp'), pairs)]
    pallas_call x35 -> x31, Pallas kernels: 1430 us -> 1340 us  [call(): pl.pallas_call(body, grid_spec=pltpu.PrefetchScalarGridSpec(num_scalar_pr...]
    ppermute x22 -> x20, waiting for transfers between devices: 80.4 us -> 123 us  [to_chip(): return lax.ppermute(x, 'tp', [(i, i ^ flip) for i in chips])]
    dynamic_update_slice x2 -> x0, local copies, waits for them, and re-layouts: 27.4 us -> none  [local_program(): lax.dynamic_update_slice_in_dim(big, x, GROUP * (1 - c), 0)]
  transfers between devices with their start and end apart: 58 -> 51, of which waited for: 16 -> 12; matrix products, arithmetic and copies ran while one was open for 3% -> 3% of each run, Pallas kernels for 69% -> 67%
where the time goes in v2:
time: 1820 us; the launch traced here: 1810 us
  Pallas kernels  1340 us (74%)
  waiting for transfers between devices  385 us (21%)
  starting transfers between devices  35.2 us (2%)
  other arithmetic  29.1 us (2%)
  local copies, waits for them, and re-layouts  23.6 us (1%)
    pallas_call x31, Pallas kernels, call(): pl.pallas_call(body, grid_spec=pltpu.PrefetchScalarGridSpec(num_scalar_pr...  1340 us
    ppermute x8, waiting for transfers between devices, to_chip_other(): return lax.ppermute(x, ('tp', 'cp'), pairs)  240 us
    ppermute x20, waiting for transfers between devices, to_chip(): return lax.ppermute(x, 'tp', [(i, i ^ flip) for i in chips])  123 us
  transfers between devices with their start and end apart: 51, of which 12 were waited for; matrix products, arithmetic and copies ran while one was open for 3% of the time, Pallas kernels for 67%

profile of v2, /device:TPU:0, one launch (start us, length us, event | category | flops | bytes accessed | tf_op | source)
XLA Modules:
  0.0 1814.5 jit_solution(14361328689226252523)
XLA Ops:
  42.4 59.4 %shard_map.111 = (bf16[2,2,512,128]{3,2,1,0:T(8,128)(2,1)}, bf16[2,2,512,128]{3,2,1,0:T(8,128)(2,1)}, bf16[2,2,12,512,128]{4,3,2,1,0:T(8,128)(2,1)}) custom-call(s32[2]{0:T(128)} %pad_add_fusion.s_ref, bf16[8,512,6144]{2,1,0:T(8,128)(2,1)} %refs_19_.6, bf16[2,512,6144]{2,1,0:T(8,128)(2,1)} %collective-permute-done.r_ref.refs_13_.refs_15_, ...), custom_call_target="tpu_custom_call" | custom-call | flops 38654705664 | bytes 93323264 | tf_op jit(solution)/shard_map/pallas_call | solution.py:80
  113.3 49.2 %shard_map.116.refs_3_ = bf16[2,2,12,512,128]{4,3,2,1,0:T(8,128)(2,1)} custom-call(s32[2]{0:T(128)} %pad_add_fusion.s_ref, bf16[8,512,6144]{2,1,0:T(8,128)(2,1)} %refs_11_.3, bf16[2,512,6144]{2,1,0:T(8,128)(2,1)} %collective-permute-done.1.r_ref.refs_1_.refs_3_, bf16[12,128,6144]{2,1,0:T(8,128)(2,1)} %refs_4_.5), custom_call_target="tpu_custom_call" | custom-call | flops 38654705664 | bytes 88080384 | tf_op jit(solution)/shard_map/pallas_call | solution.py:80
  163.0 61.7 %shard_map.117 = (bf16[2,2,12,512,128]{4,3,2,1,0:T(8,128)(2,1)}, bf16[2,2,12,512,128]{4,3,2,1,0:T(8,128)(2,1)}, f32[2,1024,128]{2,1,0:T(8,128)}, f32[2,1024,128]...) custom-call(s32[2]{0:T(128)} %pad_add_fusion.s_ref, bf16[2,2,12,512,128]{4,3,2,1,0:T(8,128)(2,1)} %get-tuple-element.98.refs_0_, ...), custom_call_target="tpu_custom_call" | custom-call | flops 48318382080 | bytes 41418752 | tf_op jit(solution)/shard_map/pallas_call | solution.py:80
  239.6 48.1 %shard_map.118.refs_12_ = f32[12,128,6144]{2,1,0:T(8,128)} custom-call(s32[2]{0:T(128)} %pad_add_fusion.s_ref, bf16[2,2,12,2,128,512]{5,4,3,2,1,0:T(8,128)(2,1)} %get-tuple-element.108.t_ref, bf16[8,512,6144]{2,1,0:T(8,128)(2,1)} %refs_11_.3, bf16[2,512,6144]{2,1,0:T(8,128)(2,1)} %collective-permute-done.1.r_ref.refs_1_.refs_3_, ...), custom_call_target="tpu_custom_call" | custom-call | flops 38654705664 | bytes 176160768 | tf_op jit(solution)/shard_map/pallas_call | solution.py:80
  288.3 51.9 %shard_map.119.refs_0_ = bf16[2,2,12,512,128]{4,3,2,1,0:T(8,128)(2,1)} custom-call(s32[2]{0:T(128)} %pad_add_fusion.s_ref, bf16[8,512,6144]{2,1,0:T(8,128)(2,1)} %refs_19_.6, bf16[2,512,6144]{2,1,0:T(8,128)(2,1)} %collective-permute-done.r_ref.refs_13_.refs_15_, f32[1024,128]{1,0:T(8,128)} %get-tuple-element.207.refs_0_, ...), custom_call_target="tpu_custom_call" | custom-call | flops 38654705664 | bytes 89128960 | tf_op jit(solution)/shard_map/pallas_call | solution.py:80
  343.3 49.5 %shard_map.120.refs_3_ = bf16[2,2,12,512,128]{4,3,2,1,0:T(8,128)(2,1)} custom-call(s32[2]{0:T(128)} %pad_add_fusion.s_ref, bf16[8,512,6144]{2,1,0:T(8,128)(2,1)} %refs_11_.3, bf16[2,512,6144]{2,1,0:T(8,128)(2,1)} %collective-permute-done.1.r_ref.refs_1_.refs_3_, bf16[3,128,6144]{2,1,0:T(8,128)(2,1)} %collective-permute-done.6.refs_0_.refs_5_, ...), custom_call_target="tpu_custom_call" | custom-call | flops 38654705664 | bytes 88080384 | tf_op jit(solution)/shard_map/pallas_call | solution.py:80
  392.9 51.8 %shard_map.121.refs_0_ = bf16[2,2,12,512,128]{4,3,2,1,0:T(8,128)(2,1)} custom-call(s32[2]{0:T(128)} %pad_add_fusion.s_ref, bf16[8,512,6144]{2,1,0:T(8,128)(2,1)} %refs_19_.6, bf16[2,512,6144]{2,1,0:T(8,128)(2,1)} %collective-permute-done.r_ref.refs_13_.refs_15_, f32[1024,128]{1,0:T(8,128)} %get-tuple-element.207.refs_0_, ...), custom_call_target="tpu_custom_call" | custom-call | flops 38654705664 | bytes 89128960 | tf_op jit(solution)/shard_map/pallas_call | solution.py:80
  448.4 61.9 %shard_map.122 = (bf16[2,2,12,512,128]{4,3,2,1,0:T(8,128)(2,1)}, bf16[2,2,12,512,128]{4,3,2,1,0:T(8,128)(2,1)}, f32[2,1024,128]{2,1,0:T(8,128)}, f32[2,1024,128]...) custom-call(s32[2]{0:T(128)} %pad_add_fusion.s_ref, bf16[2,2,12,512,128]{4,3,2,1,0:T(8,128)(2,1)} %shard_map.119.refs_0_, ...), custom_call_target="tpu_custom_call" | custom-call | flops 48318382080 | bytes 54001664 | tf_op jit(solution)/shard_map/pallas_call | solution.py:80
  510.3 49.3 %shard_map.123.refs_3_ = bf16[2,2,12,512,128]{4,3,2,1,0:T(8,128)(2,1)} custom-call(s32[2]{0:T(128)} %pad_add_fusion.s_ref, bf16[8,512,6144]{2,1,0:T(8,128)(2,1)} %refs_11_.3, bf16[2,512,6144]{2,1,0:T(8,128)(2,1)} %collective-permute-done.1.r_ref.refs_1_.refs_3_, bf16[3,128,6144]{2,1,0:T(8,128)(2,1)} %collective-permute-done.14.refs_0_.refs_9_, ...), custom_call_target="tpu_custom_call" | custom-call | flops 38654705664 | bytes 88080384 | tf_op jit(solution)/shard_map/pallas_call | solution.py:80
  562.1 62.3 %shard_map.124 = (bf16[2,2,12,512,128]{4,3,2,1,0:T(8,128)(2,1)}, bf16[2,2,12,512,128]{4,3,2,1,0:T(8,128)(2,1)}, f32[2,1024,128]{2,1,0:T(8,128)}, f32[2,1024,128]...) custom-call(s32[2]{0:T(128)} %pad_add_fusion.s_ref, ...), custom_call_target="tpu_custom_call", output_to_operand_aliasing={{4}: (7, {})} | custom-call | flops 48318382080 | bytes 79167488 | tf_op jit(solution)/shard_map/pallas_call | solution.py:80
  624.4 51.8 %shard_map.125.refs_0_ = bf16[2,2,12,512,128]{4,3,2,1,0:T(8,128)(2,1)} custom-call(s32[2]{0:T(128)} %pad_add_fusion.s_ref, bf16[8,512,6144]{2,1,0:T(8,128)(2,1)} %refs_19_.6, bf16[2,512,6144]{2,1,0:T(8,128)(2,1)} %collective-permute-done.r_ref.refs_13_.refs_15_, f32[1024,128]{1,0:T(8,128)} %get-tuple-element.207.refs_0_, ...), custom_call_target="tpu_custom_call" | custom-call | flops 38654705664 | bytes 89128960 | tf_op jit(solution)/shard_map/pallas_call | solution.py:80
  706.6 89.1 %shard_map.127 = (bf16[8,512,6144]{2,1,0:T(8,128)(2,1)}, bf16[512,6144]{1,0:T(8,128)(2,1)}, bf16[512,6144]{1,0:T(8,128)(2,1)}) custom-call(s32[2]{0:T(128)} %pad_add_fusion.s_ref, bf16[2,2,12,512,128]{4,3,2,1,0:T(8,128)(2,1)} %get-tuple-element.106.refs_0_, bf16[2,2,12,512,128]{4,3,2,1,0:T(8,128)(2,1)} %get-tuple-element.119.refs_1_, ...), custom_call_target="tpu_custom_call" | custom-call | flops 77309411328 | bytes 160432128 | tf_op jit(solution)/shard_map/pallas_call | solution.py:80
  795.7 49.1 %shard_map.128.refs_3_ = bf16[2,2,12,512,128]{4,3,2,1,0:T(8,128)(2,1)} custom-call(s32[2]{0:T(128)} %pad_add_fusion.s_ref, bf16[8,512,6144]{2,1,0:T(8,128)(2,1)} %refs_11_.3, bf16[2,512,6144]{2,1,0:T(8,128)(2,1)} %collective-permute-done.1.r_ref.refs_1_.refs_3_, bf16[3,128,6144]{2,1,0:T(8,128)(2,1)} %collective-permute-done.22.refs_13_.refs_0_, ...), custom_call_target="tpu_custom_call" | custom-call | flops 38654705664 | bytes 88080384 | tf_op jit(solution)/shard_map/pallas_call | solution.py:80
  874.8 93.4 %shard_map.130 = (bf16[8,512,6144]{2,1,0:T(8,128)(2,1)}, bf16[512,6144]{1,0:T(8,128)(2,1)}, bf16[512,6144]{1,0:T(8,128)(2,1)}) custom-call(s32[2]{0:T(128)} %pad_add_fusion.s_ref, bf16[2,2,12,512,128]{4,3,2,1,0:T(8,128)(2,1)} %get-tuple-element.141.refs_0_, bf16[2,2,12,512,128]{4,3,2,1,0:T(8,128)(2,1)} %get-tuple-element.142.refs_1_, ...), custom_call_target="tpu_custom_call" | custom-call | flops 80530636800 | bytes 164102144 | tf_op jit(solution)/shard_map/pallas_call | solution.py:80
  968.1 32.3 %shard_map.131 = (bf16[1,2,12,512,128]{4,3,2,1,0:T(8,128)(2,1)}, bf16[1,2,12,512,128]{4,3,2,1,0:T(8,128)(2,1)}, f32[1,1024,128]{2,1,0:T(8,128)}, f32[1,1024,128]{2,1,0:T(8,128)}) custom-call(s32[2]{0:T(128)} %pad_add_fusion.s_ref, bf16[2,2,12,512,128]{4,3,2,1,0:T(8,128)(2,1)} %shard_map.125.refs_0_, bf16[2,2,512,128]{3,2,1,0:T(8,128)(2,1)} %get-tuple-element.96.refs_1_, ...), custom_call_target="tpu_custom_call" | custom-call | flops 24159191040 | bytes 21495808 | tf_op jit(solution)/shard_map/pallas_call | solution.py:80
  1055.4 56.1 %shard_map.133 = f32[7,128,6144]{2,1,0:T(8,128)} custom-call(s32[2]{0:T(128)} %pad_add_fusion.s_ref, bf16[2,2,12,2,128,512]{5,4,3,2,1,0:T(8,128)(2,1)} %get-tuple-element.108.t_ref, bf16[2,2,128,512]{3,2,1,0:T(8,128)(2,1)} %copy.21.u0_ref, bf16[2,2,128,512]{3,2,1,0:T(8,128)(2,1)} %copy.22.u1_ref, ...), custom_call_target="tpu_custom_call" | custom-call | flops 45097156608 | bytes 389021696 | tf_op jit(solution)/shard_map/pallas_call | solution.py:80
  1111.9 39.8 %shard_map.134 = (f32[12,128,6144]{2,1,0:T(8,128)}, f32[6,128,6144]{2,1,0:T(8,128)}) custom-call(s32[2]{0:T(128)} %pad_add_fusion.s_ref, bf16[12,2,128,512]{3,2,1,0:T(8,128)(2,1)} %collective-permute-done.26.refs_0_.refs_1_, bf16[12,2,128,512]{3,2,1,0:T(8,128)(2,1)} %collective-permute-done.26.refs_0_.refs_1_, ...), custom_call_target="tpu_custom_call" | custom-call | flops 19327352832 | bytes 339738624 | tf_op jit(solution)/shard_map/pallas_call | solution.py:80
  1154.0 59.9 %shard_map.135 = (f32[12,6144,128]{2,1,0:T(8,128)}, f32[6,6144,128]{2,1,0:T(8,128)}, f32[6144,128]{1,0:T(8,128)}) custom-call(s32[2]{0:T(128)} %pad_add_fusion.s_ref, bf16[2,2,12,2,128,512]{5,4,3,2,1,0:T(8,128)(2,1)} %get-tuple-element.108.t_ref, bf16[2,2,128,512]{3,2,1,0:T(8,128)(2,1)} %copy.21.u0_ref, bf16[2,2,128,512]{3,2,1,0:T(8,128)(2,1)} %copy.22.u1_ref, ...), custom_call_target="tpu_custom_call" | custom-call | flops 45097156608 | bytes 448790528 | tf_op jit(solution)/shard_map/pallas_call | solution.py:80
  1215.2 75.2 %collective-permute-done.36.refs_23_ = bf16[512,6144]{1,0:T(8,128)(2,1)} collective-permute-done((bf16[512,6144]{1,0:T(8,128)(2,1)}, bf16[512,6144]{1,0:T(8,128)(2,1)}, u32[]{:S(2)}, u32[]{:S(2)}) %collective-permute-start.36) | collective-permute-done | bytes 6291488 | tf_op jit(solution)/shard_map/ppermute | solution.py:683
  1292.0 132.2 %collective-permute-done.38.refs_25_ = bf16[512,6144]{1,0:T(8,128)(2,1)} collective-permute-done((bf16[512,6144]{1,0:T(8,128)(2,1)}, bf16[512,6144]{1,0:T(8,128)(2,1)}, u32[]{:S(2)}, u32[]{:S(2)}) %collective-permute-start.38) | collective-permute-done | bytes 6291488 | tf_op jit(solution)/shard_map/ppermute | solution.py:687
  1429.3 103.5 %shard_map.136 = (bf16[8,512,6144]{2,1,0:T(8,128)(2,1)}, bf16[512,6144]{1,0:T(8,128)(2,1)}, bf16[8,512,6144]{2,1,0:T(8,128)(2,1)}, f32[12,128,6144]{2,1,0:T(8,128)}) custom-call(s32[2]{0:T(128)} %pad_add_fusion.s_ref, bf16[2,2,12,512,128]{4,3,2,1,0:T(8,128)(2,1)} %get-tuple-element.141.refs_0_, ...), custom_call_target="tpu_custom_call", output_to_operand_aliasing={{0}: (21, {}), {2}: (22, {}), {3}: (23, {})} | custom-call | flops 80530636800 | bytes 434634752 | tf_op jit(solution)/shard_map/pallas_call | solution.py:80
  1532.8 29.8 %collective-permute-done.42.refs_20_ = bf16[512,6144]{1,0:T(8,128)(2,1)} collective-permute-done((bf16[512,6144]{1,0:T(8,128)(2,1)}, bf16[512,6144]{1,0:T(8,128)(2,1)}, u32[]{:S(2)}, u32[]{:S(2)}) %collective-permute-start.42) | collective-permute-done | bytes 6291488 | tf_op jit(solution)/shard_map/ppermute | solution.py:683
  1566.4 94.8 %shard_map.137 = (bf16[8,512,6144]{2,1,0:T(8,128)(2,1)}, bf16[512,6144]{1,0:T(8,128)(2,1)}, bf16[8,512,6144]{2,1,0:T(8,128)(2,1)}, f32[12,6144,128]{2,1,0:T(8,128)}) custom-call(s32[2]{0:T(128)} %pad_add_fusion.s_ref, bf16[2,2,12,512,128]{4,3,2,1,0:T(8,128)(2,1)} %get-tuple-element.106.refs_0_, ...), custom_call_target="tpu_custom_call", output_to_operand_aliasing={{0}: (18, {}), {2}: (19, {}), {3}: (20, {})} | custom-call | flops 77309411328 | bytes 418381824 | tf_op jit(solution)/shard_map/pallas_call | solution.py:80
  1696.1 102.7 %collective-permute-done.47.refs_0_ = bf16[512,6144]{1,0:T(8,128)(2,1)} collective-permute-done((bf16[512,6144]{1,0:T(8,128)(2,1)}, bf16[512,6144]{1,0:T(8,128)(2,1)}, u32[]{:S(2)}, u32[]{:S(2)}) %collective-permute-start.47) | collective-permute-done | bytes 6291488 | tf_op jit(solution)/shard_map/ppermute | solution.py:687
  (157 shorter events, 258.4 us)
Async XLA Ops:
  30.5 131.9 %collective-permute-start.2 = (bf16[3,6144,128]{2,1,0:T(8,128)(2,1)}, bf16[3,6144,128]{2,1,0:T(8,128)(2,1)}, u32[]{:S(2)}, u32[]{:S(2)}) collective-permute-start(bf16[3,6144,128]{2,1,0:T(8,128)(2,1)} %shard_map.109), channel_id=1, source_target_pairs={{0,2},{2,0},{4,6},{6,4},{1,3},{3,1},{5,7},{7,5}} | collective-permute-start | bytes 14155784 | tf_op jit(solution)/shard_map/ppermute | solution.py:683
  33.5 129.0 %collective-permute-start.4 = (bf16[3,6144,128]{2,1,0:T(8,128)(2,1)}, bf16[3,6144,128]{2,1,0:T(8,128)(2,1)}, u32[]{:S(2)}, u32[]{:S(2)}) collective-permute-start(bf16[3,6144,128]{2,1,0:T(8,128)(2,1)} %shard_map.109), channel_id=1, source_target_pairs={{0,4},{2,6},{4,0},{6,2},{1,5},{3,7},{5,1},{7,3}} | collective-permute-start | bytes 14155784 | tf_op jit(solution)/shard_map/ppermute | solution.py:683
  35.0 202.6 %collective-permute-start.6 = (bf16[3,128,6144]{2,1,0:T(8,128)(2,1)}, bf16[3,128,6144]{2,1,0:T(8,128)(2,1)}, u32[]{:S(2)}, u32[]{:S(2)}) collective-permute-start(bf16[3,128,6144]{2,1,0:T(8,128)(2,1)} %shard_map.114), channel_id=1, source_target_pairs={{0,2},{2,0},{4,6},{6,4},{1,3},{3,1},{5,7},{7,5}} | collective-permute-start | bytes 14155784 | tf_op jit(solution)/shard_map/ppermute | solution.py:683
  42.4 245.4 %collective-permute-start.8 = (bf16[3,128,6144]{2,1,0:T(8,128)(2,1)}, bf16[3,128,6144]{2,1,0:T(8,128)(2,1)}, u32[]{:S(2)}, u32[]{:S(2)}) collective-permute-start(bf16[3,128,6144]{2,1,0:T(8,128)(2,1)} %shard_map.114), channel_id=1, source_target_pairs={{0,4},{2,6},{4,0},{6,2},{1,5},{3,7},{5,1},{7,3}} | collective-permute-start | bytes 14155784 | tf_op jit(solution)/shard_map/ppermute | solution.py:683
  111.3 228.9 %collective-permute-start.10 = (bf16[3,6144,128]{2,1,0:T(8,128)(2,1)}, bf16[3,6144,128]{2,1,0:T(8,128)(2,1)}, u32[]{:S(2)}, u32[]{:S(2)}) collective-permute-start(bf16[3,6144,128]{2,1,0:T(8,128)(2,1)} %shard_map.112), channel_id=1, source_target_pairs={{0,2},{2,0},{4,6},{6,4},{1,3},{3,1},{5,7},{7,5}} | collective-permute-start | bytes 14155784 | tf_op jit(solution)/shard_map/ppermute | solution.py:683
  162.4 125.3 %collective-permute-start.3 = (bf16[3,6144,128]{2,1,0:T(8,128)(2,1)}, bf16[3,6144,128]{2,1,0:T(8,128)(2,1)}, u32[]{:S(2)}, u32[]{:S(2)}) collective-permute-start(bf16[3,6144,128]{2,1,0:T(8,128)(2,1)} %collective-permute-done.2.refs_2_.refs_6_), channel_id=1, source_target_pairs={{0,1},{1,0},{2,3},{3,2},{4,5},{5,4},{6,7},{7,6}} | collective-permute-start | bytes 14155784 | tf_op jit(solution)/shard_map/ppermute | solution.py:680
  162.5 125.8 %collective-permute-start.5 = (bf16[3,6144,128]{2,1,0:T(8,128)(2,1)}, bf16[3,6144,128]{2,1,0:T(8,128)(2,1)}, u32[]{:S(2)}, u32[]{:S(2)}) collective-permute-start(bf16[3,6144,128]{2,1,0:T(8,128)(2,1)} %collective-permute-done.4.refs_4_.refs_8_), channel_id=1, source_target_pairs={{0,1},{1,0},{2,3},{3,2},{4,5},{5,4},{6,7},{7,6}} | collective-permute-start | bytes 14155784 | tf_op jit(solution)/shard_map/ppermute | solution.py:680
  689.1 321.6 %collective-permute-start.26 = (bf16[12,2,128,512]{3,2,1,0:T(8,128)(2,1)}, bf16[12,2,128,512]{3,2,1,0:T(8,128)(2,1)}, u32[]{:S(2)}, u32[]{:S(2)}) collective-permute-start(bf16[12,2,128,512]{3,2,1,0:T(8,128)(2,1)} %get-tuple-element.187), channel_id=1, source_target_pairs={{0,2},{2,0},{4,6},{6,4},{1,3},{3,1},{5,7},{7,5}} | collective-permute-start | bytes 9437192 | tf_op jit(solution)/shard_map/ppermute | solution.py:683
  690.0 322.1 %collective-permute-start.27 = (bf16[12,2,128,512]{3,2,1,0:T(8,128)(2,1)}, bf16[12,2,128,512]{3,2,1,0:T(8,128)(2,1)}, u32[]{:S(2)}, u32[]{:S(2)}) collective-permute-start(bf16[12,2,128,512]{3,2,1,0:T(8,128)(2,1)} %get-tuple-element.186), channel_id=1, source_target_pairs={{0,4},{2,6},{4,0},{6,2},{1,5},{3,7},{5,1},{7,3}} | collective-permute-start | bytes 9437192 | tf_op jit(solution)/shard_map/ppermute | solution.py:683
  691.3 320.8 %collective-permute-start.28 = (bf16[12,2,128,512]{3,2,1,0:T(8,128)(2,1)}, bf16[12,2,128,512]{3,2,1,0:T(8,128)(2,1)}, u32[]{:S(2)}, u32[]{:S(2)}) collective-permute-start(bf16[12,2,128,512]{3,2,1,0:T(8,128)(2,1)} %get-tuple-element.185), channel_id=1, source_target_pairs={{0,3},{1,2},{2,1},{3,0},{4,7},{5,6},{6,5},{7,4}} | collective-permute-start | bytes 9437192 | tf_op jit(solution)/shard_map/ppermute | solution.py:687
  705.4 308.3 %collective-permute-start.29 = (bf16[12,2,128,512]{3,2,1,0:T(8,128)(2,1)}, bf16[12,2,128,512]{3,2,1,0:T(8,128)(2,1)}, u32[]{:S(2)}, u32[]{:S(2)}) collective-permute-start(bf16[12,2,128,512]{3,2,1,0:T(8,128)(2,1)} %get-tuple-element.184), channel_id=1, source_target_pairs={{0,5},{1,4},{2,7},{3,6},{4,1},{5,0},{6,3},{7,2}} | collective-permute-start | bytes 9437192 | tf_op jit(solution)/shard_map/ppermute | solution.py:687
  1151.7 277.6 %collective-permute-start.41 = (f32[6,128,6144]{2,1,0:T(8,128)}, f32[6,128,6144]{2,1,0:T(8,128)}, u32[]{:S(2)}, u32[]{:S(2)}) collective-permute-start(f32[6,128,6144]{2,1,0:T(8,128)} %get-tuple-element.169), channel_id=1, source_target_pairs={{0,1},{1,0},{2,3},{3,2},{4,5},{5,4},{6,7},{7,6}} | collective-permute-start | bytes 56623112 | tf_op jit(solution)/shard_map/ppermute | solution.py:680
  1151.8 138.7 %collective-permute-start.36 = (bf16[512,6144]{1,0:T(8,128)(2,1)}, bf16[512,6144]{1,0:T(8,128)(2,1)}, u32[]{:S(2)}, u32[]{:S(2)}) collective-permute-start(bf16[512,6144]{1,0:T(8,128)(2,1)} %get-tuple-element.166), channel_id=1, source_target_pairs={{0,2},{2,0},{4,6},{6,4},{1,3},{3,1},{5,7},{7,5}} | collective-permute-start | bytes 18874376 | tf_op jit(solution)/shard_map/ppermute | solution.py:683
  1152.6 137.9 %collective-permute-start.37 = (bf16[512,6144]{1,0:T(8,128)(2,1)}, bf16[512,6144]{1,0:T(8,128)(2,1)}, u32[]{:S(2)}, u32[]{:S(2)}) collective-permute-start(bf16[512,6144]{1,0:T(8,128)(2,1)} %get-tuple-element.166), channel_id=1, source_target_pairs={{0,4},{2,6},{4,0},{6,2},{1,5},{3,7},{5,1},{7,3}} | collective-permute-start | bytes 18874376 | tf_op jit(solution)/shard_map/ppermute | solution.py:683
  1213.9 352.5 %collective-permute-start.45 = (f32[6,6144,128]{2,1,0:T(8,128)}, f32[6,6144,128]{2,1,0:T(8,128)}, u32[]{:S(2)}, u32[]{:S(2)}) collective-permute-start(f32[6,6144,128]{2,1,0:T(8,128)} %get-tuple-element.175), channel_id=1, source_target_pairs={{0,1},{1,0},{2,3},{3,2},{4,5},{5,4},{6,7},{7,6}} | collective-permute-start | bytes 56623112 | tf_op jit(solution)/shard_map/ppermute | solution.py:680
  1213.9 210.3 %collective-permute-start.38 = (bf16[512,6144]{1,0:T(8,128)(2,1)}, bf16[512,6144]{1,0:T(8,128)(2,1)}, u32[]{:S(2)}, u32[]{:S(2)}) collective-permute-start(bf16[512,6144]{1,0:T(8,128)(2,1)} %get-tuple-element.168), channel_id=1, source_target_pairs={{0,3},{1,2},{2,1},{3,0},{4,7},{5,6},{6,5},{7,4}} | collective-permute-start | bytes 18874376 | tf_op jit(solution)/shard_map/ppermute | solution.py:687
  1290.5 138.1 %collective-permute-start.39 = (bf16[512,6144]{1,0:T(8,128)(2,1)}, bf16[512,6144]{1,0:T(8,128)(2,1)}, u32[]{:S(2)}, u32[]{:S(2)}) collective-permute-start(bf16[512,6144]{1,0:T(8,128)(2,1)} %get-tuple-element.168), channel_id=1, source_target_pairs={{0,5},{1,4},{2,7},{3,6},{4,1},{5,0},{6,3},{7,2}} | collective-permute-start | bytes 18874376 | tf_op jit(solution)/shard_map/ppermute | solution.py:687
  1290.5 138.7 %collective-permute-start.40 = (bf16[512,6144]{1,0:T(8,128)(2,1)}, bf16[512,6144]{1,0:T(8,128)(2,1)}, u32[]{:S(2)}, u32[]{:S(2)}) collective-permute-start(bf16[512,6144]{1,0:T(8,128)(2,1)} %get-tuple-element.168), channel_id=1, source_target_pairs={{0,1},{1,0},{2,3},{3,2},{4,5},{5,4},{6,7},{7,6}} | collective-permute-start | bytes 18874376 | tf_op jit(solution)/shard_map/ppermute | solution.py:680
  1424.2 138.4 %collective-permute-start.42 = (bf16[512,6144]{1,0:T(8,128)(2,1)}, bf16[512,6144]{1,0:T(8,128)(2,1)}, u32[]{:S(2)}, u32[]{:S(2)}) collective-permute-start(bf16[512,6144]{1,0:T(8,128)(2,1)} %get-tuple-element.173), channel_id=1, source_target_pairs={{0,2},{2,0},{4,6},{6,4},{1,3},{3,1},{5,7},{7,5}} | collective-permute-start | bytes 18874376 | tf_op jit(solution)/shard_map/ppermute | solution.py:683
  1428.6 137.8 %collective-permute-start.43 = (bf16[512,6144]{1,0:T(8,128)(2,1)}, bf16[512,6144]{1,0:T(8,128)(2,1)}, u32[]{:S(2)}, u32[]{:S(2)}) collective-permute-start(bf16[512,6144]{1,0:T(8,128)(2,1)} %get-tuple-element.173), channel_id=1, source_target_pairs={{0,4},{2,6},{4,0},{6,2},{1,5},{3,7},{5,1},{7,3}} | collective-permute-start | bytes 18874376 | tf_op jit(solution)/shard_map/ppermute | solution.py:683
  1429.2 137.2 %collective-permute-start.44 = (bf16[512,6144]{1,0:T(8,128)(2,1)}, bf16[512,6144]{1,0:T(8,128)(2,1)}, u32[]{:S(2)}, u32[]{:S(2)}) collective-permute-start(bf16[512,6144]{1,0:T(8,128)(2,1)} %get-tuple-element.174), channel_id=1, source_target_pairs={{0,1},{1,0},{2,3},{3,2},{4,5},{5,4},{6,7},{7,6}} | collective-permute-start | bytes 18874376 | tf_op jit(solution)/shard_map/ppermute | solution.py:680
  1661.3 137.5 %collective-permute-start.47 = (bf16[512,6144]{1,0:T(8,128)(2,1)}, bf16[512,6144]{1,0:T(8,128)(2,1)}, u32[]{:S(2)}, u32[]{:S(2)}) collective-permute-start(bf16[512,6144]{1,0:T(8,128)(2,1)} %get-tuple-element.174), channel_id=1, source_target_pairs={{0,3},{1,2},{2,1},{3,0},{4,7},{5,6},{6,5},{7,4}} | collective-permute-start | bytes 18874376 | tf_op jit(solution)/shard_map/ppermute | solution.py:687
  1662.1 137.9 %collective-permute-start.48 = (bf16[512,6144]{1,0:T(8,128)(2,1)}, bf16[512,6144]{1,0:T(8,128)(2,1)}, u32[]{:S(2)}, u32[]{:S(2)}) collective-permute-start(bf16[512,6144]{1,0:T(8,128)(2,1)} %get-tuple-element.174), channel_id=1, source_target_pairs={{0,5},{1,4},{2,7},{3,6},{4,1},{5,0},{6,3},{7,2}} | collective-permute-start | bytes 18874376 | tf_op jit(solution)/shard_map/ppermute | solution.py:687
  1662.1 137.9 %collective-permute-start.49 = (bf16[512,6144]{1,0:T(8,128)(2,1)}, bf16[512,6144]{1,0:T(8,128)(2,1)}, u32[]{:S(2)}, u32[]{:S(2)}) collective-permute-start(bf16[512,6144]{1,0:T(8,128)(2,1)} %get-tuple-element.179), channel_id=1, source_target_pairs={{0,1},{1,0},{2,3},{3,2},{4,5},{5,4},{6,7},{7,6}} | collective-permute-start | bytes 18874376 | tf_op jit(solution)/shard_map/ppermute | solution.py:680
  (36 other events, 1784.9 us)

commit v3 on v2

--- a/solution.py
+++ b/solution.py
@@ -2,6 +2,7 @@
 
 import jax
 import jax.numpy as jnp
+import numpy as np
 from jax import lax
 from jax.experimental import pallas as pl
 from jax.experimental.pallas import tpu as pltpu
@@ -30,10 +31,10 @@
 HBM = pl.BlockSpec(memory_space=pl.ANY)
 
 
-def rope_angles(n_pos):
-    inv_freq = 1.0 / jnp.power(ROPE_BASE, jnp.arange(HALF, dtype=F32) * (2.0 / E))
-    angles = jnp.arange(n_pos).astype(F32)[:, None] * inv_freq[None, :]
-    return jnp.cos(angles), jnp.sin(angles)
+def rope_tables(n_pos):
+    inv_freq = 1.0 / np.power(np.float32(ROPE_BASE), np.arange(HALF, dtype=np.float32) * np.float32(2.0 / E))
+    angles = np.arange(n_pos, dtype=np.float32)[:, None] * inv_freq.astype(np.float32)[None, :]
+    return np.cos(angles), np.sin(angles)
 
 
 def dot_nn(a, b):
@@ -93,14 +94,43 @@
     return 2 * jnp.where(l == 0, s[0], 3 - s[0]) + s[1]
 
 
-def proj_body(kind, n_w, n_kv, steps, nl, s_ref, x_ref, r_ref, *refs):
+def in_flight(n, steps, chunks, buf, sem, first=0):
+    def load(i):
+        return pltpu.make_async_copy(chunks[i][0], buf.at[i % 2], sem.at[0, i % 2])
+
+    def save(i):
+        return pltpu.make_async_copy(buf.at[i % 2], chunks[i][1], sem.at[1, i % 2])
+
+    def at(i, *work):
+        @pl.when(n == i)
+        def _():
+            for f, copy in work:
+                getattr(copy, f)()
+
+    count = len(chunks)
+    for i in range(count):
+        done = [("wait", save(i - 2))] if i > 1 else []
+        at(first + i, *done, ("start", load(i)))
+        at(first + i + 1, ("wait", load(i)), ("start", save(i)))
+    return lambda: at(steps - 1, *(("wait", save(i)) for i in range(max(count - 2, 0), count)))
+
+
+def proj_body(kind, n_w, n_kv, steps, nl, moves, s_ref, x_ref, r_ref, *refs):
     queries = kind == "q"
     if queries:
         cos_ref, sin_ref, *refs = refs
     w_refs, kv_refs, refs = refs[:n_w], refs[n_w : n_w + n_kv], refs[n_w + n_kv :]
-    *outs, a_buf, w_buf, kv_buf, a_sem, w_sem, kv_sem = refs
     l, n = pl.program_id(0), pl.program_id(1)
     c = s_ref[1]
+    finish = []
+    if moves:
+        side, out, *moved, a_buf, w_buf, kv_buf, a_sem, w_sem, kv_sem, buf_0, sem_0, buf_1, sem_1 = refs
+        outs = [out]
+        for src, dst, buf, sem in zip((w_refs[0], side), moved, (buf_0, buf_1), (sem_0, sem_1), strict=True):
+            chunks = [(src.at[UNIT * (2 * c + 1) + i], dst.at[i]) for i in range(UNIT)]
+            finish.append(in_flight(steps * l + n, nl * steps, chunks, buf, sem))
+    else:
+        *outs, a_buf, w_buf, kv_buf, a_sem, w_sem, kv_sem = refs
     per = n_w // steps if n_w > 1 else 1
     size = GROUP // per
 
@@ -131,13 +161,14 @@
         at = pl.ds(pl.multiple_of(PIECE * jnp.bitwise_xor(p, c), PIECE), PIECE)
         return x * cos_ref[at, :] + pltpu.roll(x, HALF, 1) * sin_ref[at, :]
 
-    everything = lambda: sum(
-        [row_copies(0), *map(weight_copies, range(steps)), kv_copies(), *map(row_copies, range(1, nl))], []
-    )
-    at_step(0, 0, "start", everything)
-    for i in range(nl):
+    now = lambda: row_copies(0) + weight_copies(0)
+    later = lambda: sum([*map(weight_copies, range(1, steps)), kv_copies(), *map(row_copies, range(1, nl))], [])
+    at_step(0, 0, "start", now)
+    at_step(0, 0, "wait", now)
+    at_step(0, 0, "start", later)
+    for i in range(1, nl):
         at_step(i, 0, "wait", functools.partial(row_copies, i))
-    for j in range(steps):
+    for j in range(1, steps):
         at_step(0, j, "wait", functools.partial(weight_copies, j))
 
     @pl.when(n < steps)
@@ -150,7 +181,7 @@
         for p in range(2):
             for e in range(GROUP):
                 part = x[rows(p), heads(e)]
-                outs[-1][p, e] = (rotated(part, p) * SCALE if queries else part).astype(BF16)
+                outs[0][p, e] = (rotated(part, p) * SCALE if queries else part).astype(BF16)
 
     if n_kv:
         at_step(0, steps, "wait", kv_copies)
@@ -159,25 +190,32 @@
         def _():
             x = product([kv_buf[i] for i in range(n_kv)])
             for p in range(2):
-                outs[0][p] = rotated(x[rows(p), :E], p).astype(BF16)
-                outs[1][p] = x[rows(p), E:].astype(BF16)
-
-
-def proj(scal, kind, x, x_recv, weights, tables=(), kv=(), nl=2):
+                outs[1][p] = rotated(x[rows(p), :E], p).astype(BF16)
+                outs[2][p] = x[rows(p), E:].astype(BF16)
+
+    for f in finish:
+        f()
+
+
+def proj(scal, kind, x, x_recv, weights, tables=(), kv=(), nl=2, side=()):
     d = x.shape[-1]
     steps = 2 if len(weights) == 1 else len(weights) // 2
     shape = (d, E) if kind == "q" else (E, d)
     dma = pltpu.SemaphoreType.DMA
     last = steps - 1
+    moved = [*weights, *side] if side else []
     return call(
-        functools.partial(proj_body, kind, len(weights), len(kv), steps, nl),
+        functools.partial(proj_body, kind, len(weights), len(kv), steps, nl, len(side)),
         (nl, steps + len(kv) // 2),
         scal,
-        [x, x_recv, *tables, *weights, *kv],
-        [HBM] * 2 + [spec((ROWS, E))] * len(tables) + [HBM] * (len(weights) + len(kv)),
-        [struct(BF16, nl, 2, PIECE, E)] * len(kv) + [struct(BF16, nl, 2, steps * GROUP, PIECE, E)],
-        [spec((None, 2, PIECE, E), lambda l, n, s: (l,))] * len(kv)
-        + [spec((None, 2, GROUP, PIECE, E), lambda l, n, s: (l, 0, jnp.minimum(n, last)))],
+        [x, x_recv, *tables, *weights, *kv, *side],
+        [HBM] * 2 + [spec((ROWS, E))] * len(tables) + [HBM] * (len(weights) + len(kv) + len(side)),
+        [struct(BF16, nl, 2, steps * GROUP, PIECE, E)]
+        + [struct(BF16, nl, 2, PIECE, E)] * len(kv)
+        + [struct(BF16, UNIT, *w.shape[1:]) for w in moved],
+        [spec((None, 2, GROUP, PIECE, E), lambda l, n, s: (l, 0, jnp.minimum(n, last)))]
+        + [spec((None, 2, PIECE, E), lambda l, n, s: (l,))] * len(kv)
+        + [HBM] * len(moved),
         2 * nl * ROWS * d * steps * WIDE,
         scratch=[
             pltpu.VMEM((nl, 2, PIECE, d), BF16),
@@ -186,6 +224,7 @@
             dma((nl, 2)),
             dma((steps, 2)),
             dma((2,)),
+            *(x for w in moved for x in (pltpu.VMEM((2, *w.shape[1:]), BF16), dma((2, 2)))),
         ],
     )
 
@@ -389,37 +428,6 @@
     )
 
 
-def in_flight(n, steps, chunks, buf, sem):
-    slots = buf.shape[0]
-    per = slots // 2
-
-    def load(i):
-        return pltpu.make_async_copy(chunks[i][0], buf.at[i % slots], sem.at[0, i % slots])
-
-    def save(i):
-        return pltpu.make_async_copy(buf.at[i % slots], chunks[i][1], sem.at[1, i % slots])
-
-    for m in range(steps):
-
-        @pl.when(n == m)
-        def _():
-            for i in range(max(per * (m - 1), 0), min(per * m, len(chunks))):
-                load(i).wait()
-                save(i).start()
-            for i in range(per * m, min(per * (m + 1), len(chunks))):
-                if i >= slots:
-                    save(i - slots).wait()
-                load(i).start()
-
-    def finish():
-        @pl.when(n == steps - 1)
-        def _():
-            for i in range(max(len(chunks) - slots, 0), len(chunks)):
-                save(i).wait()
-
-    return finish
-
-
 def seq_near(s, flip, other):
     return 2 * jnp.bitwise_xor(s[0], flip) + jnp.bitwise_xor(s[1], other)
 
@@ -442,7 +450,7 @@
         ]
         grad_chunks = [(theirs.at[i], grad_out.at[GROUP * (1 - c) + i]) for i in range(GROUP)]
         finish.append(in_flight(n, steps, row_chunks, row_buf, row_sem))
-        finish.append(in_flight(n, steps, grad_chunks, grad_buf, grad_sem))
+        finish.append(in_flight(n, steps, grad_chunks, grad_buf, grad_sem, first=steps - GROUP - 1))
     a = lanes([stack([r[0, h], r[1, h]]) for r in acts for h in range(r.shape[1])])
     held = [ws[0][pl.ds(GROUP * i, GROUP)] for i in (c, 1 - c)] + [w[...] for w in ws[1:]]
     if kind == "out":
@@ -458,11 +466,11 @@
         f()
 
 
-def combine(scal, kind, l, acts, ls, weights, kv=(), big=None, side=None):
+def combine(scal, kind, l, acts, weights, kv=(), big=None, side=None):
     d = weights[0].shape[2 if kind == "out" else 1]
     steps = d // COLS
     in_specs = [
-        spec((None, 2, a.shape[2], PIECE, E), lambda n, s, i=i: (i,), once=True) for a, i in zip(acts, ls, strict=True)
+        spec((None, 2, a.shape[2], PIECE, E), lambda n, s, i=min(l, a.shape[0] - 1): (i,), once=True) for a in acts
     ]
     if kind == "out":
         in_specs += [spec((w.shape[0], E, COLS), lambda n, s: (0, 0, n)) for w in weights]
@@ -482,9 +490,9 @@
         out_specs += [HBM] * 2
         dma = pltpu.SemaphoreType.DMA
         scratch = [
-            pltpu.VMEM((4, SUB, d), BF16),
+            pltpu.VMEM((2, SUB, d), BF16),
             pltpu.VMEM((2, *theirs.shape[1:]), F32),
-            dma((2, 4)),
+            dma((2, 2)),
             dma((2, 2)),
         ]
     for i, o in zip(range(3 if side else len(moved)), (0, 2, 3), strict=False):
@@ -537,7 +545,7 @@
         o[...] = acc
 
 
-NEAR = ((1, 0), (2, 0), (1, 1), (2, 1))
+NEAR = tuple((flip, other) for other in range(2) for flip in (1, 2))
 
 
 def near_specs(half, which):
@@ -715,35 +723,31 @@
             chain[0] = after(chain[0], jax.tree.leaves(out)[0])
             return out
 
-        cos, sin = rope_angles(ROWS)
-        tables = lanes([cos, cos]), lanes([-sin, sin])
-        tables_t = cos.T, sin.T
+        cos, sin = rope_tables(ROWS)
+        tables = [jnp.asarray(np.concatenate(x, axis=1)) for x in ((cos, cos), (-sin, sin))]
+        tables_t = [jnp.asarray(np.ascontiguousarray(x.T)) for x in (cos, sin)]
         wq, wo = w_query.transpose(1, 0, 2), w_out
         kv_w = (w_key, w_value)
         own, ext, nx, ny = 2 * t, 2 * (3 - t), 2 * (t ^ 1), 2 * (t ^ 2)
         theirs = jnp.stack([own + 1 - c, ext + 1 - c]).astype(jnp.int32)
-        unit = lambda u: (2 * c + u).astype(jnp.int32)[None]
+        unit = (2 * c).astype(jnp.int32)[None]
 
         wq_in, wo_in = {}, {}
-        sent = pick(unit(0), wq, UNIT)
+        sent = pick(theirs, hidden, 1)
+        h_recv = on_chip(sent)
+        sent = pick(after(unit, sent), wq, UNIT)
         for a in (1, 2):
             wq_in[a, 0] = to_chip(sent, a)
-        sent = pick(after(theirs, sent), hidden, 1)
-        h_recv = on_chip(sent)
-        sent = pick(after(unit(0), sent), wo, UNIT)
+        sent = pick(after(unit, sent), wo, UNIT)
         for a in (1, 2):
             wo_in[a, 0] = to_chip(sent, a)
-        sent = pick(after(theirs, sent), grad, 1)
-        g_recv = on_chip(sent)
-
-        k, v, q_0 = step(proj, "q", hidden, h_recv, [wq], tables, kv=kv_w)
-        sent_q = pick(after(unit(1), q_0), wq, UNIT)
-        sent_o = pick(after(unit(1), sent_q), wo, UNIT)
-        for w_in, sent in ((wq_in, sent_q), (wo_in, sent_o)):
-            for a in (1, 2):
-                w_in[a, 1] = to_chip(sent, a)
-        chain[0] = after(chain[0], sent_o)
-        (do_0,) = step(proj, "do", grad, g_recv, [wo])
+        g_recv = on_chip(pick(after(theirs, sent), grad, 1))
+
+        q_0, k, v = step(proj, "q", hidden, h_recv, [wq], tables, kv=kv_w)
+        do_0, wo_sent, wq_sent = step(proj, "do", grad, g_recv, [wo], side=[wq])
+        for a in (1, 2):
+            wq_in[a, 1] = to_chip(wq_sent, a)
+            wo_in[a, 1] = to_chip(wo_sent, a)
         wq_n0, wq_d0 = relay(wq_in, 0, do_0)
         o_0, dq_0, dk_0, dv_0, t_0 = step(attention, "fused", q_0, k, v, do_0, tables_t, turned=OWN)
         dwo = step(dw_local, 0, t_0, grad, g_recv)
@@ -765,7 +769,7 @@
         wo_all = [wo, *wo_n0, *wo_n1, *wo_d]
         wq_all = [wq, *wq_n0, *wq_n1, *wq_d]
         o_d, ot_d, lse_d = step(attention, "fwd", q_d, k, v, nl=1)
-        out_big, out_r, out_m = step(combine, "out", 0, [o_0, o_n0, o_n1, o_d], [0] * 4, wo_all)
+        out_big, out_r, out_m = step(combine, "out", 0, [o_0, o_n0, o_n1, o_d], wo_all)
         out_m = to_both(to_chip, out_m)
         (do_d,) = step(proj, "do", grad, g_recv, wo_d)
         dq_d, dk_d, dv_d = step(attention, "bwd", q_d, k, v, do_d, tables_t, saved=[ot_d, lse_d], nl=1)
@@ -784,7 +788,7 @@
         kv_nb = spread(dkv_t[0], dkv_t[1])
         out_r = after(out_r, dkv_t)
         out_r = to_both(to_chip_other, out_r) + [on_chip(out_r)]
-        dh_big, dh_r, dh_m = step(combine, "dh", 0, [dq_0, dq_n0, dq_n1, dq_d, dkv_0], [0] * 5, wq_all, kv=kv_w)
+        dh_big, dh_r, dh_m = step(combine, "dh", 0, [dq_0, dq_n0, dq_n1, dq_d, dkv_0], wq_all, kv=kv_w)
         dh_in = spread(dh_m, dh_r) + [on_chip(dh_r)]
 
         o_e, dq_e, dk_e, dv_e = step(attention, "fused", q_d, k, v, do_d, tables_t, l0=1, nl=1)
@@ -803,19 +807,15 @@
 
         acts = [dq_0, dq_n0, dq_n1, dq_e, dkv_1]
         side = out_big, out_m + out_r, [*NEAR, (0, 1)], dwo_big, dwo_theirs
-        dh_big, dh_er, out_big, d_w_out = step(
-            combine, "dh", 1, acts, [1, 1, 1, 0, 0], wq_all, kv=kv_w, big=dh_big, side=side
-        )
+        dh_big, dh_er, out_big, d_w_out = step(combine, "dh", 1, acts, wq_all, kv=kv_w, big=dh_big, side=side)
         dh_er = on_chip(dh_er)
         early = dh_in[:2] + dh_in[4:]
         side = dh_big, early, [*NEAR[:2], (0, 1)], dwq_big, dwq_theirs
-        out_big, out_er, dh_big, dwq = step(
-            combine, "out", 1, [o_0, o_n0, o_n1, o_e], [1, 1, 1, 0], wo_all, big=out_big, side=side
-        )
+        out_big, out_er, dh_big, dwq = step(combine, "out", 1, [o_0, o_n0, o_n1, o_e], wo_all, big=out_big, side=side)
         out_er = on_chip(out_er)
         late = jnp.stack([nx + 1 - c, ny + 1 - c, ext + 1 - c]).astype(jnp.int32)
-        d_hidden = place(after(late, out_er), dh_big, [*dh_in[2:4], dh_er])
-        attn_out = place(late[2:], out_big, [out_er])
+        d_hidden = place(after(late, out_big), dh_big, [*dh_in[2:4], dh_er])
+        attn_out = place(after(late[2:], d_hidden), out_big, [out_er])
         d_w_key = jnp.where(c == 0, dkv_mine, dkv_theirs)
         d_w_value = jnp.where(c == 0, dkv_theirs, dkv_mine)
         return attn_out, d_hidden, dwq.transpose(1, 0, 2), d_w_key, d_w_value, d_w_out

time: 1820 us -> 1730 us (0.951)
  waiting for transfers between devices: 385 us -> 319 us
  Pallas kernels: 1340 us -> 1320 us
    ppermute x8, waiting for transfers between devices: 240 us -> 160 us  [to_chip_other(): return lax.ppermute(x, ('tp', 'cp'), pairs)]
    pallas_call x31 -> x29, Pallas kernels: 1340 us -> 1320 us  [call(): pl.pallas_call(body, grid_spec=pltpu.PrefetchScalarGridSpec(num_scalar_pr...]
    ppermute x20, waiting for transfers between devices: 123 us -> 145 us  [to_chip(): return lax.ppermute(x, 'tp', [(i, i ^ flip) for i in chips])]
  transfers between devices with their start and end apart: 51 -> 51, of which waited for: 12 -> 12; matrix products, arithmetic and copies ran while one was open for 3% -> 2% of each run, Pallas kernels for 67% -> 76%
where the time goes in v3:
time: 1730 us; the launch traced here: 1720 us
  Pallas kernels  1320 us (76%)
  waiting for transfers between devices  319 us (18%)
  starting transfers between devices  37.1 us (2%)
  local copies, waits for them, and re-layouts  23.5 us (1%)
  other arithmetic  18.5 us (1%)
    pallas_call x29, Pallas kernels, call(): pl.pallas_call(body, grid_spec=pltpu.PrefetchScalarGridSpec(num_scalar_pr...  1320 us
    ppermute x8, waiting for transfers between devices, to_chip_other(): return lax.ppermute(x, ('tp', 'cp'), pairs)  160 us
    ppermute x20, waiting for transfers between devices, to_chip(): return lax.ppermute(x, 'tp', [(i, i ^ flip) for i in chips])  145 us
  transfers between devices with their start and end apart: 51, of which 12 were waited for; matrix products, arithmetic and copies ran while one was open for 2% of the time, Pallas kernels for 76%

profile of v3, /device:TPU:0, one launch (start us, length us, event | category | flops | bytes accessed | tf_op | source)
XLA Modules:
  0.0 1716.8 jit_solution(2673938143030664513)
XLA Ops:
  36.1 58.9 %shard_map.146 = (bf16[2,2,12,512,128]{4,3,2,1,0:T(8,128)(2,1)}, bf16[2,2,512,128]{3,2,1,0:T(8,128)(2,1)}, bf16[2,2,512,128]{3,2,1,0:T(8,128)(2,1)}) custom-call(s32[2]{0:T(128)} %pad_add_fusion.1.s_ref, bf16[8,512,6144]{2,1,0:T(8,128)(2,1)} %refs_19_.6, bf16[2,512,6144]{2,1,0:T(8,128)(2,1)} %collective-permute-done.r_ref.refs_13_.refs_15_, ...), custom_call_target="tpu_custom_call" | custom-call | flops 38654705664 | bytes 93323264 | tf_op jit(solution)/shard_map/pallas_call | solution.py:81
  95.0 50.6 %shard_map.150 = (bf16[2,2,12,512,128]{4,3,2,1,0:T(8,128)(2,1)}, bf16[3,128,6144]{2,1,0:T(8,128)(2,1)}, bf16[3,6144,128]{2,1,0:T(8,128)(2,1)}) custom-call(s32[2]{0:T(128)} %pad_add_fusion.1.s_ref, bf16[8,512,6144]{2,1,0:T(8,128)(2,1)} %refs_11_.3, bf16[2,512,6144]{2,1,0:T(8,128)(2,1)} %collective-permute-done.1.r_ref.refs_1_.refs_3_, ...), custom_call_target="tpu_custom_call" | custom-call | flops 38654705664 | bytes 116391936 | tf_op jit(solution)/shard_map/pallas_call | solution.py:81
  146.1 61.6 %shard_map.151 = (bf16[2,2,12,512,128]{4,3,2,1,0:T(8,128)(2,1)}, bf16[2,2,12,512,128]{4,3,2,1,0:T(8,128)(2,1)}, f32[2,1024,128]{2,1,0:T(8,128)}, f32[2,1024,128]...) custom-call(s32[2]{0:T(128)} %pad_add_fusion.1.s_ref, bf16[2,2,12,512,128]{4,3,2,1,0:T(8,128)(2,1)} %get-tuple-element.96.refs_0_, ...), custom_call_target="tpu_custom_call" | custom-call | flops 48318382080 | bytes 41418752 | tf_op jit(solution)/shard_map/pallas_call | solution.py:81
  239.6 48.3 %shard_map.152.refs_12_ = f32[12,128,6144]{2,1,0:T(8,128)} custom-call(s32[2]{0:T(128)} %pad_add_fusion.1.s_ref, bf16[2,2,12,2,128,512]{5,4,3,2,1,0:T(8,128)(2,1)} %get-tuple-element.107.t_ref, bf16[8,512,6144]{2,1,0:T(8,128)(2,1)} %refs_11_.3, bf16[2,512,6144]{2,1,0:T(8,128)(2,1)} %collective-permute-done.1.r_ref.refs_1_.refs_3_, ...), custom_call_target="tpu_custom_call" | custom-call | flops 38654705664 | bytes 176160768 | tf_op jit(solution)/shard_map/pallas_call | solution.py:81
  288.4 51.7 %shard_map.153.refs_0_ = bf16[2,2,12,512,128]{4,3,2,1,0:T(8,128)(2,1)} custom-call(s32[2]{0:T(128)} %pad_add_fusion.1.s_ref, bf16[8,512,6144]{2,1,0:T(8,128)(2,1)} %refs_19_.6, bf16[2,512,6144]{2,1,0:T(8,128)(2,1)} %collective-permute-done.r_ref.refs_13_.refs_15_, f32[1024,128]{1,0:T(8,128)} %constant.24.clone.refs_0_, f32[1024,128]{1,0:T(8,128)} %constant.25.clone.refs_1_, ...), custom_call_target="tpu_custom_call" | custom-call | flops 38654705664 | bytes 89128960 | tf_op jit(solution)/shard_map/pallas_call | solution.py:81
  343.3 49.3 %shard_map.154.refs_3_ = bf16[2,2,12,512,128]{4,3,2,1,0:T(8,128)(2,1)} custom-call(s32[2]{0:T(128)} %pad_add_fusion.1.s_ref, bf16[8,512,6144]{2,1,0:T(8,128)(2,1)} %refs_11_.3, bf16[2,512,6144]{2,1,0:T(8,128)(2,1)} %collective-permute-done.1.r_ref.refs_1_.refs_3_, bf16[3,128,6144]{2,1,0:T(8,128)(2,1)} %collective-permute-done.6.refs_0_.refs_5_, ...), custom_call_target="tpu_custom_call" | custom-call | flops 38654705664 | bytes 88080384 | tf_op jit(solution)/shard_map/pallas_call | solution.py:81
  392.6 52.1 %shard_map.155.refs_0_ = bf16[2,2,12,512,128]{4,3,2,1,0:T(8,128)(2,1)} custom-call(s32[2]{0:T(128)} %pad_add_fusion.1.s_ref, bf16[8,512,6144]{2,1,0:T(8,128)(2,1)} %refs_19_.6, bf16[2,512,6144]{2,1,0:T(8,128)(2,1)} %collective-permute-done.r_ref.refs_13_.refs_15_, f32[1024,128]{1,0:T(8,128)} %constant.24.clone.refs_0_, f32[1024,128]{1,0:T(8,128)} %constant.25.clone.refs_1_, ...), custom_call_target="tpu_custom_call" | custom-call | flops 38654705664 | bytes 89128960 | tf_op jit(solution)/shard_map/pallas_call | solution.py:81
  448.3 61.9 %shard_map.156 = (bf16[2,2,12,512,128]{4,3,2,1,0:T(8,128)(2,1)}, bf16[2,2,12,512,128]{4,3,2,1,0:T(8,128)(2,1)}, f32[2,1024,128]{2,1,0:T(8,128)}, f32[2,1024,128]...) custom-call(s32[2]{0:T(128)} %pad_add_fusion.1.s_ref, bf16[2,2,12,512,128]{4,3,2,1,0:T(8,128)(2,1)} %shard_map.153.refs_0_, ...), custom_call_target="tpu_custom_call" | custom-call | flops 48318382080 | bytes 54001664 | tf_op jit(solution)/shard_map/pallas_call | solution.py:81
  510.2 49.3 %shard_map.157.refs_3_ = bf16[2,2,12,512,128]{4,3,2,1,0:T(8,128)(2,1)} custom-call(s32[2]{0:T(128)} %pad_add_fusion.1.s_ref, bf16[8,512,6144]{2,1,0:T(8,128)(2,1)} %refs_11_.3, bf16[2,512,6144]{2,1,0:T(8,128)(2,1)} %collective-permute-done.1.r_ref.refs_1_.refs_3_, bf16[3,128,6144]{2,1,0:T(8,128)(2,1)} %collective-permute-done.14.refs_0_.refs_9_, ...), custom_call_target="tpu_custom_call" | custom-call | flops 38654705664 | bytes 88080384 | tf_op jit(solution)/shard_map/pallas_call | solution.py:81
  561.8 62.1 %shard_map.158 = (bf16[2,2,12,512,128]{4,3,2,1,0:T(8,128)(2,1)}, bf16[2,2,12,512,128]{4,3,2,1,0:T(8,128)(2,1)}, f32[2,1024,128]{2,1,0:T(8,128)}, f32[2,1024,128]...) custom-call(s32[2]{0:T(128)} %pad_add_fusion.1.s_ref, ...), custom_call_target="tpu_custom_call", output_to_operand_aliasing={{4}: (7, {})} | custom-call | flops 48318382080 | bytes 79167488 | tf_op jit(solution)/shard_map/pallas_call | solution.py:81
  623.9 52.1 %shard_map.159.refs_0_ = bf16[2,2,12,512,128]{4,3,2,1,0:T(8,128)(2,1)} custom-call(s32[2]{0:T(128)} %pad_add_fusion.1.s_ref, bf16[8,512,6144]{2,1,0:T(8,128)(2,1)} %refs_19_.6, bf16[2,512,6144]{2,1,0:T(8,128)(2,1)} %collective-permute-done.r_ref.refs_13_.refs_15_, f32[1024,128]{1,0:T(8,128)} %constant.24.clone.refs_0_, f32[1024,128]{1,0:T(8,128)} %constant.25.clone.refs_1_, ...), custom_call_target="tpu_custom_call" | custom-call | flops 38654705664 | bytes 89128960 | tf_op jit(solution)/shard_map/pallas_call | solution.py:81
  703.2 89.0 %shard_map.161 = (bf16[8,512,6144]{2,1,0:T(8,128)(2,1)}, bf16[512,6144]{1,0:T(8,128)(2,1)}, bf16[512,6144]{1,0:T(8,128)(2,1)}) custom-call(s32[2]{0:T(128)} %pad_add_fusion.1.s_ref, bf16[2,2,12,512,128]{4,3,2,1,0:T(8,128)(2,1)} %get-tuple-element.105.refs_0_, bf16[2,2,12,512,128]{4,3,2,1,0:T(8,128)(2,1)} %get-tuple-element.119.refs_1_, ...), custom_call_target="tpu_custom_call" | custom-call | flops 77309411328 | bytes 160432128 | tf_op jit(solution)/shard_map/pallas_call | solution.py:81
  792.2 49.1 %shard_map.162.refs_3_ = bf16[2,2,12,512,128]{4,3,2,1,0:T(8,128)(2,1)} custom-call(s32[2]{0:T(128)} %pad_add_fusion.1.s_ref, bf16[8,512,6144]{2,1,0:T(8,128)(2,1)} %refs_11_.3, bf16[2,512,6144]{2,1,0:T(8,128)(2,1)} %collective-permute-done.1.r_ref.refs_1_.refs_3_, bf16[3,128,6144]{2,1,0:T(8,128)(2,1)} %collective-permute-done.22.refs_13_.refs_0_, ...), custom_call_target="tpu_custom_call" | custom-call | flops 38654705664 | bytes 88080384 | tf_op jit(solution)/shard_map/pallas_call | solution.py:81
  870.6 93.4 %shard_map.164 = (bf16[8,512,6144]{2,1,0:T(8,128)(2,1)}, bf16[512,6144]{1,0:T(8,128)(2,1)}, bf16[512,6144]{1,0:T(8,128)(2,1)}) custom-call(s32[2]{0:T(128)} %pad_add_fusion.1.s_ref, bf16[2,2,12,512,128]{4,3,2,1,0:T(8,128)(2,1)} %get-tuple-element.142.refs_0_, bf16[2,2,12,512,128]{4,3,2,1,0:T(8,128)(2,1)} %get-tuple-element.143.refs_1_, ...), custom_call_target="tpu_custom_call" | custom-call | flops 80530636800 | bytes 164102144 | tf_op jit(solution)/shard_map/pallas_call | solution.py:81
  963.9 32.5 %shard_map.165 = (bf16[1,2,12,512,128]{4,3,2,1,0:T(8,128)(2,1)}, bf16[1,2,12,512,128]{4,3,2,1,0:T(8,128)(2,1)}, f32[1,1024,128]{2,1,0:T(8,128)}, f32[1,1024,128]{2,1,0:T(8,128)}) custom-call(s32[2]{0:T(128)} %pad_add_fusion.1.s_ref, bf16[2,2,12,512,128]{4,3,2,1,0:T(8,128)(2,1)} %shard_map.159.refs_0_, bf16[2,2,512,128]{3,2,1,0:T(8,128)(2,1)} %get-tuple-element.103.refs_1_, ...), custom_call_target="tpu_custom_call" | custom-call | flops 24159191040 | bytes 21495808 | tf_op jit(solution)/shard_map/pallas_call | solution.py:81
  1009.7 29.0 %shard_map.166 = f32[6,128,6144]{2,1,0:T(8,128)} custom-call(s32[2]{0:T(128)} %pad_add_fusion.1.s_ref, bf16[12,2,128,512]{3,2,1,0:T(8,128)(2,1)} %collective-permute-done.26.refs_0_.refs_1_, bf16[12,2,128,512]{3,2,1,0:T(8,128)(2,1)} %collective-permute-done.26.refs_0_.refs_1_, bf16[12,2,128,512]{3,2,1,0:T(8,128)(2,1)} %collective-permute-done.27.refs_2_.refs_3_, ...), custom_call_target="tpu_custom_call" | custom-call | flops 19327352832 | bytes 283115520 | tf_op jit(solution)/shard_map/pallas_call | solution.py:81
  1050.9 55.9 %shard_map.167 = f32[7,128,6144]{2,1,0:T(8,128)} custom-call(s32[2]{0:T(128)} %pad_add_fusion.1.s_ref, bf16[2,2,12,2,128,512]{5,4,3,2,1,0:T(8,128)(2,1)} %get-tuple-element.107.t_ref, bf16[2,2,128,512]{3,2,1,0:T(8,128)(2,1)} %copy.25.u0_ref, bf16[2,2,128,512]{3,2,1,0:T(8,128)(2,1)} %copy.26.u1_ref, ...), custom_call_target="tpu_custom_call" | custom-call | flops 45097156608 | bytes 389021696 | tf_op jit(solution)/shard_map/pallas_call | solution.py:81
  1107.3 39.7 %shard_map.168 = (f32[12,128,6144]{2,1,0:T(8,128)}, f32[6,128,6144]{2,1,0:T(8,128)}) custom-call(s32[2]{0:T(128)} %pad_add_fusion.1.s_ref, bf16[12,2,128,512]{3,2,1,0:T(8,128)(2,1)} %collective-permute-done.26.refs_0_.refs_1_, bf16[12,2,128,512]{3,2,1,0:T(8,128)(2,1)} %collective-permute-done.26.refs_0_.refs_1_, ...), custom_call_target="tpu_custom_call" | custom-call | flops 19327352832 | bytes 339738624 | tf_op jit(solution)/shard_map/pallas_call | solution.py:81
  1149.5 59.9 %shard_map.169 = (f32[12,6144,128]{2,1,0:T(8,128)}, f32[6,6144,128]{2,1,0:T(8,128)}, f32[6144,128]{1,0:T(8,128)}) custom-call(s32[2]{0:T(128)} %pad_add_fusion.1.s_ref, bf16[2,2,12,2,128,512]{5,4,3,2,1,0:T(8,128)(2,1)} %get-tuple-element.107.t_ref, bf16[2,2,128,512]{3,2,1,0:T(8,128)(2,1)} %copy.25.u0_ref, bf16[2,2,128,512]{3,2,1,0:T(8,128)(2,1)} %copy.26.u1_ref, ...), custom_call_target="tpu_custom_call" | custom-call | flops 45097156608 | bytes 448790528 | tf_op jit(solution)/shard_map/pallas_call | solution.py:81
  1210.8 75.0 %collective-permute-done.36.refs_23_ = bf16[512,6144]{1,0:T(8,128)(2,1)} collective-permute-done((bf16[512,6144]{1,0:T(8,128)(2,1)}, bf16[512,6144]{1,0:T(8,128)(2,1)}, u32[]{:S(2)}, u32[]{:S(2)}) %collective-permute-start.36) | collective-permute-done | bytes 6291488 | tf_op jit(solution)/shard_map/ppermute | solution.py:691
  1287.6 131.9 %collective-permute-done.38.refs_25_ = bf16[512,6144]{1,0:T(8,128)(2,1)} collective-permute-done((bf16[512,6144]{1,0:T(8,128)(2,1)}, bf16[512,6144]{1,0:T(8,128)(2,1)}, u32[]{:S(2)}, u32[]{:S(2)}) %collective-permute-start.38) | collective-permute-done | bytes 6291488 | tf_op jit(solution)/shard_map/ppermute | solution.py:695
  1425.8 94.5 %shard_map.170 = (bf16[8,512,6144]{2,1,0:T(8,128)(2,1)}, bf16[512,6144]{1,0:T(8,128)(2,1)}, bf16[8,512,6144]{2,1,0:T(8,128)(2,1)}, f32[12,128,6144]{2,1,0:T(8,128)}) custom-call(s32[2]{0:T(128)} %pad_add_fusion.1.s_ref, bf16[2,2,12,512,128]{4,3,2,1,0:T(8,128)(2,1)} %get-tuple-element.142.refs_0_, ...), custom_call_target="tpu_custom_call", output_to_operand_aliasing={{0}: (21, {}), {2}: (22, {}), {3}: (23, {})} | custom-call | flops 80530636800 | bytes 434634752 | tf_op jit(solution)/shard_map/pallas_call | solution.py:81
  1520.3 37.9 %collective-permute-done.42.refs_20_ = bf16[512,6144]{1,0:T(8,128)(2,1)} collective-permute-done((bf16[512,6144]{1,0:T(8,128)(2,1)}, bf16[512,6144]{1,0:T(8,128)(2,1)}, u32[]{:S(2)}, u32[]{:S(2)}) %collective-permute-start.42) | collective-permute-done | bytes 6291488 | tf_op jit(solution)/shard_map/ppermute | solution.py:691
  1562.1 89.6 %shard_map.171 = (bf16[8,512,6144]{2,1,0:T(8,128)(2,1)}, bf16[512,6144]{1,0:T(8,128)(2,1)}, bf16[8,512,6144]{2,1,0:T(8,128)(2,1)}, f32[12,6144,128]{2,1,0:T(8,128)}) custom-call(s32[2]{0:T(128)} %pad_add_fusion.1.s_ref, bf16[2,2,12,512,128]{4,3,2,1,0:T(8,128)(2,1)} %get-tuple-element.105.refs_0_, ...), custom_call_target="tpu_custom_call", output_to_operand_aliasing={{0}: (18, {}), {2}: (19, {}), {3}: (20, {})} | custom-call | flops 77309411328 | bytes 418381824 | tf_op jit(solution)/shard_map/pallas_call | solution.py:81
  (147 shorter events, 240.1 us)
Async XLA Ops:
  34.9 202.6 %collective-permute-start.6 = (bf16[3,128,6144]{2,1,0:T(8,128)(2,1)}, bf16[3,128,6144]{2,1,0:T(8,128)(2,1)}, u32[]{:S(2)}, u32[]{:S(2)}) collective-permute-start(bf16[3,128,6144]{2,1,0:T(8,128)(2,1)} %shard_map.148), channel_id=1, source_target_pairs={{0,2},{2,0},{4,6},{6,4},{1,3},{3,1},{5,7},{7,5}} | collective-permute-start | bytes 14155784 | tf_op jit(solution)/shard_map/ppermute | solution.py:691
  36.1 251.8 %collective-permute-start.8 = (bf16[3,128,6144]{2,1,0:T(8,128)(2,1)}, bf16[3,128,6144]{2,1,0:T(8,128)(2,1)}, u32[]{:S(2)}, u32[]{:S(2)}) collective-permute-start(bf16[3,128,6144]{2,1,0:T(8,128)(2,1)} %shard_map.148), channel_id=1, source_target_pairs={{0,4},{2,6},{4,0},{6,2},{1,5},{3,7},{5,1},{7,3}} | collective-permute-start | bytes 14155784 | tf_op jit(solution)/shard_map/ppermute | solution.py:691
  145.6 142.4 %collective-permute-start.3 = (bf16[3,6144,128]{2,1,0:T(8,128)(2,1)}, bf16[3,6144,128]{2,1,0:T(8,128)(2,1)}, u32[]{:S(2)}, u32[]{:S(2)}) collective-permute-start(bf16[3,6144,128]{2,1,0:T(8,128)(2,1)} %collective-permute-done.2.refs_2_.refs_6_), channel_id=1, source_target_pairs={{0,1},{1,0},{2,3},{3,2},{4,5},{5,4},{6,7},{7,6}} | collective-permute-start | bytes 14155784 | tf_op jit(solution)/shard_map/ppermute | solution.py:688
  145.6 142.8 %collective-permute-start.5 = (bf16[3,6144,128]{2,1,0:T(8,128)(2,1)}, bf16[3,6144,128]{2,1,0:T(8,128)(2,1)}, u32[]{:S(2)}, u32[]{:S(2)}) collective-permute-start(bf16[3,6144,128]{2,1,0:T(8,128)(2,1)} %collective-permute-done.4.refs_4_.refs_8_), channel_id=1, source_target_pairs={{0,1},{1,0},{2,3},{3,2},{4,5},{5,4},{6,7},{7,6}} | collective-permute-start | bytes 14155784 | tf_op jit(solution)/shard_map/ppermute | solution.py:688
  207.7 132.4 %collective-permute-start.10 = (bf16[3,6144,128]{2,1,0:T(8,128)(2,1)}, bf16[3,6144,128]{2,1,0:T(8,128)(2,1)}, u32[]{:S(2)}, u32[]{:S(2)}) collective-permute-start(bf16[3,6144,128]{2,1,0:T(8,128)(2,1)} %get-tuple-element.115), channel_id=1, source_target_pairs={{0,2},{2,0},{4,6},{6,4},{1,3},{3,1},{5,7},{7,5}} | collective-permute-start | bytes 14155784 | tf_op jit(solution)/shard_map/ppermute | solution.py:691
  560.1 115.9 %collective-permute-start.22 = (bf16[3,128,6144]{2,1,0:T(8,128)(2,1)}, bf16[3,128,6144]{2,1,0:T(8,128)(2,1)}, u32[]{:S(2)}, u32[]{:S(2)}) collective-permute-start(bf16[3,128,6144]{2,1,0:T(8,128)(2,1)} %collective-permute-done.6.refs_0_.refs_5_), channel_id=1, source_target_pairs={{0,4},{2,6},{4,0},{6,2},{1,5},{3,7},{5,1},{7,3}} | collective-permute-start | bytes 14155784 | tf_op jit(solution)/shard_map/ppermute | solution.py:691
  560.6 115.4 %collective-permute-start.24 = (bf16[3,128,6144]{2,1,0:T(8,128)(2,1)}, bf16[3,128,6144]{2,1,0:T(8,128)(2,1)}, u32[]{:S(2)}, u32[]{:S(2)}) collective-permute-start(bf16[3,128,6144]{2,1,0:T(8,128)(2,1)} %collective-permute-done.16.refs_2_.refs_11_), channel_id=1, source_target_pairs={{0,2},{2,0},{4,6},{6,4},{1,3},{3,1},{5,7},{7,5}} | collective-permute-start | bytes 14155784 | tf_op jit(solution)/shard_map/ppermute | solution.py:691
  685.7 321.1 %collective-permute-start.26 = (bf16[12,2,128,512]{3,2,1,0:T(8,128)(2,1)}, bf16[12,2,128,512]{3,2,1,0:T(8,128)(2,1)}, u32[]{:S(2)}, u32[]{:S(2)}) collective-permute-start(bf16[12,2,128,512]{3,2,1,0:T(8,128)(2,1)} %get-tuple-element.189), channel_id=1, source_target_pairs={{0,2},{2,0},{4,6},{6,4},{1,3},{3,1},{5,7},{7,5}} | collective-permute-start | bytes 9437192 | tf_op jit(solution)/shard_map/ppermute | solution.py:691
  686.5 321.8 %collective-permute-start.27 = (bf16[12,2,128,512]{3,2,1,0:T(8,128)(2,1)}, bf16[12,2,128,512]{3,2,1,0:T(8,128)(2,1)}, u32[]{:S(2)}, u32[]{:S(2)}) collective-permute-start(bf16[12,2,128,512]{3,2,1,0:T(8,128)(2,1)} %get-tuple-element.188), channel_id=1, source_target_pairs={{0,4},{2,6},{4,0},{6,2},{1,5},{3,7},{5,1},{7,3}} | collective-permute-start | bytes 9437192 | tf_op jit(solution)/shard_map/ppermute | solution.py:691
  688.0 320.4 %collective-permute-start.28 = (bf16[12,2,128,512]{3,2,1,0:T(8,128)(2,1)}, bf16[12,2,128,512]{3,2,1,0:T(8,128)(2,1)}, u32[]{:S(2)}, u32[]{:S(2)}) collective-permute-start(bf16[12,2,128,512]{3,2,1,0:T(8,128)(2,1)} %get-tuple-element.187), channel_id=1, source_target_pairs={{0,3},{1,2},{2,1},{3,0},{4,7},{5,6},{6,5},{7,4}} | collective-permute-start | bytes 9437192 | tf_op jit(solution)/shard_map/ppermute | solution.py:695
  702.0 307.7 %collective-permute-start.29 = (bf16[12,2,128,512]{3,2,1,0:T(8,128)(2,1)}, bf16[12,2,128,512]{3,2,1,0:T(8,128)(2,1)}, u32[]{:S(2)}, u32[]{:S(2)}) collective-permute-start(bf16[12,2,128,512]{3,2,1,0:T(8,128)(2,1)} %get-tuple-element.186), channel_id=1, source_target_pairs={{0,5},{1,4},{2,7},{3,6},{4,1},{5,0},{6,3},{7,2}} | collective-permute-start | bytes 9437192 | tf_op jit(solution)/shard_map/ppermute | solution.py:695
  1147.0 277.9 %collective-permute-start.41 = (f32[6,128,6144]{2,1,0:T(8,128)}, f32[6,128,6144]{2,1,0:T(8,128)}, u32[]{:S(2)}, u32[]{:S(2)}) collective-permute-start(f32[6,128,6144]{2,1,0:T(8,128)} %get-tuple-element.170), channel_id=1, source_target_pairs={{0,1},{1,0},{2,3},{3,2},{4,5},{5,4},{6,7},{7,6}} | collective-permute-start | bytes 56623112 | tf_op jit(solution)/shard_map/ppermute | solution.py:688
  1147.1 138.7 %collective-permute-start.36 = (bf16[512,6144]{1,0:T(8,128)(2,1)}, bf16[512,6144]{1,0:T(8,128)(2,1)}, u32[]{:S(2)}, u32[]{:S(2)}) collective-permute-start(bf16[512,6144]{1,0:T(8,128)(2,1)} %get-tuple-element.167), channel_id=1, source_target_pairs={{0,2},{2,0},{4,6},{6,4},{1,3},{3,1},{5,7},{7,5}} | collective-permute-start | bytes 18874376 | tf_op jit(solution)/shard_map/ppermute | solution.py:691
  1147.9 138.3 %collective-permute-start.37 = (bf16[512,6144]{1,0:T(8,128)(2,1)}, bf16[512,6144]{1,0:T(8,128)(2,1)}, u32[]{:S(2)}, u32[]{:S(2)}) collective-permute-start(bf16[512,6144]{1,0:T(8,128)(2,1)} %get-tuple-element.167), channel_id=1, source_target_pairs={{0,4},{2,6},{4,0},{6,2},{1,5},{3,7},{5,1},{7,3}} | collective-permute-start | bytes 18874376 | tf_op jit(solution)/shard_map/ppermute | solution.py:691
  1209.4 352.7 %collective-permute-start.45 = (f32[6,6144,128]{2,1,0:T(8,128)}, f32[6,6144,128]{2,1,0:T(8,128)}, u32[]{:S(2)}, u32[]{:S(2)}) collective-permute-start(f32[6,6144,128]{2,1,0:T(8,128)} %get-tuple-element.176), channel_id=1, source_target_pairs={{0,1},{1,0},{2,3},{3,2},{4,5},{5,4},{6,7},{7,6}} | collective-permute-start | bytes 56623112 | tf_op jit(solution)/shard_map/ppermute | solution.py:688
  1209.5 210.1 %collective-permute-start.38 = (bf16[512,6144]{1,0:T(8,128)(2,1)}, bf16[512,6144]{1,0:T(8,128)(2,1)}, u32[]{:S(2)}, u32[]{:S(2)}) collective-permute-start(bf16[512,6144]{1,0:T(8,128)(2,1)} %get-tuple-element.169), channel_id=1, source_target_pairs={{0,3},{1,2},{2,1},{3,0},{4,7},{5,6},{6,5},{7,4}} | collective-permute-start | bytes 18874376 | tf_op jit(solution)/shard_map/ppermute | solution.py:695
  1285.9 137.9 %collective-permute-start.39 = (bf16[512,6144]{1,0:T(8,128)(2,1)}, bf16[512,6144]{1,0:T(8,128)(2,1)}, u32[]{:S(2)}, u32[]{:S(2)}) collective-permute-start(bf16[512,6144]{1,0:T(8,128)(2,1)} %get-tuple-element.169), channel_id=1, source_target_pairs={{0,5},{1,4},{2,7},{3,6},{4,1},{5,0},{6,3},{7,2}} | collective-permute-start | bytes 18874376 | tf_op jit(solution)/shard_map/ppermute | solution.py:695
  1286.2 138.7 %collective-permute-start.40 = (bf16[512,6144]{1,0:T(8,128)(2,1)}, bf16[512,6144]{1,0:T(8,128)(2,1)}, u32[]{:S(2)}, u32[]{:S(2)}) collective-permute-start(bf16[512,6144]{1,0:T(8,128)(2,1)} %get-tuple-element.169), channel_id=1, source_target_pairs={{0,1},{1,0},{2,3},{3,2},{4,5},{5,4},{6,7},{7,6}} | collective-permute-start | bytes 18874376 | tf_op jit(solution)/shard_map/ppermute | solution.py:688
  1419.5 138.7 %collective-permute-start.42 = (bf16[512,6144]{1,0:T(8,128)(2,1)}, bf16[512,6144]{1,0:T(8,128)(2,1)}, u32[]{:S(2)}, u32[]{:S(2)}) collective-permute-start(bf16[512,6144]{1,0:T(8,128)(2,1)} %get-tuple-element.174), channel_id=1, source_target_pairs={{0,2},{2,0},{4,6},{6,4},{1,3},{3,1},{5,7},{7,5}} | collective-permute-start | bytes 18874376 | tf_op jit(solution)/shard_map/ppermute | solution.py:691
  1423.8 138.3 %collective-permute-start.43 = (bf16[512,6144]{1,0:T(8,128)(2,1)}, bf16[512,6144]{1,0:T(8,128)(2,1)}, u32[]{:S(2)}, u32[]{:S(2)}) collective-permute-start(bf16[512,6144]{1,0:T(8,128)(2,1)} %get-tuple-element.174), channel_id=1, source_target_pairs={{0,4},{2,6},{4,0},{6,2},{1,5},{3,7},{5,1},{7,3}} | collective-permute-start | bytes 18874376 | tf_op jit(solution)/shard_map/ppermute | solution.py:691
  1424.9 137.2 %collective-permute-start.44 = (bf16[512,6144]{1,0:T(8,128)(2,1)}, bf16[512,6144]{1,0:T(8,128)(2,1)}, u32[]{:S(2)}, u32[]{:S(2)}) collective-permute-start(bf16[512,6144]{1,0:T(8,128)(2,1)} %get-tuple-element.175), channel_id=1, source_target_pairs={{0,1},{1,0},{2,3},{3,2},{4,5},{5,4},{6,7},{7,6}} | collective-permute-start | bytes 18874376 | tf_op jit(solution)/shard_map/ppermute | solution.py:688
  1424.9 267.6 %collective-permute-start.46 = (bf16[512,6144]{1,0:T(8,128)(2,1)}, bf16[512,6144]{1,0:T(8,128)(2,1)}, u32[]{:S(2)}, u32[]{:S(2)}) collective-permute-start(bf16[512,6144]{1,0:T(8,128)(2,1)} %get-tuple-element.175), channel_id=1, source_target_pairs={{0,3},{1,2},{2,1},{3,0},{4,7},{5,6},{6,5},{7,4}} | collective-permute-start | bytes 18874376 | tf_op jit(solution)/shard_map/ppermute | solution.py:695
  1558.2 138.1 %collective-permute-start.47 = (bf16[512,6144]{1,0:T(8,128)(2,1)}, bf16[512,6144]{1,0:T(8,128)(2,1)}, u32[]{:S(2)}, u32[]{:S(2)}) collective-permute-start(bf16[512,6144]{1,0:T(8,128)(2,1)} %get-tuple-element.175), channel_id=1, source_target_pairs={{0,5},{1,4},{2,7},{3,6},{4,1},{5,0},{6,3},{7,2}} | collective-permute-start | bytes 18874376 | tf_op jit(solution)/shard_map/ppermute | solution.py:695
  1562.1 134.3 %collective-permute-start.48 = (bf16[512,6144]{1,0:T(8,128)(2,1)}, bf16[512,6144]{1,0:T(8,128)(2,1)}, u32[]{:S(2)}, u32[]{:S(2)}) collective-permute-start(bf16[512,6144]{1,0:T(8,128)(2,1)} %get-tuple-element.179), channel_id=1, source_target_pairs={{0,1},{1,0},{2,3},{3,2},{4,5},{5,4},{6,7},{7,6}} | collective-permute-start | bytes 18874376 | tf_op jit(solution)/shard_map/ppermute | solution.py:688
  (35 other events, 1765.9 us)

commit v4 on v3

--- a/solution.py
+++ b/solution.py
@@ -512,26 +512,32 @@
 
 
 def dw_local_body(s_ref, t_ref, *refs):
-    xs, o_ref = refs[:4], refs[4]
+    xs, o_ref = refs[:4], refs[-1]
     a = lanes([stack([t_ref[l, p, h] for h in range(t_ref.shape[2])]) for l in range(2) for p in range(2)])
     o_ref[...] = dot_nn(a, stack([x[...] for x in xs])).reshape(o_ref.shape)
 
 
-def dw_local(scal, which, turned, x, x_recv):
+def dw_local(scal, turned, x, x_recv, prior=()):
     d = x.shape[-1]
+    steps = d // DW_COLS // 2
+    shift = steps * len(prior)
     block = (None, PIECE, DW_COLS)
-    mine = [spec(block, lambda n, s, l=l: (seq_of(l, s), 0, n)) for l in range(2)]
-    recv = [spec(block, lambda n, s, l=l: (l, 0, n)) for l in range(2)]
+    rows_at = []
+    for l in range(2):
+        rows_at.append(spec(block, lambda n, s, l=l: (seq_of(l, s), 0, n + shift)))
+        rows_at.append(spec(block, lambda n, s, l=l: (l, 0, n + shift)))
     n_heads = turned.shape[2]
+    ins = [turned, x, x_recv, x, x_recv]
     return call(
         dw_local_body,
-        (d // DW_COLS,),
+        (steps,),
         scal,
-        [turned, x, x_recv, x, x_recv],
-        [spec((2, 2, n_heads, None, E, PIECE), lambda n, s: (0, 0, 0, which)), mine[0], recv[0], mine[1], recv[1]],
+        [*ins, *prior],
+        [spec((2, 2, n_heads, None, E, PIECE)), *rows_at] + [HBM] * len(prior),
         struct(F32, n_heads, E, d),
-        spec((n_heads, E, DW_COLS), lambda n, s: (0, 0, n)),
-        4 * n_heads * E * ROWS * d,
+        spec((n_heads, E, DW_COLS), lambda n, s: (0, 0, n + shift)),
+        2 * n_heads * E * ROWS * d,
+        aliases={1 + len(ins): 0} if prior else None,
     )
 
 
@@ -584,11 +590,14 @@
 
 def dw_in_body(last, s_ref, t_ref, u0_ref, u1_ref, *refs):
     ts, kvs, xs, refs = refs[:8], refs[8:12], refs[12:20], refs[20:]
+    turn = lambda x: [x.astype(F32).T.astype(BF16)]
     groups = [
-        stack([t_ref[l, p, h] for h in range(GROUP)] + [u[p]]) for l, u in enumerate((u0_ref, u1_ref)) for p in range(2)
+        stack([t_ref[l, p, h] for h in range(GROUP)] + turn(u[p]))
+        for l, u in enumerate((u0_ref, u1_ref))
+        for p in range(2)
     ]
     groups += [
-        stack([t[h] for t in ts[2 * g : 2 * g + 2] for h in range(UNIT)] + [kvs[g][...]]) for g in range(len(kvs))
+        stack([t[h] for t in ts[2 * g : 2 * g + 2] for h in range(UNIT)] + turn(kv[...])) for g, kv in enumerate(kvs)
     ]
     acc = dot_nn(lanes(groups), stack([x[...] for x in xs])).reshape(GROUP + 1, E, DW_COLS)
     if not last:
@@ -605,12 +614,12 @@
     kv_half = lambda s: jnp.bitwise_xor(half, s[1])
     near, rows_at = near_specs(half, 1)
     local = [spec((2, 2, GROUP, None, E, PIECE), lambda n, s: (0, 0, half, 1))]
-    local += [spec((2, None, E, PIECE), lambda n, s: (0, kv_half(s)))] * 2
+    local += [spec((None, 2, None, PIECE, E), lambda n, s: (0, 0, kv_half(s)))] * 2
     block = (None, PIECE, DW_COLS)
     for l in range(2):
         rows_at.insert(2 * l, spec(block, lambda n, s, l=l: (seq_of(l, s), 0, n)))
         rows_at.insert(2 * l + 1, spec(block, lambda n, s, l=l: (l, 0, n)))
-    near += [spec((None, E, PIECE), lambda n, s: (kv_half(s),))] * len(kv)
+    near += [spec((None, PIECE, E), lambda n, s: (kv_half(s),))] * len(kv)
     ins = [turned_0, kv_0, kv_1, *(t for t in turned for _ in range(2)), *kv, x, x_recv, x, x_recv, x, x, x, x]
     specs = local + near + rows_at
     part = spec((GROUP + 1, E, DW_COLS), lambda n, s: (0, 0, n))
@@ -750,15 +759,16 @@
             wo_in[a, 1] = to_chip(wo_sent, a)
         wq_n0, wq_d0 = relay(wq_in, 0, do_0)
         o_0, dq_0, dk_0, dv_0, t_0 = step(attention, "fused", q_0, k, v, do_0, tables_t, turned=OWN)
-        dwo = step(dw_local, 0, t_0, grad, g_recv)
+        dwo = step(dw_local, t_0, grad, g_recv)
 
         wo_n0, wo_d0 = relay(wo_in, 0, dwo)
         (q_n0,) = step(proj, "q", hidden, h_recv, wq_n0, tables)
-        wq_n1, wq_d1 = relay(wq_in, 1, q_n0)
         (do_n0,) = step(proj, "do", grad, g_recv, wo_n0)
+        wq_n1, wq_d1 = relay(wq_in, 1, do_n0)
+        o_n0, dq_n0, dk_n0, dv_n0, t_n0 = step(attention, "fused", q_n0, k, v, do_n0, tables_t, turned=0)
         (q_n1,) = step(proj, "q", hidden, h_recv, wq_n1, tables)
         wo_n1, wo_d1 = relay(wo_in, 1, q_n1)
-        o_n0, dq_n0, dk_n0, dv_n0, t_n0 = step(attention, "fused", q_n0, k, v, do_n0, tables_t, turned=0)
+        dwo = step(dw_local, t_0, grad, g_recv, prior=[dwo])
         (do_n1,) = step(proj, "do", grad, g_recv, wo_n1)
         wq_d = with_partner([after(w, do_n1) for w in (wq_d0, wq_d1)])
         o_n1, dq_n1, dk_n1, dv_n1, t_n1 = step(attention, "fused", q_n1, k, v, do_n1, tables_t, turned=1, prior=[t_n0])
@@ -781,22 +791,21 @@
             ]
             dk = dk * tables[0] - jnp.roll(dk, HALF, axis=1) * tables[1]
             x = jnp.stack([dk, dv]).astype(BF16).reshape(2, 2, PIECE, E).transpose(1, 0, 2, 3)
-            x = jnp.where(c == 0, x, x[::-1])
-            return x[None], x.transpose(0, 1, 3, 2)
-
-        dkv_0, dkv_t = finish_kv(0, dk_d, dv_d)
-        kv_nb = spread(dkv_t[0], dkv_t[1])
-        out_r = after(out_r, dkv_t)
+            return jnp.where(c == 0, x, x[::-1])[None]
+
+        dkv_0 = finish_kv(0, dk_d, dv_d)
+        kv_nb = spread(dkv_0[0, 0], dkv_0[0, 1])
+        out_r = after(out_r, dkv_0)
         out_r = to_both(to_chip_other, out_r) + [on_chip(out_r)]
         dh_big, dh_r, dh_m = step(combine, "dh", 0, [dq_0, dq_n0, dq_n1, dq_d, dkv_0], wq_all, kv=kv_w)
         dh_in = spread(dh_m, dh_r) + [on_chip(dh_r)]
 
         o_e, dq_e, dk_e, dv_e = step(attention, "fused", q_d, k, v, do_d, tables_t, l0=1, nl=1)
-        dkv_1, dkv_u = finish_kv(1, dk_e, dv_e)
+        dkv_1 = finish_kv(1, dk_e, dv_e)
 
         (wo_part,) = step(dw_rest, 1, t_nb, grad, dwo)
         wo_part = on_chip(wo_part)
-        dw_args = t_0, dkv_t, dkv_u, t_nb, kv_nb, hidden, h_recv
+        dw_args = t_0, dkv_0, dkv_1, t_nb, kv_nb, hidden, h_recv
         (wq_part,) = step(dw_in, 1, *dw_args)
         wq_part = on_chip(wq_part)
         dwo_big, dwo_mine = step(dw_rest, 0, t_nb, grad, dwo, wo_part)

time: 1730 us -> 1720 us (level)
    pallas_call x29 -> x30, Pallas kernels: 1320 us -> 1320 us  [call(): pl.pallas_call(body, grid_spec=pltpu.PrefetchScalarGridSpec(num_scalar_pr...]
  transfers between devices with their start and end apart: 51 -> 51, of which waited for: 12 -> 15; matrix products, arithmetic and copies ran while one was open for 2% -> 2% of each run, Pallas kernels for 76% -> 77%
where the time goes in v4:
time: 1720 us; the launch traced here: 1710 us
  Pallas kernels  1320 us (77%)
  waiting for transfers between devices  321 us (19%)
  starting transfers between devices  32.7 us (2%)
  other arithmetic  18.8 us (1%)
    pallas_call x30, Pallas kernels, call(): pl.pallas_call(body, grid_spec=pltpu.PrefetchScalarGridSpec(num_scalar_pr...  1320 us
    ppermute x8, waiting for transfers between devices, to_chip_other(): return lax.ppermute(x, ('tp', 'cp'), pairs)  161 us
    ppermute x20, waiting for transfers between devices, to_chip(): return lax.ppermute(x, 'tp', [(i, i ^ flip) for i in chips])  146 us
  transfers between devices with their start and end apart: 51, of which 15 were waited for; matrix products, arithmetic and copies ran while one was open for 2% of the time, Pallas kernels for 77%

profile of v4, /device:TPU:0, one launch (start us, length us, event | category | flops | bytes accessed | tf_op | source)
XLA Modules:
  0.0 1711.4 jit_solution(16001874541786654204)
XLA Ops:
  36.2 58.9 %shard_map.146 = (bf16[2,2,12,512,128]{4,3,2,1,0:T(8,128)(2,1)}, bf16[2,2,512,128]{3,2,1,0:T(8,128)(2,1)}, bf16[2,2,512,128]{3,2,1,0:T(8,128)(2,1)}) custom-call(s32[2]{0:T(128)} %pad_add_fusion.1.s_ref, bf16[8,512,6144]{2,1,0:T(8,128)(2,1)} %refs_19_.6, bf16[2,512,6144]{2,1,0:T(8,128)(2,1)} %collective-permute-done.r_ref.refs_13_.refs_15_, ...), custom_call_target="tpu_custom_call" | custom-call | flops 38654705664 | bytes 93323264 | tf_op jit(solution)/shard_map/pallas_call | solution.py:81
  95.0 50.6 %shard_map.150 = (bf16[2,2,12,512,128]{4,3,2,1,0:T(8,128)(2,1)}, bf16[3,128,6144]{2,1,0:T(8,128)(2,1)}, bf16[3,6144,128]{2,1,0:T(8,128)(2,1)}) custom-call(s32[2]{0:T(128)} %pad_add_fusion.1.s_ref, bf16[8,512,6144]{2,1,0:T(8,128)(2,1)} %refs_11_.3, bf16[2,512,6144]{2,1,0:T(8,128)(2,1)} %collective-permute-done.1.r_ref.refs_1_.refs_3_, ...), custom_call_target="tpu_custom_call" | custom-call | flops 38654705664 | bytes 116391936 | tf_op jit(solution)/shard_map/pallas_call | solution.py:81
  146.2 61.7 %shard_map.151 = (bf16[2,2,12,512,128]{4,3,2,1,0:T(8,128)(2,1)}, bf16[2,2,12,512,128]{4,3,2,1,0:T(8,128)(2,1)}, f32[2,1024,128]{2,1,0:T(8,128)}, f32[2,1024,128]...) custom-call(s32[2]{0:T(128)} %pad_add_fusion.1.s_ref, bf16[2,2,12,512,128]{4,3,2,1,0:T(8,128)(2,1)} %get-tuple-element.97.refs_0_, ...), custom_call_target="tpu_custom_call" | custom-call | flops 48318382080 | bytes 41418752 | tf_op jit(solution)/shard_map/pallas_call | solution.py:81
  207.9 28.0 %shard_map.152.refs_4_ = f32[12,128,6144]{2,1,0:T(8,128)} custom-call(s32[2]{0:T(128)} %pad_add_fusion.1.s_ref, bf16[2,2,12,2,128,512]{5,4,3,2,1,0:T(8,128)(2,1)} %get-tuple-element.108.t_ref, bf16[8,512,6144]{2,1,0:T(8,128)(2,1)} %refs_11_.3, bf16[2,512,6144]{2,1,0:T(8,128)(2,1)} %collective-permute-done.1.r_ref.refs_1_.refs_3_, ...), custom_call_target="tpu_custom_call" | custom-call | flops 19327352832 | bytes 176160768 | tf_op jit(solution)/shard_map/pallas_call | solution.py:81
  240.7 51.7 %shard_map.153.refs_0_ = bf16[2,2,12,512,128]{4,3,2,1,0:T(8,128)(2,1)} custom-call(s32[2]{0:T(128)} %pad_add_fusion.1.s_ref, bf16[8,512,6144]{2,1,0:T(8,128)(2,1)} %refs_19_.6, bf16[2,512,6144]{2,1,0:T(8,128)(2,1)} %collective-permute-done.r_ref.refs_13_.refs_15_, f32[1024,128]{1,0:T(8,128)} %constant.24.clone.refs_0_, f32[1024,128]{1,0:T(8,128)} %constant.25.clone.refs_1_, ...), custom_call_target="tpu_custom_call" | custom-call | flops 38654705664 | bytes 89128960 | tf_op jit(solution)/shard_map/pallas_call | solution.py:81
  292.4 49.3 %shard_map.154.refs_3_ = bf16[2,2,12,512,128]{4,3,2,1,0:T(8,128)(2,1)} custom-call(s32[2]{0:T(128)} %pad_add_fusion.1.s_ref, bf16[8,512,6144]{2,1,0:T(8,128)(2,1)} %refs_11_.3, bf16[2,512,6144]{2,1,0:T(8,128)(2,1)} %collective-permute-done.1.r_ref.refs_1_.refs_3_, bf16[3,128,6144]{2,1,0:T(8,128)(2,1)} %collective-permute-done.6.refs_0_.refs_5_, ...), custom_call_target="tpu_custom_call" | custom-call | flops 38654705664 | bytes 88080384 | tf_op jit(solution)/shard_map/pallas_call | solution.py:81
  346.2 62.2 %shard_map.155 = (bf16[2,2,12,512,128]{4,3,2,1,0:T(8,128)(2,1)}, bf16[2,2,12,512,128]{4,3,2,1,0:T(8,128)(2,1)}, f32[2,1024,128]{2,1,0:T(8,128)}, f32[2,1024,128]...) custom-call(s32[2]{0:T(128)} %pad_add_fusion.1.s_ref, bf16[2,2,12,512,128]{4,3,2,1,0:T(8,128)(2,1)} %shard_map.153.refs_0_, ...), custom_call_target="tpu_custom_call" | custom-call | flops 48318382080 | bytes 54001664 | tf_op jit(solution)/shard_map/pallas_call | solution.py:81
  408.4 51.8 %shard_map.156.refs_0_ = bf16[2,2,12,512,128]{4,3,2,1,0:T(8,128)(2,1)} custom-call(s32[2]{0:T(128)} %pad_add_fusion.1.s_ref, bf16[8,512,6144]{2,1,0:T(8,128)(2,1)} %refs_19_.6, bf16[2,512,6144]{2,1,0:T(8,128)(2,1)} %collective-permute-done.r_ref.refs_13_.refs_15_, f32[1024,128]{1,0:T(8,128)} %constant.24.clone.refs_0_, f32[1024,128]{1,0:T(8,128)} %constant.25.clone.refs_1_, ...), custom_call_target="tpu_custom_call" | custom-call | flops 38654705664 | bytes 89128960 | tf_op jit(solution)/shard_map/pallas_call | solution.py:81
  489.8 49.5 %shard_map.158.refs_3_ = bf16[2,2,12,512,128]{4,3,2,1,0:T(8,128)(2,1)} custom-call(s32[2]{0:T(128)} %pad_add_fusion.1.s_ref, bf16[8,512,6144]{2,1,0:T(8,128)(2,1)} %refs_11_.3, bf16[2,512,6144]{2,1,0:T(8,128)(2,1)} %collective-permute-done.1.r_ref.refs_1_.refs_3_, bf16[3,128,6144]{2,1,0:T(8,128)(2,1)} %collective-permute-done.14.refs_0_.refs_9_, ...), custom_call_target="tpu_custom_call" | custom-call | flops 38654705664 | bytes 88080384 | tf_op jit(solution)/shard_map/pallas_call | solution.py:81
  567.3 61.8 %shard_map.159 = (bf16[2,2,12,512,128]{4,3,2,1,0:T(8,128)(2,1)}, bf16[2,2,12,512,128]{4,3,2,1,0:T(8,128)(2,1)}, f32[2,1024,128]{2,1,0:T(8,128)}, f32[2,1024,128]...) custom-call(s32[2]{0:T(128)} %pad_add_fusion.1.s_ref, ...), custom_call_target="tpu_custom_call", output_to_operand_aliasing={{4}: (7, {})} | custom-call | flops 48318382080 | bytes 79167488 | tf_op jit(solution)/shard_map/pallas_call | solution.py:81
  629.1 51.8 %shard_map.160.refs_0_ = bf16[2,2,12,512,128]{4,3,2,1,0:T(8,128)(2,1)} custom-call(s32[2]{0:T(128)} %pad_add_fusion.1.s_ref, bf16[8,512,6144]{2,1,0:T(8,128)(2,1)} %refs_19_.6, bf16[2,512,6144]{2,1,0:T(8,128)(2,1)} %collective-permute-done.r_ref.refs_13_.refs_15_, f32[1024,128]{1,0:T(8,128)} %constant.24.clone.refs_0_, f32[1024,128]{1,0:T(8,128)} %constant.25.clone.refs_1_, ...), custom_call_target="tpu_custom_call" | custom-call | flops 38654705664 | bytes 89128960 | tf_op jit(solution)/shard_map/pallas_call | solution.py:81
  708.1 89.2 %shard_map.162 = (bf16[8,512,6144]{2,1,0:T(8,128)(2,1)}, bf16[512,6144]{1,0:T(8,128)(2,1)}, bf16[512,6144]{1,0:T(8,128)(2,1)}) custom-call(s32[2]{0:T(128)} %pad_add_fusion.1.s_ref, bf16[2,2,12,512,128]{4,3,2,1,0:T(8,128)(2,1)} %get-tuple-element.106.refs_0_, bf16[2,2,12,512,128]{4,3,2,1,0:T(8,128)(2,1)} %get-tuple-element.116.refs_1_, ...), custom_call_target="tpu_custom_call" | custom-call | flops 77309411328 | bytes 160432128 | tf_op jit(solution)/shard_map/pallas_call | solution.py:81
  797.3 49.1 %shard_map.163.refs_3_ = bf16[2,2,12,512,128]{4,3,2,1,0:T(8,128)(2,1)} custom-call(s32[2]{0:T(128)} %pad_add_fusion.1.s_ref, bf16[8,512,6144]{2,1,0:T(8,128)(2,1)} %refs_11_.3, bf16[2,512,6144]{2,1,0:T(8,128)(2,1)} %collective-permute-done.1.r_ref.refs_1_.refs_3_, bf16[3,128,6144]{2,1,0:T(8,128)(2,1)} %collective-permute-done.22.refs_13_.refs_0_, ...), custom_call_target="tpu_custom_call" | custom-call | flops 38654705664 | bytes 88080384 | tf_op jit(solution)/shard_map/pallas_call | solution.py:81
  875.6 93.3 %shard_map.165 = (bf16[8,512,6144]{2,1,0:T(8,128)(2,1)}, bf16[512,6144]{1,0:T(8,128)(2,1)}, bf16[512,6144]{1,0:T(8,128)(2,1)}) custom-call(s32[2]{0:T(128)} %pad_add_fusion.1.s_ref, bf16[2,2,12,512,128]{4,3,2,1,0:T(8,128)(2,1)} %get-tuple-element.144.refs_0_, bf16[2,2,12,512,128]{4,3,2,1,0:T(8,128)(2,1)} %get-tuple-element.145.refs_1_, ...), custom_call_target="tpu_custom_call" | custom-call | flops 80530636800 | bytes 164102144 | tf_op jit(solution)/shard_map/pallas_call | solution.py:81
  969.0 32.3 %shard_map.166 = (bf16[1,2,12,512,128]{4,3,2,1,0:T(8,128)(2,1)}, bf16[1,2,12,512,128]{4,3,2,1,0:T(8,128)(2,1)}, f32[1,1024,128]{2,1,0:T(8,128)}, f32[1,1024,128]{2,1,0:T(8,128)}) custom-call(s32[2]{0:T(128)} %pad_add_fusion.1.s_ref, bf16[2,2,12,512,128]{4,3,2,1,0:T(8,128)(2,1)} %shard_map.160.refs_0_, bf16[2,2,512,128]{3,2,1,0:T(8,128)(2,1)} %get-tuple-element.104.refs_1_, ...), custom_call_target="tpu_custom_call" | custom-call | flops 24159191040 | bytes 21495808 | tf_op jit(solution)/shard_map/pallas_call | solution.py:81
  1012.7 29.0 %shard_map.167 = f32[6,128,6144]{2,1,0:T(8,128)} custom-call(s32[2]{0:T(128)} %pad_add_fusion.1.s_ref, bf16[12,2,128,512]{3,2,1,0:T(8,128)(2,1)} %collective-permute-done.26.refs_0_.refs_1_, bf16[12,2,128,512]{3,2,1,0:T(8,128)(2,1)} %collective-permute-done.26.refs_0_.refs_1_, bf16[12,2,128,512]{3,2,1,0:T(8,128)(2,1)} %collective-permute-done.27.refs_2_.refs_3_, ...), custom_call_target="tpu_custom_call" | custom-call | flops 19327352832 | bytes 283115520 | tf_op jit(solution)/shard_map/pallas_call | solution.py:81
  1045.6 56.1 %shard_map.168 = f32[7,128,6144]{2,1,0:T(8,128)} custom-call(s32[2]{0:T(128)} %pad_add_fusion.1.s_ref, bf16[2,2,12,2,128,512]{5,4,3,2,1,0:T(8,128)(2,1)} %get-tuple-element.108.t_ref, bf16[1,2,2,512,128]{4,3,2,1,0:T(8,128)(2,1)} %fusion.refs_4_.u0_ref, bf16[1,2,2,512,128]{4,3,2,1,0:T(8,128)(2,1)} %fusion.1.u1_ref.refs_4_, ...), custom_call_target="tpu_custom_call" | custom-call | flops 45097156608 | bytes 389021696 | tf_op jit(solution)/shard_map/pallas_call | solution.py:81
  1102.3 39.5 %shard_map.169 = (f32[12,128,6144]{2,1,0:T(8,128)}, f32[6,128,6144]{2,1,0:T(8,128)}) custom-call(s32[2]{0:T(128)} %pad_add_fusion.1.s_ref, bf16[12,2,128,512]{3,2,1,0:T(8,128)(2,1)} %collective-permute-done.26.refs_0_.refs_1_, bf16[12,2,128,512]{3,2,1,0:T(8,128)(2,1)} %collective-permute-done.26.refs_0_.refs_1_, ...), custom_call_target="tpu_custom_call" | custom-call | flops 19327352832 | bytes 339738624 | tf_op jit(solution)/shard_map/pallas_call | solution.py:81
  1144.0 60.3 %shard_map.170 = (f32[12,6144,128]{2,1,0:T(8,128)}, f32[6,6144,128]{2,1,0:T(8,128)}, f32[6144,128]{1,0:T(8,128)}) custom-call(s32[2]{0:T(128)} %pad_add_fusion.1.s_ref, bf16[2,2,12,2,128,512]{5,4,3,2,1,0:T(8,128)(2,1)} %get-tuple-element.108.t_ref, bf16[1,2,2,512,128]{4,3,2,1,0:T(8,128)(2,1)} %fusion.refs_4_.u0_ref, ...), custom_call_target="tpu_custom_call" | custom-call | flops 45097156608 | bytes 448790528 | tf_op jit(solution)/shard_map/pallas_call | solution.py:81
  1205.4 75.2 %collective-permute-done.36.refs_23_ = bf16[512,6144]{1,0:T(8,128)(2,1)} collective-permute-done((bf16[512,6144]{1,0:T(8,128)(2,1)}, bf16[512,6144]{1,0:T(8,128)(2,1)}, u32[]{:S(2)}, u32[]{:S(2)}) %collective-permute-start.36) | collective-permute-done | bytes 6291488 | tf_op jit(solution)/shard_map/ppermute | solution.py:700
  1281.6 132.8 %collective-permute-done.38.refs_25_ = bf16[512,6144]{1,0:T(8,128)(2,1)} collective-permute-done((bf16[512,6144]{1,0:T(8,128)(2,1)}, bf16[512,6144]{1,0:T(8,128)(2,1)}, u32[]{:S(2)}, u32[]{:S(2)}) %collective-permute-start.38) | collective-permute-done | bytes 6291488 | tf_op jit(solution)/shard_map/ppermute | solution.py:704
  1420.6 94.3 %shard_map.171 = (bf16[8,512,6144]{2,1,0:T(8,128)(2,1)}, bf16[512,6144]{1,0:T(8,128)(2,1)}, bf16[8,512,6144]{2,1,0:T(8,128)(2,1)}, f32[12,128,6144]{2,1,0:T(8,128)}) custom-call(s32[2]{0:T(128)} %pad_add_fusion.1.s_ref, bf16[2,2,12,512,128]{4,3,2,1,0:T(8,128)(2,1)} %get-tuple-element.144.refs_0_, ...), custom_call_target="tpu_custom_call", output_to_operand_aliasing={{0}: (21, {}), {2}: (22, {}), {3}: (23, {})} | custom-call | flops 80530636800 | bytes 434634752 | tf_op jit(solution)/shard_map/pallas_call | solution.py:81
  1514.9 38.2 %collective-permute-done.42.refs_20_ = bf16[512,6144]{1,0:T(8,128)(2,1)} collective-permute-done((bf16[512,6144]{1,0:T(8,128)(2,1)}, bf16[512,6144]{1,0:T(8,128)(2,1)}, u32[]{:S(2)}, u32[]{:S(2)}) %collective-permute-start.42) | collective-permute-done | bytes 6291488 | tf_op jit(solution)/shard_map/ppermute | solution.py:700
  1555.5 89.6 %shard_map.172 = (bf16[8,512,6144]{2,1,0:T(8,128)(2,1)}, bf16[512,6144]{1,0:T(8,128)(2,1)}, bf16[8,512,6144]{2,1,0:T(8,128)(2,1)}, f32[12,6144,128]{2,1,0:T(8,128)}) custom-call(s32[2]{0:T(128)} %pad_add_fusion.1.s_ref, bf16[2,2,12,512,128]{4,3,2,1,0:T(8,128)(2,1)} %get-tuple-element.106.refs_0_, ...), custom_call_target="tpu_custom_call", output_to_operand_aliasing={{0}: (18, {}), {2}: (19, {}), {3}: (20, {})} | custom-call | flops 77309411328 | bytes 418381824 | tf_op jit(solution)/shard_map/pallas_call | solution.py:81
  (136 shorter events, 254.0 us)
Async XLA Ops:
  30.5 115.1 %collective-permute-start.2 = (bf16[3,6144,128]{2,1,0:T(8,128)(2,1)}, bf16[3,6144,128]{2,1,0:T(8,128)(2,1)}, u32[]{:S(2)}, u32[]{:S(2)}) collective-permute-start(bf16[3,6144,128]{2,1,0:T(8,128)(2,1)} %shard_map.147), channel_id=1, source_target_pairs={{0,2},{2,0},{4,6},{6,4},{1,3},{3,1},{5,7},{7,5}} | collective-permute-start | bytes 14155784 | tf_op jit(solution)/shard_map/ppermute | solution.py:700
  35.0 201.9 %collective-permute-start.6 = (bf16[3,128,6144]{2,1,0:T(8,128)(2,1)}, bf16[3,128,6144]{2,1,0:T(8,128)(2,1)}, u32[]{:S(2)}, u32[]{:S(2)}) collective-permute-start(bf16[3,128,6144]{2,1,0:T(8,128)(2,1)} %shard_map.148), channel_id=1, source_target_pairs={{0,2},{2,0},{4,6},{6,4},{1,3},{3,1},{5,7},{7,5}} | collective-permute-start | bytes 14155784 | tf_op jit(solution)/shard_map/ppermute | solution.py:700
  36.2 202.2 %collective-permute-start.8 = (bf16[3,128,6144]{2,1,0:T(8,128)(2,1)}, bf16[3,128,6144]{2,1,0:T(8,128)(2,1)}, u32[]{:S(2)}, u32[]{:S(2)}) collective-permute-start(bf16[3,128,6144]{2,1,0:T(8,128)(2,1)} %shard_map.148), channel_id=1, source_target_pairs={{0,4},{2,6},{4,0},{6,2},{1,5},{3,7},{5,1},{7,3}} | collective-permute-start | bytes 14155784 | tf_op jit(solution)/shard_map/ppermute | solution.py:700
  343.4 116.8 %collective-permute-start.14 = (bf16[3,128,6144]{2,1,0:T(8,128)(2,1)}, bf16[3,128,6144]{2,1,0:T(8,128)(2,1)}, u32[]{:S(2)}, u32[]{:S(2)}) collective-permute-start(bf16[3,128,6144]{2,1,0:T(8,128)(2,1)} %get-tuple-element.123), channel_id=1, source_target_pairs={{0,2},{2,0},{4,6},{6,4},{1,3},{3,1},{5,7},{7,5}} | collective-permute-start | bytes 14155784 | tf_op jit(solution)/shard_map/ppermute | solution.py:700
  344.7 115.6 %collective-permute-start.16 = (bf16[3,128,6144]{2,1,0:T(8,128)(2,1)}, bf16[3,128,6144]{2,1,0:T(8,128)(2,1)}, u32[]{:S(2)}, u32[]{:S(2)}) collective-permute-start(bf16[3,128,6144]{2,1,0:T(8,128)(2,1)} %get-tuple-element.123), channel_id=1, source_target_pairs={{0,4},{2,6},{4,0},{6,2},{1,5},{3,7},{5,1},{7,3}} | collective-permute-start | bytes 14155784 | tf_op jit(solution)/shard_map/ppermute | solution.py:700
  565.3 115.6 %collective-permute-start.22 = (bf16[3,128,6144]{2,1,0:T(8,128)(2,1)}, bf16[3,128,6144]{2,1,0:T(8,128)(2,1)}, u32[]{:S(2)}, u32[]{:S(2)}) collective-permute-start(bf16[3,128,6144]{2,1,0:T(8,128)(2,1)} %collective-permute-done.6.refs_0_.refs_5_), channel_id=1, source_target_pairs={{0,4},{2,6},{4,0},{6,2},{1,5},{3,7},{5,1},{7,3}} | collective-permute-start | bytes 14155784 | tf_op jit(solution)/shard_map/ppermute | solution.py:700
  566.5 114.4 %collective-permute-start.24 = (bf16[3,128,6144]{2,1,0:T(8,128)(2,1)}, bf16[3,128,6144]{2,1,0:T(8,128)(2,1)}, u32[]{:S(2)}, u32[]{:S(2)}) collective-permute-start(bf16[3,128,6144]{2,1,0:T(8,128)(2,1)} %collective-permute-done.16.refs_2_.refs_11_), channel_id=1, source_target_pairs={{0,2},{2,0},{4,6},{6,4},{1,3},{3,1},{5,7},{7,5}} | collective-permute-start | bytes 14155784 | tf_op jit(solution)/shard_map/ppermute | solution.py:700
  690.6 319.6 %collective-permute-start.26 = (bf16[12,2,128,512]{3,2,1,0:T(8,128)(2,1)}, bf16[12,2,128,512]{3,2,1,0:T(8,128)(2,1)}, u32[]{:S(2)}, u32[]{:S(2)}) collective-permute-start(bf16[12,2,128,512]{3,2,1,0:T(8,128)(2,1)} %get-tuple-element.191), channel_id=1, source_target_pairs={{0,2},{2,0},{4,6},{6,4},{1,3},{3,1},{5,7},{7,5}} | collective-permute-start | bytes 9437192 | tf_op jit(solution)/shard_map/ppermute | solution.py:700
  691.8 319.2 %collective-permute-start.27 = (bf16[12,2,128,512]{3,2,1,0:T(8,128)(2,1)}, bf16[12,2,128,512]{3,2,1,0:T(8,128)(2,1)}, u32[]{:S(2)}, u32[]{:S(2)}) collective-permute-start(bf16[12,2,128,512]{3,2,1,0:T(8,128)(2,1)} %get-tuple-element.190), channel_id=1, source_target_pairs={{0,4},{2,6},{4,0},{6,2},{1,5},{3,7},{5,1},{7,3}} | collective-permute-start | bytes 9437192 | tf_op jit(solution)/shard_map/ppermute | solution.py:700
  692.6 318.4 %collective-permute-start.28 = (bf16[12,2,128,512]{3,2,1,0:T(8,128)(2,1)}, bf16[12,2,128,512]{3,2,1,0:T(8,128)(2,1)}, u32[]{:S(2)}, u32[]{:S(2)}) collective-permute-start(bf16[12,2,128,512]{3,2,1,0:T(8,128)(2,1)} %get-tuple-element.189), channel_id=1, source_target_pairs={{0,3},{1,2},{2,1},{3,0},{4,7},{5,6},{6,5},{7,4}} | collective-permute-start | bytes 9437192 | tf_op jit(solution)/shard_map/ppermute | solution.py:704
  706.3 306.4 %collective-permute-start.29 = (bf16[12,2,128,512]{3,2,1,0:T(8,128)(2,1)}, bf16[12,2,128,512]{3,2,1,0:T(8,128)(2,1)}, u32[]{:S(2)}, u32[]{:S(2)}) collective-permute-start(bf16[12,2,128,512]{3,2,1,0:T(8,128)(2,1)} %get-tuple-element.188), channel_id=1, source_target_pairs={{0,5},{1,4},{2,7},{3,6},{4,1},{5,0},{6,3},{7,2}} | collective-permute-start | bytes 9437192 | tf_op jit(solution)/shard_map/ppermute | solution.py:704
  1141.8 277.5 %collective-permute-start.41 = (f32[6,128,6144]{2,1,0:T(8,128)}, f32[6,128,6144]{2,1,0:T(8,128)}, u32[]{:S(2)}, u32[]{:S(2)}) collective-permute-start(f32[6,128,6144]{2,1,0:T(8,128)} %get-tuple-element.172), channel_id=1, source_target_pairs={{0,1},{1,0},{2,3},{3,2},{4,5},{5,4},{6,7},{7,6}} | collective-permute-start | bytes 56623112 | tf_op jit(solution)/shard_map/ppermute | solution.py:697
  1141.9 138.7 %collective-permute-start.36 = (bf16[512,6144]{1,0:T(8,128)(2,1)}, bf16[512,6144]{1,0:T(8,128)(2,1)}, u32[]{:S(2)}, u32[]{:S(2)}) collective-permute-start(bf16[512,6144]{1,0:T(8,128)(2,1)} %get-tuple-element.169), channel_id=1, source_target_pairs={{0,2},{2,0},{4,6},{6,4},{1,3},{3,1},{5,7},{7,5}} | collective-permute-start | bytes 18874376 | tf_op jit(solution)/shard_map/ppermute | solution.py:700
  1143.1 137.9 %collective-permute-start.37 = (bf16[512,6144]{1,0:T(8,128)(2,1)}, bf16[512,6144]{1,0:T(8,128)(2,1)}, u32[]{:S(2)}, u32[]{:S(2)}) collective-permute-start(bf16[512,6144]{1,0:T(8,128)(2,1)} %get-tuple-element.169), channel_id=1, source_target_pairs={{0,4},{2,6},{4,0},{6,2},{1,5},{3,7},{5,1},{7,3}} | collective-permute-start | bytes 18874376 | tf_op jit(solution)/shard_map/ppermute | solution.py:700
  1204.3 351.2 %collective-permute-start.45 = (f32[6,6144,128]{2,1,0:T(8,128)}, f32[6,6144,128]{2,1,0:T(8,128)}, u32[]{:S(2)}, u32[]{:S(2)}) collective-permute-start(f32[6,6144,128]{2,1,0:T(8,128)} %get-tuple-element.178), channel_id=1, source_target_pairs={{0,1},{1,0},{2,3},{3,2},{4,5},{5,4},{6,7},{7,6}} | collective-permute-start | bytes 56623112 | tf_op jit(solution)/shard_map/ppermute | solution.py:697
  1204.4 210.0 %collective-permute-start.38 = (bf16[512,6144]{1,0:T(8,128)(2,1)}, bf16[512,6144]{1,0:T(8,128)(2,1)}, u32[]{:S(2)}, u32[]{:S(2)}) collective-permute-start(bf16[512,6144]{1,0:T(8,128)(2,1)} %get-tuple-element.171), channel_id=1, source_target_pairs={{0,3},{1,2},{2,1},{3,0},{4,7},{5,6},{6,5},{7,4}} | collective-permute-start | bytes 18874376 | tf_op jit(solution)/shard_map/ppermute | solution.py:704
  1280.6 137.6 %collective-permute-start.39 = (bf16[512,6144]{1,0:T(8,128)(2,1)}, bf16[512,6144]{1,0:T(8,128)(2,1)}, u32[]{:S(2)}, u32[]{:S(2)}) collective-permute-start(bf16[512,6144]{1,0:T(8,128)(2,1)} %get-tuple-element.171), channel_id=1, source_target_pairs={{0,5},{1,4},{2,7},{3,6},{4,1},{5,0},{6,3},{7,2}} | collective-permute-start | bytes 18874376 | tf_op jit(solution)/shard_map/ppermute | solution.py:704
  1281.0 138.3 %collective-permute-start.40 = (bf16[512,6144]{1,0:T(8,128)(2,1)}, bf16[512,6144]{1,0:T(8,128)(2,1)}, u32[]{:S(2)}, u32[]{:S(2)}) collective-permute-start(bf16[512,6144]{1,0:T(8,128)(2,1)} %get-tuple-element.171), channel_id=1, source_target_pairs={{0,1},{1,0},{2,3},{3,2},{4,5},{5,4},{6,7},{7,6}} | collective-permute-start | bytes 18874376 | tf_op jit(solution)/shard_map/ppermute | solution.py:697
  1414.4 138.7 %collective-permute-start.42 = (bf16[512,6144]{1,0:T(8,128)(2,1)}, bf16[512,6144]{1,0:T(8,128)(2,1)}, u32[]{:S(2)}, u32[]{:S(2)}) collective-permute-start(bf16[512,6144]{1,0:T(8,128)(2,1)} %get-tuple-element.176), channel_id=1, source_target_pairs={{0,2},{2,0},{4,6},{6,4},{1,3},{3,1},{5,7},{7,5}} | collective-permute-start | bytes 18874376 | tf_op jit(solution)/shard_map/ppermute | solution.py:700
  1418.2 137.3 %collective-permute-start.43 = (bf16[512,6144]{1,0:T(8,128)(2,1)}, bf16[512,6144]{1,0:T(8,128)(2,1)}, u32[]{:S(2)}, u32[]{:S(2)}) collective-permute-start(bf16[512,6144]{1,0:T(8,128)(2,1)} %get-tuple-element.176), channel_id=1, source_target_pairs={{0,4},{2,6},{4,0},{6,2},{1,5},{3,7},{5,1},{7,3}} | collective-permute-start | bytes 18874376 | tf_op jit(solution)/shard_map/ppermute | solution.py:700
  1419.3 136.2 %collective-permute-start.44 = (bf16[512,6144]{1,0:T(8,128)(2,1)}, bf16[512,6144]{1,0:T(8,128)(2,1)}, u32[]{:S(2)}, u32[]{:S(2)}) collective-permute-start(bf16[512,6144]{1,0:T(8,128)(2,1)} %get-tuple-element.177), channel_id=1, source_target_pairs={{0,1},{1,0},{2,3},{3,2},{4,5},{5,4},{6,7},{7,6}} | collective-permute-start | bytes 18874376 | tf_op jit(solution)/shard_map/ppermute | solution.py:697
  1419.3 267.9 %collective-permute-start.46 = (bf16[512,6144]{1,0:T(8,128)(2,1)}, bf16[512,6144]{1,0:T(8,128)(2,1)}, u32[]{:S(2)}, u32[]{:S(2)}) collective-permute-start(bf16[512,6144]{1,0:T(8,128)(2,1)} %get-tuple-element.177), channel_id=1, source_target_pairs={{0,3},{1,2},{2,1},{3,0},{4,7},{5,6},{6,5},{7,4}} | collective-permute-start | bytes 18874376 | tf_op jit(solution)/shard_map/ppermute | solution.py:704
  1553.1 137.7 %collective-permute-start.47 = (bf16[512,6144]{1,0:T(8,128)(2,1)}, bf16[512,6144]{1,0:T(8,128)(2,1)}, u32[]{:S(2)}, u32[]{:S(2)}) collective-permute-start(bf16[512,6144]{1,0:T(8,128)(2,1)} %get-tuple-element.177), channel_id=1, source_target_pairs={{0,5},{1,4},{2,7},{3,6},{4,1},{5,0},{6,3},{7,2}} | collective-permute-start | bytes 18874376 | tf_op jit(solution)/shard_map/ppermute | solution.py:704
  1555.5 135.3 %collective-permute-start.48 = (bf16[512,6144]{1,0:T(8,128)(2,1)}, bf16[512,6144]{1,0:T(8,128)(2,1)}, u32[]{:S(2)}, u32[]{:S(2)}) collective-permute-start(bf16[512,6144]{1,0:T(8,128)(2,1)} %get-tuple-element.181), channel_id=1, source_target_pairs={{0,1},{1,0},{2,3},{3,2},{4,5},{5,4},{6,7},{7,6}} | collective-permute-start | bytes 18874376 | tf_op jit(solution)/shard_map/ppermute | solution.py:697
  (32 other events, 1626.2 us)
